TPU v7x, 256 devices: a whole 4x4x8 slice. The times are simulated.
256 devices in a mesh: blk: 16 (over x, y_hi, core), grp: 16 (over y_lo, z).
Axes of the slice: x: 4, y: 4 (y_hi: 2, y_lo: 2; y = y_hi * 2 + y_lo), z: 8, core: 2. Of those that a mesh axis runs over, the one named last changes fastest.
Arguments:
- amplitudes: bfloat16 [896, 4, 896], P('blk', None, 'grp'), may hold values from -6 to 6
- grid_factor: bfloat16 [8192, 896], P(('blk', 'grp')), may hold values from -0.1875 to 0.1875
- metric: float32 [8192, 16, 512], P('blk', 'grp'), may hold values from -0.625 to 0.625
- virt_energy: float32 [896], replicated, may hold values from 0.2 to 4
- pair_energy: float32 [4], replicated, may hold values from -2 to -0.5
Outputs:
- residual: float32 [896, 4, 896], P('blk', None, 'grp')
All inputs are finite; a program needn't handle non-finite values.
Results may differ from a plain program's by a relative error of at most 0.005.
Values may be sent and summed in bfloat16 or wider, within the bound.
No kernel may reach another device: no remote copies, remote signals or barrier semaphores. Data moves between devices by JAX's collectives and lax.ppermute only.
A program may use at most 64 MiB of HBM per device.

v0:
```python
import jax
import jax.numpy as jnp
from jax import lax
from jax.sharding import Mesh
from jax.sharding import PartitionSpec as P

GRP = ("grp_0", "grp_1")
BLK_GRP = ("blk", "grp_0", "grp_1")


def from_everyone(x, axis):
    count = lax.axis_size(axis)
    return lax.all_to_all(jnp.broadcast_to(x[None], (count, *x.shape)), axis, 0, 0, tiled=True)


def joined_along(pieces, dim):
    shape = list(pieces.shape[1:])
    shape[dim] *= pieces.shape[0]
    return jnp.moveaxis(pieces, 0, dim).reshape(shape)


def gather_directly(x, axis, dim):
    pieces = from_everyone(x, axis)
    return joined_along(pieces, dim)


def stacked_from(x, axes, sequence):
    pieces = x[None]
    for k in sequence:
        pieces = lax.all_gather(pieces, axes[k], axis=0, tiled=True)
    current = [lax.axis_size(axes[k]) for k in reversed(sequence)]
    pieces = pieces.reshape(*current, *x.shape)
    turned = sorted(range(len(sequence)), key=lambda place: sequence[len(sequence) - 1 - place])
    return pieces.transpose(*turned, *range(len(sequence), pieces.ndim)).reshape(-1, *x.shape)


def gather_axes(x, axes, sequence, dim):
    return joined_along(stacked_from(x, axes, sequence), dim)


def own_block(pieces, axes, sequence):
    shape = [lax.axis_size(a) for a in axes]
    pieces = pieces.reshape(*shape, *pieces.shape[1:])
    pieces = pieces.transpose(*sequence, *range(len(axes), pieces.ndim))
    pieces = pieces.reshape(-1, *pieces.shape[len(axes) :])
    for k in sequence:
        pieces = lax.psum_scatter(pieces, axes[k], scatter_dimension=0, tiled=True)
    return pieces[0]


def cut_along(x, dim, count):
    shape = x.shape
    pieces = x.reshape(*shape[:dim], count, shape[dim] // count, *shape[dim + 1 :])
    return jnp.moveaxis(pieces, dim, 0)


def sum_by_axis(x, axes, sequence, dim):
    count = lax.axis_size(axes)
    return own_block(cut_along(x, dim, count), axes, sequence)


def sent_and_summed(x, axis, dim):
    pieces = cut_along(x, dim, lax.axis_size(axis))
    arrived = lax.all_to_all(pieces, axis, split_axis=0, concat_axis=0, tiled=True)
    return arrived.astype(jnp.float32).sum(axis=0)


def local(amplitudes, grid_factor, metric, virt_energy, pair_energy):
    row_factor = gather_directly(grid_factor, GRP, 0)
    column_factor = gather_directly(grid_factor, "blk", 0)
    amplitude_rows = gather_directly(amplitudes, "blk", 0)
    row_count = row_factor.shape[0]
    left_part = jnp.einsum(
        "pc,ckd->kpd", row_factor, amplitude_rows, preferred_element_type=jnp.float32
    ).astype(jnp.bfloat16)
    columns = column_factor
    products = jnp.einsum(
        "kpd,qd->kpq",
        gather_axes(left_part, GRP, (0, 1), 2),
        columns,
        preferred_element_type=jnp.float32,
    )
    weighted = (metric.reshape(row_count, -1)[None] * products).astype(jnp.bfloat16)
    columns = column_factor
    mixed = (
        sum_by_axis(
            jnp.einsum("kpq,qb->bkp", weighted, columns, preferred_element_type=jnp.float32).astype(
                jnp.bfloat16
            ),
            GRP,
            (1, 0),
            0,
        )
        .astype(jnp.float32)
        .astype(jnp.bfloat16)
    )
    columns = row_factor
    ladder = sent_and_summed(
        jnp.einsum("pa,bkp->akb", columns, mixed, preferred_element_type=jnp.float32).astype(
            jnp.bfloat16
        ),
        "blk",
        0,
    )
    first_energy = lax.dynamic_slice_in_dim(
        virt_energy, lax.axis_index("blk") * amplitudes.shape[0], amplitudes.shape[0]
    )
    second_energy = lax.dynamic_slice_in_dim(
        virt_energy, lax.axis_index(GRP) * amplitudes.shape[2], amplitudes.shape[2]
    )
    denominator = (
        first_energy[:, None, None] + second_energy[None, None, :] - pair_energy[None, :, None]
    )
    return denominator * amplitudes.astype(jnp.float32) + ladder


def solution(mesh):
    split = Mesh(mesh.devices.reshape(mesh.shape["blk"], 2, 8), ("blk", "grp_0", "grp_1"))
    in_specs = (P("blk", None, GRP), P(BLK_GRP, None), P("blk", GRP, None), P(), P())
    out_specs = P("blk", None, GRP)
    return jax.shard_map(local, mesh=split, in_specs=in_specs, out_specs=out_specs, check_vma=False)
```

profile of v0, /device:TPU:1, one launch (start us, length us, event | category | flops | bytes accessed | tf_op | source)
XLA Modules:
  0.0 239.4 jit_solution(6617497980471759122)
XLA Ops:
  6.5 0.9 copy.17
  7.5 0.1 broadcast_bitcast_fusion
  7.6 1.5 reshape.67
  9.1 18.4 %all_to_all.20 = bf16[16,2,6272]{2,1,0:T(2,128)(2,1)S(1)} all-to-all(bf16[16,2,6272]{2,1,0:T(2,128)(2,1)S(1)} %reshape.67), channel_id=1, replica_groups=mesh['blk'=16,'grp_0'=2,'grp_1'=8] {'blk'}, dimensions={0} | all-to-all | bytes 802816 | tf_op jit(solution)/shard_map/all_to_all | solution.py:13
  27.5 1.8 broadcast_in_dim.7
  29.3 8.4 %all-to-all-start.1 = ((bf16[16,32,896]{2,1,0:T(8,128)(2,1)}), bf16[16,32,896]{2,1,0:T(8,128)(2,1)S(1)}, u32[]{:S(2)}, u32[]{:S(2)}) async-start(bf16[16,32,896]{2,1,0:T(8,128)(2,1)} %broadcast_in_dim.7), calls=%async_computation.1 | async-start | bytes 1835008 | tf_op jit(solution)/shard_map/all_to_all | solution.py:13
  37.7 0.0 all-gather.3.cloned.1.call-start
  37.8 1.6 reshape.68
  39.4 0.4 copy.19
  39.8 1.1 reshape.56
  40.9 19.1 %all-to-all-done.1 = bf16[16,32,896]{2,1,0:T(8,128)(2,1)S(1)} async-done(((bf16[16,32,896]{2,1,0:T(8,128)(2,1)}), bf16[16,32,896]{2,1,0:T(8,128)(2,1)S(1)}, u32[]{:S(2)}, u32[]{:S(2)}) %all-to-all-start.1) | async-done | bytes 917536 | tf_op jit(solution)/shard_map/all_to_all | solution.py:13
  60.0 0.5 fusion.1
  60.4 5.6 %all-gather = bf16[8,512,56]{1,2,0:T(8,128)(2,1)} all-gather(bf16[4,512,56]{1,2,0:T(8,128)(2,1)S(1)} %fusion.1), channel_id=2, replica_groups=mesh['blk'=16,'grp_0'=2,'grp_1'=8] {'grp_0'}, dimensions={0}, use_global_device_ids=true | all-gather | bytes 688128 | tf_op jit(solution)/shard_map/all_gather | solution.py:30
  66.1 0.0 all-gather.3.cloned.1.call-update
  66.1 7.9 %all-to-all-start.2 = ((bf16[16,32,896]{2,1,0:T(8,128)(2,1)}), bf16[16,32,896]{2,1,0:T(8,128)(2,1)S(1)}, u32[]{:S(2)}, u32[]{:S(2)}) async-start(bf16[16,32,896]{2,1,0:T(8,128)(2,1)} %broadcast_in_dim.7), calls=%async_computation.2 | async-start | bytes 1835008 | tf_op jit(solution)/shard_map/all_to_all | solution.py:13
  74.0 0.0 reduce-scatter.3.cloned.1.call-start
  74.0 1.3 copy.33
  75.3 40.1 %all-gather.3.cloned.1.call-done = bf16[16,4,512,56]{2,3,1,0:T(8,128)(2,1)} async-done(((bf16[2,4,512,56]{2,3,1,0:T(8,128)(2,1)}), bf16[16,4,512,56]{2,3,1,0:T(8,128)(2,1)}) %all-gather.3.cloned.1.call-update) | async-done | bytes 3670032 | tf_op jit(solution)/shard_map/all_gather | solution.py:30
  115.5 2.3 copy.20
  117.8 2.1 copy.21
  119.8 0.0 all-to-all-done.2
  119.8 7.5 %convert_bitcast_fusion = bf16[896,4,512]{0,2,1:T(8,128)(2,1)} fusion(bf16[512,896,1]{1,0,2:T(8,128)(2,1)S(1)} %bitcast.61, bf16[4,512,896]{1,2,0:T(8,128)(2,1)} %bitcast.56, f32[512,512]{1,0:T(8,128)S(1)} %bitcast.60), kind=kOutput, calls=%fused_computation.1 | convolution fusion | flops 3762028544 | bytes 9306112 | tf_op jit(solution)/shard_map/kpq,qb->bkp/dot_general | solution.py:87
  127.4 5.9 %copy.23 = bf16[896,4,512]{2,0,1:T(8,128)(2,1)} copy(bf16[896,4,512]{0,2,1:T(8,128)(2,1)} %convert_bitcast_fusion) | data formatting | bytes 7340032 | tf_op jit(solution)/shard_map/convert_element_type | solution.py:87
  133.3 4.3 %copy.24 = bf16[8,2,56,4,512]{4,2,3,1,0:T(8,128)(2,1)} copy(bf16[8,2,56,4,512]{4,2,0,1,3:T(8,128)(2,1)} %bitcast.52) | data formatting | bytes 7340032 | tf_op jit(solution)/shard_map/transpose | solution.py:44
  137.6 0.0 reduce-scatter.3.cloned.1.call-update
  137.7 0.0 reduce-scatter.5.cloned.1.call-start
  137.7 49.2 %reduce-scatter.3.cloned.1.call-done = bf16[2,56,4,512]{3,1,2,0:T(8,128)(2,1)} async-done(((bf16[16,56,4,512]{3,1,2,0:T(8,128)(2,1)}), bf16[2,56,4,512]{3,1,2,0:T(8,128)(2,1)}) %reduce-scatter.3.cloned.1.call-update) | async-done | bytes 458768 | tf_op jit(solution)/shard_map/reduce_scatter | solution.py:47
  186.9 0.0 reduce-scatter.5.cloned.1.call-update
  186.9 20.5 %reduce-scatter.5.cloned.1.call-done = bf16[1,56,4,512]{3,1,2,0:T(8,128)(2,1)} async-done(((bf16[2,56,4,512]{3,1,2,0:T(8,128)(2,1)}), bf16[1,56,4,512]{3,1,2,0:T(8,128)(2,1)}) %reduce-scatter.5.cloned.1.call-update) | async-done | bytes 229392 | tf_op jit(solution)/shard_map/reduce_scatter | solution.py:47
  207.4 1.4 fusion
  208.8 0.0 copy-start
  208.8 1.5 reshape.63
  210.3 0.2 copy.34
  210.5 2.2 reshape.69
  212.7 7.2 %all-to-all-start.3 = ((bf16[16,2,6272]{2,1,0:T(2,128)(2,1)}), bf16[16,2,6272]{2,1,0:T(2,128)(2,1)S(1)}, u32[]{:S(2)}, u32[]{:S(2)}) async-start(bf16[16,2,6272]{2,1,0:T(2,128)(2,1)} %reshape.69), calls=%async_computation.5 | async-start | bytes 802816 | tf_op jit(solution)/shard_map/all_to_all | solution.py:64
  220.0 0.8 fusion.3
  220.8 0.1 broadcast_add_fusion
  220.9 9.3 %all-to-all-done.3 = bf16[16,2,6272]{2,1,0:T(2,128)(2,1)S(1)} async-done(((bf16[16,2,6272]{2,1,0:T(2,128)(2,1)}), bf16[16,2,6272]{2,1,0:T(2,128)(2,1)S(1)}, u32[]{:S(2)}, u32[]{:S(2)}) %all-to-all-start.3) | async-done | bytes 401440 | tf_op jit(solution)/shard_map/all_to_all | solution.py:64
  230.2 1.6 reshape.70
  231.8 0.2 convert_reduce_fusion
  232.0 0.0 copy-done
  232.0 0.1 multiply_add_fusion
  232.1 0.7 copy.27
Async XLA Ops:
  29.3 30.7 %all-to-all-start.1 = ((bf16[16,32,896]{2,1,0:T(8,128)(2,1)}), bf16[16,32,896]{2,1,0:T(8,128)(2,1)S(1)}, u32[]{:S(2)}, u32[]{:S(2)}) async-start(bf16[16,32,896]{2,1,0:T(8,128)(2,1)} %broadcast_in_dim.7), calls=%async_computation.1 | async-start | bytes 1835008 | tf_op jit(solution)/shard_map/all_to_all | solution.py:13
  37.7 77.8 %all-gather.3.cloned.1.call-start = ((), (), s32[]{:S(2)}) async-start(), calls=%async_computation.6 | async-start | bytes 4128768 | tf_op jit(solution)/shard_map/all_gather | solution.py:30
  66.1 53.7 %all-to-all-start.2 = ((bf16[16,32,896]{2,1,0:T(8,128)(2,1)}), bf16[16,32,896]{2,1,0:T(8,128)(2,1)S(1)}, u32[]{:S(2)}, u32[]{:S(2)}) async-start(bf16[16,32,896]{2,1,0:T(8,128)(2,1)} %broadcast_in_dim.7), calls=%async_computation.2 | async-start | bytes 1835008 | tf_op jit(solution)/shard_map/all_to_all | solution.py:13
  74.0 112.9 %reduce-scatter.3.cloned.1.call-start = ((), (), s32[]{:S(2)}) async-start(), calls=%async_computation.7 | async-start | bytes 4128768 | tf_op jit(solution)/shard_map/reduce_scatter | solution.py:47
  137.7 69.8 %reduce-scatter.5.cloned.1.call-start = ((), (), s32[]{:S(2)}) async-start(), calls=%async_computation.8 | async-start | bytes 688128 | tf_op jit(solution)/shard_map/reduce_scatter | solution.py:47
  208.8 23.2 %copy-start = (f32[4]{0:T(128)S(1)}, f32[4]{0:T(128)}, u32[]{:S(2)}) copy-start(f32[4]{0:T(128)} %param.9) | copy-start | bytes 52
  212.7 17.4 %all-to-all-start.3 = ((bf16[16,2,6272]{2,1,0:T(2,128)(2,1)}), bf16[16,2,6272]{2,1,0:T(2,128)(2,1)S(1)}, u32[]{:S(2)}, u32[]{:S(2)}) async-start(bf16[16,2,6272]{2,1,0:T(2,128)(2,1)} %reshape.69), calls=%async_computation.5 | async-start | bytes 802816 | tf_op jit(solution)/shard_map/all_to_all | solution.py:64
Sparse Core Ops, SparseCore 0:
  66.2 49.2 all-gather.2
  137.8 49.0 reduce-scatter.2
  189.4 17.9 reduce-scatter.4
where the time goes:
time: 240 us; the launch traced here: 239 us
  waiting for transfers between devices  138 us (58%)
  local copies, waits for them, and re-layouts  30.5 us (13%)
  blocking collectives  24 us (10%)
  starting transfers between devices  23.7 us (10%)
  between operations  13.2 us (6%)
  matrix products  9.37 us (4%)
    reduce_scatter x2, waiting for transfers between devices, own_block(): pieces = lax.psum_scatter(pieces, axes[k], scatter_dimension=0, tiled=True)  69.7 us
    all_gather x1, waiting for transfers between devices, stacked_from(): pieces = lax.all_gather(pieces, axes[k], axis=0, tiled=True)  40.1 us
    all_to_all x2, waiting for transfers between devices, from_everyone(): lax.all_to_all(jnp.broadcast_to(x[None], (count, *x.shape)), axis, 0, 0,...  19.1 us
    all_to_all x1, blocking collectives, from_everyone(): lax.all_to_all(jnp.broadcast_to(x[None], (count, *x.shape)), axis, 0, 0,...  18.4 us
    all_to_all x2, starting transfers between devices, from_everyone(): lax.all_to_all(jnp.broadcast_to(x[None], (count, *x.shape)), axis, 0, 0,...  16.3 us
    unnamed x9, local copies, waits for them, and re-layouts  9.32 us
    all_to_all x1, waiting for transfers between devices, sent_and_summed(): lax.all_to_all(pieces, axis, split_axis=0, concat_axis=0, tiled=True)  9.27 us
    dot_general x1, matrix products, local(): jnp.einsum('kpq,qb->bkp', weighted, columns, preferred_element_type=jnp.f...  7.54 us
  transfers between devices with their start and end apart: 6, of which 5 were waited for; matrix products, arithmetic and copies ran while one was open for 4% of the time, Pallas kernels for 0%

commit v1 on v0

v1 whole, which is shorter than its diff:
```python
import jax
import jax.numpy as jnp
from jax import lax
from jax.sharding import Mesh
from jax.sharding import PartitionSpec as P

BLK = ("x", "y_hi", "core")
GRP = ("y_lo", "z")
PLANE = ("x", "y_hi")
CHUNKS = 2
BF16 = jnp.bfloat16
F32 = jnp.float32


def from_everyone(x, axis):
    count = lax.axis_size(axis)
    return lax.all_to_all(jnp.broadcast_to(x[None], (count, *x.shape)), axis, 0, 0, tiled=True)


def exchanged(x):
    return lax.ppermute(x, "core", [(0, 1), (1, 0)])


def both_cores(own):
    other = exchanged(own)
    first = lax.axis_index("core") == 0
    return jnp.stack([jnp.where(first, own, other), jnp.where(first, other, own)], axis=1)


def local(amplitudes, grid_factor, metric, virt_energy, pair_energy):
    n_c, n_k, n_d = amplitudes.shape
    nv = grid_factor.shape[1]
    n_blk, n_grp = lax.axis_size(BLK), lax.axis_size(GRP)
    turned = amplitudes.transpose(2, 1, 0).reshape(n_d, n_k * n_c)
    turned = from_everyone(turned, GRP).reshape(nv, n_k * n_c)
    columns = both_cores(from_everyone(grid_factor, PLANE)).reshape(-1, nv)
    rows = from_everyone(grid_factor, GRP).reshape(-1, nv)
    n_q = columns.shape[0]
    n_p = rows.shape[0]
    z = metric.reshape(n_p, 1, n_q)
    right = lax.dot_general(
        turned, columns, (((0,), (1,)), ((), ())), preferred_element_type=F32
    ).astype(BF16)
    per = n_k // CHUNKS
    right = right.reshape(CHUNKS, per, n_c, n_q).transpose(0, 2, 1, 3).reshape(CHUNKS, n_c, per * n_q)
    parts = []
    for h in range(CHUNKS):
        full = both_cores(from_everyone(right[h], PLANE)).reshape(nv, per * n_q)
        products = jnp.dot(rows, full, preferred_element_type=F32)
        weighted = (products.reshape(n_p, per, n_q) * z).astype(BF16).reshape(n_p, per * n_q)
        back = lax.dot_general(
            rows, weighted, (((0,), (0,)), ((), ())), preferred_element_type=F32
        ).astype(BF16)
        back = back.reshape(n_blk // 2, 2, n_c, per * n_q)
        first = lax.axis_index("core") == 0
        keep = jnp.where(first, back[:, 0], back[:, 1])
        give = jnp.where(first, back[:, 1], back[:, 0])
        chip = (keep.astype(F32) + exchanged(give).astype(F32)).astype(BF16)
        arrived = lax.all_to_all(chip, PLANE, 0, 0, tiled=True)
        summed = arrived.astype(F32).sum(axis=0).astype(BF16)
        summed = summed.reshape(n_c, per, n_q).transpose(1, 0, 2).reshape(per * n_c, n_q)
        parts.append(
            lax.dot_general(
                columns, summed, (((0,), (1,)), ((), ())), preferred_element_type=F32
            ).astype(BF16)
        )
    ladder = jnp.concatenate(parts, axis=1).reshape(n_grp, n_d, n_k * n_c)
    ladder = lax.all_to_all(ladder, GRP, 0, 0, tiled=True).astype(F32).sum(axis=0)
    ladder = ladder.reshape(n_d, n_k, n_c).transpose(2, 1, 0)
    first_energy = lax.dynamic_slice_in_dim(virt_energy, lax.axis_index(BLK) * n_c, n_c)
    second_energy = lax.dynamic_slice_in_dim(virt_energy, lax.axis_index(GRP) * n_d, n_d)
    denominator = (
        first_energy[:, None, None] + second_energy[None, None, :] - pair_energy[None, :, None]
    )
    return denominator * amplitudes.astype(F32) + ladder


def solution(mesh):
    split = Mesh(mesh.devices.reshape(4, 2, 2, 2, 8), ("x", "y_hi", "core", "y_lo", "z"))
    in_specs = (P(BLK, None, GRP), P(BLK + GRP, None), P(BLK, GRP, None), P(), P())
    return jax.shard_map(
        local, mesh=split, in_specs=in_specs, out_specs=P(BLK, None, GRP), check_vma=False
    )
```

time: 240 us -> 185 us (0.77)
  waiting for transfers between devices: 138 us -> 73 us
  starting transfers between devices: 23.7 us -> 43.5 us
  local copies, waits for them, and re-layouts: 30.5 us -> 11.8 us
  between operations: 13.2 us -> 0.37 us
  other arithmetic: 0.34 us -> 11.8 us
  blocking collectives: 24 us -> 34.8 us
    reduce_scatter x2 -> x0, waiting for transfers between devices: 69.7 us -> none  [own_block(): pieces = lax.psum_scatter(pieces, axes[k], scatter_dimension=0, tiled=True)]
    all_gather x1 -> x0, waiting for transfers between devices: 40.1 us -> none  [stacked_from(): pieces = lax.all_gather(pieces, axes[k], axis=0, tiled=True)]
    all_to_all x1 -> x3, waiting for transfers between devices: 9.27 us -> 36.4 us  [the longest x2 25.3 us: local(): arrived = lax.all_to_all(chip, PLANE, 0, 0, tiled=True)]
    all_to_all x2 -> x3, waiting for transfers between devices: 19.1 us -> 36.6 us  [from_everyone(): lax.all_to_all(jnp.broadcast_to(x[None], (count, *x.shape)), axis, 0, 0,...]
    all_to_all x1 -> x2, blocking collectives: 18.4 us -> 34.8 us  [from_everyone(): lax.all_to_all(jnp.broadcast_to(x[None], (count, *x.shape)), axis, 0, 0,...]
    ppermute x0 -> x5, starting transfers between devices: none -> 12.1 us  [exchanged(): return lax.ppermute(x, 'core', [(0, 1), (1, 0)])]
    unnamed x9 -> x14, local copies, waits for them, and re-layouts: 9.32 us -> 1.3 us
    transpose x3, local copies, waits for them, and re-layouts: 8.66 us -> 0.96 us  [the longest x1 0.93 us: local(): turned = amplitudes.transpose(2, 1, 0).reshape(n_d, n_k * n_c)]
  transfers between devices with their start and end apart: 6 -> 11, of which waited for: 5 -> 6; matrix products, arithmetic and copies ran while one was open for 4% -> 13% of each run, Pallas kernels for 0% -> 0%
where the time goes in v1:
time: 185 us; the launch traced here: 183 us
  waiting for transfers between devices  73 us (39%)
  starting transfers between devices  43.5 us (24%)
  blocking collectives  34.8 us (19%)
  local copies, waits for them, and re-layouts  11.8 us (6%)
  other arithmetic  11.8 us (6%)
  matrix products  7.54 us (4%)
    all_to_all x3, waiting for transfers between devices, from_everyone(): lax.all_to_all(jnp.broadcast_to(x[None], (count, *x.shape)), axis, 0, 0,...  36.6 us
    all_to_all x2, blocking collectives, from_everyone(): lax.all_to_all(jnp.broadcast_to(x[None], (count, *x.shape)), axis, 0, 0,...  34.8 us
    all_to_all x2, waiting for transfers between devices, local(): arrived = lax.all_to_all(chip, PLANE, 0, 0, tiled=True)  25.3 us
    all_to_all x3, starting transfers between devices, from_everyone(): lax.all_to_all(jnp.broadcast_to(x[None], (count, *x.shape)), axis, 0, 0,...  18.8 us
    ppermute x5, starting transfers between devices, exchanged(): return lax.ppermute(x, 'core', [(0, 1), (1, 0)])  12.1 us
    all_to_all x1, waiting for transfers between devices, local(): lax.all_to_all(ladder, GRP, 0, 0, tiled=True).astype(F32).sum(axis=0)  11.1 us
    all_to_all x2, starting transfers between devices, local(): arrived = lax.all_to_all(chip, PLANE, 0, 0, tiled=True)  8 us
    another operation x6, other arithmetic, both_cores(): jnp.stack([jnp.where(first, own, other), jnp.where(first, other, own)], a...  4.77 us
  transfers between devices with their start and end apart: 11, of which 6 were waited for; matrix products, arithmetic and copies ran while one was open for 13% of the time, Pallas kernels for 0%

profile of v1, /device:TPU:1, one launch (start us, length us, event | category | flops | bytes accessed | tf_op | source)
XLA Modules:
  0.0 182.9 jit_solution(1273889646460310980)
XLA Ops:
  0.0 0.9 broadcast_in_dim.16
  0.9 16.4 %all_to_all.40 = bf16[8,32,896]{2,1,0:T(8,128)(2,1)S(1)} all-to-all(bf16[8,32,896]{2,1,0:T(8,128)(2,1)S(1)} %broadcast_in_dim.16), channel_id=1, replica_groups=mesh['x'=4,'y_hi'=2,'core'=2,'y_lo'=2,'z'=8] {'x','y_hi'}, dimensions={0} | all-to-all | bytes 917504 | tf_op jit(solution)/shard_map/all_to_all | solution.py:17
  17.2 2.5 %collective-permute-start = (bf16[8,32,896]{2,1,0:T(8,128)(2,1)S(1)}, bf16[8,32,896]{2,1,0:T(8,128)(2,1)S(1)}, u32[]{:S(2)}, u32[]{:S(2)}) collective-permute-start(bf16[8,32,896]{2,1,0:T(8,128)(2,1)S(1)} %all_to_all.40), channel_id=1, source_target_pairs={{0,16},{16,0},{1,17},{17,1},{2,18},{18,2},{3,19},{19,3},{4,20},{20... | collective-permute-start | bytes 1376264 | tf_op jit(solution)/shard_map/ppermute | solution.py:21
  19.7 0.9 copy.47
  20.7 0.8 broadcast_in_dim.18
  21.6 8.4 %all-to-all-start.1 = ((bf16[16,56,224]{2,1,0:T(8,128)(2,1)}), bf16[16,56,224]{2,1,0:T(8,128)(2,1)S(1)}, u32[]{:S(2)}, u32[]{:S(2)}) async-start(bf16[16,56,224]{2,1,0:T(8,128)(2,1)} %broadcast_in_dim.18), calls=%async_computation.1 | async-start | bytes 917504 | tf_op jit(solution)/shard_map/all_to_all | solution.py:17
  30.2 12.7 %all-to-all-done.1 = bf16[16,56,224]{2,1,0:T(8,128)(2,1)S(1)} async-done(((bf16[16,56,224]{2,1,0:T(8,128)(2,1)}), bf16[16,56,224]{2,1,0:T(8,128)(2,1)S(1)}, u32[]{:S(2)}, u32[]{:S(2)}) %all-to-all-start.1) | async-done | bytes 401440 | tf_op jit(solution)/shard_map/all_to_all | solution.py:17
  42.9 0.5 convolution_convert_fusion.2
  43.4 0.2 copy.72
  43.5 0.2 fusion.6
  43.7 1.1 broadcast_in_dim.40
  44.8 4.2 %all-to-all-start.2 = ((bf16[8,56,1024]{2,1,0:T(8,128)(2,1)}), bf16[8,56,1024]{2,1,0:T(8,128)(2,1)}, u32[]{:S(2)}, u32[]{:S(2)}) async-start(bf16[8,56,1024]{2,1,0:T(8,128)(2,1)} %broadcast_in_dim.40), calls=%async_computation.2 | async-start | bytes 1835008 | tf_op jit(solution)/shard_map/all_to_all | solution.py:17
  49.1 13.2 %all-to-all-done.2 = bf16[8,56,1024]{2,1,0:T(8,128)(2,1)} async-done(((bf16[8,56,1024]{2,1,0:T(8,128)(2,1)}), bf16[8,56,1024]{2,1,0:T(8,128)(2,1)}, u32[]{:S(2)}, u32[]{:S(2)}) %all-to-all-start.2) | async-done | bytes 917536 | tf_op jit(solution)/shard_map/all_to_all | solution.py:17
  62.4 18.5 %all_to_all.41 = bf16[8,56,1024]{2,1,0:T(8,128)(2,1)} all-to-all(bf16[8,56,1024]{2,1,0:T(8,128)(2,1)S(1)} %broadcast_in_dim.43), channel_id=1, replica_groups=mesh['x'=4,'y_hi'=2,'core'=2,'y_lo'=2,'z'=8] {'x','y_hi'}, dimensions={0} | all-to-all | bytes 1835008 | tf_op jit(solution)/shard_map/all_to_all | solution.py:17
  80.8 1.0 broadcast_in_dim.41
  81.8 6.1 %all-to-all-start.3 = ((bf16[16,32,896]{2,1,0:T(8,128)(2,1)}), bf16[16,32,896]{2,1,0:T(8,128)(2,1)S(1)}, u32[]{:S(2)}, u32[]{:S(2)}) async-start(bf16[16,32,896]{2,1,0:T(8,128)(2,1)} %broadcast_in_dim.41), calls=%async_computation.3 | async-start | bytes 1835008 | tf_op jit(solution)/shard_map/all_to_all | solution.py:17
  88.0 3.3 %collective-permute-start.1 = (bf16[8,56,1024]{2,1,0:T(8,128)(2,1)}, bf16[8,56,1024]{2,1,0:T(8,128)(2,1)}, u32[]{:S(2)}, u32[]{:S(2)}) collective-permute-start(bf16[8,56,1024]{2,1,0:T(8,128)(2,1)} %all-to-all-done.2), channel_id=1, source_target_pairs={{0,16},{16,0},{1,17},{17,1},{2,18},{18,2},{3,19},{19,3},{4,20},{20... | collective-permute-start | bytes 2752520 | tf_op jit(solution)/shard_map/ppermute | solution.py:21
  91.3 2.3 %copy.63 = f32[512,1,512]{0,2,1:T(8,128)S(1)} copy(f32[512,1,512]{2,1,0:T(1,128)} %param.7) | data formatting | bytes 2097152 | tf_op jit(solution)/shard_map/mul | solution.py:50
  93.6 0.1 collective-permute-start.3
  93.7 1.6 select_bitcast_fusion.4
  95.3 1.4 pad_maximum_fusion
  96.7 10.8 %all-to-all-done.3 = bf16[16,32,896]{2,1,0:T(8,128)(2,1)S(1)} async-done(((bf16[16,32,896]{2,1,0:T(8,128)(2,1)}), bf16[16,32,896]{2,1,0:T(8,128)(2,1)S(1)}, u32[]{:S(2)}, u32[]{:S(2)}) %all-to-all-start.3) | async-done | bytes 917536 | tf_op jit(solution)/shard_map/all_to_all | solution.py:17
  107.5 2.8 %fusion = bf16[512,1024]{0,1:T(8,128)(2,1)S(1)} fusion(bf16[896,1024]{1,0:T(8,128)(2,1)} %bitcast.121, bf16[512,896]{1,0:T(8,128)(2,1)S(1)} %bitcast.117, f32[512,512]{0,1:T(8,128)S(1)} %bitcast.115), kind=kOutput, calls=%fused_computation.2 | convolution fusion | flops 940572672 | bytes 4849664 | tf_op jit(solution)/shard_map/dot_general | solution.py:49
  110.3 1.2 convolution_convert_fusion.1
  111.6 5.3 %collective-permute-start.2 = (bf16[8,56,1024]{2,1,0:T(8,128)(2,1)S(1)}, bf16[8,56,1024]{2,1,0:T(8,128)(2,1)S(1)}, u32[]{:S(2)}, u32[]{:S(2)}) collective-permute-start(bf16[8,56,1024]{2,1,0:T(8,128)(2,1)S(1)} %fusion.4), channel_id=1, source_target_pairs={{0,16},{16,0},{1,17},{17,1},{2,18},{18,2},{3,19},{19,3},{4,20},{20... | collective-permute-start | bytes 2752520 | tf_op jit(solution)/shard_map/ppermute | solution.py:21
  116.8 1.4 select_bitcast_fusion.2
  118.2 0.2 pad_maximum_fusion.1
  118.4 0.2 copy.56
  118.6 1.3 fusion.1
  120.0 1.2 convolution_convert_fusion
  121.1 1.2 copy-done
  122.4 1.1 select_bitcast_fusion
  123.4 1.0 collective-permute-start.4
  124.4 1.5 fusion.3
  125.9 4.4 %all-to-all-start.4 = ((bf16[8,56,1024]{2,1,0:T(8,128)(2,1)}), bf16[8,56,1024]{2,1,0:T(8,128)(2,1)}, u32[]{:S(2)}, u32[]{:S(2)}) async-start(bf16[8,56,1024]{2,1,0:T(8,128)(2,1)} %fusion.3), calls=%async_computation.4 | async-start | bytes 1835008 | tf_op jit(solution)/shard_map/all_to_all | solution.py:59
  130.3 2.6 %fusion.2 = bf16[8,56,1024]{2,1,0:T(8,128)(2,1)} fusion(bf16[8,56,1024]{2,1,0:T(8,128)(2,1)} %collective-permute-done.4, pred[]{:T(512)S(6)} %eq.2, bf16[8,2,56,1024]{3,2,1,0:T(8,128)(2,1)S(1)} %bitcast.126), kind=kLoop, calls=%fused_computation.7 | loop fusion | flops 2293760 | bytes 3670017 | tf_op jit(solution)/shard_map/convert_element_type | solution.py:58
  132.9 12.6 %all-to-all-done.4 = bf16[8,56,1024]{2,1,0:T(8,128)(2,1)} async-done(((bf16[8,56,1024]{2,1,0:T(8,128)(2,1)}), bf16[8,56,1024]{2,1,0:T(8,128)(2,1)}, u32[]{:S(2)}, u32[]{:S(2)}) %all-to-all-start.4) | async-done | bytes 917536 | tf_op jit(solution)/shard_map/all_to_all | solution.py:59
  145.5 3.6 %all-to-all-start.6 = ((bf16[8,56,1024]{2,1,0:T(8,128)(2,1)}), bf16[8,56,1024]{2,1,0:T(8,128)(2,1)S(1)}, u32[]{:S(2)}, u32[]{:S(2)}) async-start(bf16[8,56,1024]{2,1,0:T(8,128)(2,1)} %fusion.2), calls=%async_computation.6 | async-start | bytes 1835008 | tf_op jit(solution)/shard_map/all_to_all | solution.py:59
  149.2 1.3 reduce_sum.33
  150.6 0.3 convolution_convert_fusion.4
  150.9 12.7 %all-to-all-done.6 = bf16[8,56,1024]{2,1,0:T(8,128)(2,1)S(1)} async-done(((bf16[8,56,1024]{2,1,0:T(8,128)(2,1)}), bf16[8,56,1024]{2,1,0:T(8,128)(2,1)S(1)}, u32[]{:S(2)}, u32[]{:S(2)}) %all-to-all-start.6) | async-done | bytes 917536 | tf_op jit(solution)/shard_map/all_to_all | solution.py:59
  163.6 0.2 reduce_sum.34
  163.9 0.3 convolution_convert_fusion.3
  164.2 1.0 copy.60
  165.2 4.7 %all-to-all-start.7 = ((bf16[16,56,224]{2,1,0:T(8,128)(2,1)}), bf16[16,56,224]{2,1,0:T(8,128)(2,1)S(1)}, u32[]{:S(2)}, u32[]{:S(2)}) async-start(bf16[16,56,224]{2,1,0:T(8,128)(2,1)} %bitcast.38), calls=%async_computation.7 | async-start | bytes 917504 | tf_op jit(solution)/shard_map/all_to_all | solution.py:68
  170.0 0.8 fusion.7
  170.9 11.1 %all-to-all-done.7 = bf16[16,56,224]{2,1,0:T(8,128)(2,1)S(1)} async-done(((bf16[16,56,224]{2,1,0:T(8,128)(2,1)}), bf16[16,56,224]{2,1,0:T(8,128)(2,1)S(1)}, u32[]{:S(2)}, u32[]{:S(2)}) %all-to-all-start.7) | async-done | bytes 401440 | tf_op jit(solution)/shard_map/all_to_all | solution.py:68
  182.3 0.7 copy.62
  (32 shorter events, 1.1 us)
Async XLA Ops:
  17.2 12.7 %collective-permute-start = (bf16[8,32,896]{2,1,0:T(8,128)(2,1)S(1)}, bf16[8,32,896]{2,1,0:T(8,128)(2,1)S(1)}, u32[]{:S(2)}, u32[]{:S(2)}) collective-permute-start(bf16[8,32,896]{2,1,0:T(8,128)(2,1)S(1)} %all_to_all.40), channel_id=1, source_target_pairs={{0,16},{16,0},{1,17},{17,1},{2,18},{18,2},{3,19},{19,3},{4,20},{20... | collective-permute-start | bytes 1376264 | tf_op jit(solution)/shard_map/ppermute | solution.py:21
  21.6 21.3 %all-to-all-start.1 = ((bf16[16,56,224]{2,1,0:T(8,128)(2,1)}), bf16[16,56,224]{2,1,0:T(8,128)(2,1)S(1)}, u32[]{:S(2)}, u32[]{:S(2)}) async-start(bf16[16,56,224]{2,1,0:T(8,128)(2,1)} %broadcast_in_dim.18), calls=%async_computation.1 | async-start | bytes 917504 | tf_op jit(solution)/shard_map/all_to_all | solution.py:17
  44.8 17.4 %all-to-all-start.2 = ((bf16[8,56,1024]{2,1,0:T(8,128)(2,1)}), bf16[8,56,1024]{2,1,0:T(8,128)(2,1)}, u32[]{:S(2)}, u32[]{:S(2)}) async-start(bf16[8,56,1024]{2,1,0:T(8,128)(2,1)} %broadcast_in_dim.40), calls=%async_computation.2 | async-start | bytes 1835008 | tf_op jit(solution)/shard_map/all_to_all | solution.py:17
  49.1 31.8 %copy-start.4 = (bf16[32,896]{1,0:T(8,128)(2,1)S(1)}, bf16[32,896]{1,0:T(8,128)(2,1)}, u32[]{:S(2)}) copy-start(bf16[32,896]{1,0:T(8,128)(2,1)} %param.6) | copy-start | bytes 172036
  81.8 25.6 %all-to-all-start.3 = ((bf16[16,32,896]{2,1,0:T(8,128)(2,1)}), bf16[16,32,896]{2,1,0:T(8,128)(2,1)S(1)}, u32[]{:S(2)}, u32[]{:S(2)}) async-start(bf16[16,32,896]{2,1,0:T(8,128)(2,1)} %broadcast_in_dim.41), calls=%async_computation.3 | async-start | bytes 1835008 | tf_op jit(solution)/shard_map/all_to_all | solution.py:17
  88.0 5.7 %collective-permute-start.1 = (bf16[8,56,1024]{2,1,0:T(8,128)(2,1)}, bf16[8,56,1024]{2,1,0:T(8,128)(2,1)}, u32[]{:S(2)}, u32[]{:S(2)}) collective-permute-start(bf16[8,56,1024]{2,1,0:T(8,128)(2,1)} %all-to-all-done.2), channel_id=1, source_target_pairs={{0,16},{16,0},{1,17},{17,1},{2,18},{18,2},{3,19},{19,3},{4,20},{20... | collective-permute-start | bytes 2752520 | tf_op jit(solution)/shard_map/ppermute | solution.py:21
  93.6 23.2 %collective-permute-start.3 = (bf16[8,56,1024]{2,1,0:T(8,128)(2,1)}, bf16[8,56,1024]{2,1,0:T(8,128)(2,1)}, u32[]{:S(2)}, u32[]{:S(2)}) collective-permute-start(bf16[8,56,1024]{2,1,0:T(8,128)(2,1)} %all_to_all.41), channel_id=1, source_target_pairs={{0,16},{16,0},{1,17},{17,1},{2,18},{18,2},{3,19},{19,3},{4,20},{20... | collective-permute-start | bytes 2752520 | tf_op jit(solution)/shard_map/ppermute | solution.py:21
  111.4 5.4 %copy-start.2 = (bf16[8,56,1024]{2,1,0:T(8,128)(2,1)S(1)}, bf16[8,56,1024]{2,1,0:T(8,128)(2,1)}, u32[]{:S(2)}) copy-start(bf16[8,56,1024]{2,1,0:T(8,128)(2,1)} %all_to_all.41) | copy-start | bytes 2752516
  111.6 12.9 %collective-permute-start.2 = (bf16[8,56,1024]{2,1,0:T(8,128)(2,1)S(1)}, bf16[8,56,1024]{2,1,0:T(8,128)(2,1)S(1)}, u32[]{:S(2)}, u32[]{:S(2)}) collective-permute-start(bf16[8,56,1024]{2,1,0:T(8,128)(2,1)S(1)} %fusion.4), channel_id=1, source_target_pairs={{0,16},{16,0},{1,17},{17,1},{2,18},{18,2},{3,19},{19,3},{4,20},{20... | collective-permute-start | bytes 2752520 | tf_op jit(solution)/shard_map/ppermute | solution.py:21
  121.1 1.3 copy-start
  123.4 6.8 %collective-permute-start.4 = (bf16[8,56,1024]{2,1,0:T(8,128)(2,1)}, bf16[8,56,1024]{2,1,0:T(8,128)(2,1)}, u32[]{:S(2)}, u32[]{:S(2)}) collective-permute-start(bf16[8,56,1024]{2,1,0:T(8,128)(2,1)} %select_bitcast_fusion), channel_id=1, source_target_pairs={{0,16},{16,0},{1,17},{17,1},{2,18},{18,2},{3,19},{19,3},{4,20},{20... | collective-permute-start | bytes 2752520 | tf_op jit(solution)/shard_map/ppermute | solution.py:21
  125.9 4.4 %copy-start.1 = (bf16[1024,896]{0,1:T(8,128)(2,1)S(1)}, bf16[1024,896]{0,1:T(8,128)(2,1)}, u32[]{:S(2)}) copy-start(bf16[1024,896]{0,1:T(8,128)(2,1)} %copy-done) | copy-start | bytes 5505028
  125.9 19.6 %all-to-all-start.4 = ((bf16[8,56,1024]{2,1,0:T(8,128)(2,1)}), bf16[8,56,1024]{2,1,0:T(8,128)(2,1)}, u32[]{:S(2)}, u32[]{:S(2)}) async-start(bf16[8,56,1024]{2,1,0:T(8,128)(2,1)} %fusion.3), calls=%async_computation.4 | async-start | bytes 1835008 | tf_op jit(solution)/shard_map/all_to_all | solution.py:59
  145.5 18.1 %all-to-all-start.6 = ((bf16[8,56,1024]{2,1,0:T(8,128)(2,1)}), bf16[8,56,1024]{2,1,0:T(8,128)(2,1)S(1)}, u32[]{:S(2)}, u32[]{:S(2)}) async-start(bf16[8,56,1024]{2,1,0:T(8,128)(2,1)} %fusion.2), calls=%async_computation.6 | async-start | bytes 1835008 | tf_op jit(solution)/shard_map/all_to_all | solution.py:59
  164.2 18.0 %copy-start.3 = (bf16[56,4,56]{2,1,0:T(4,128)(2,1)S(1)}, bf16[56,4,56]{2,1,0:T(4,128)(2,1)}, u32[]{:S(2)}) copy-start(bf16[56,4,56]{2,1,0:T(4,128)(2,1)} %param.5) | copy-start | bytes 75268
  164.2 18.0 %copy-start.5 = (f32[4]{0:T(128)S(1)}, f32[4]{0:T(128)}, u32[]{:S(2)}) copy-start(f32[4]{0:T(128)} %param.9) | copy-start | bytes 52
  165.2 16.7 %all-to-all-start.7 = ((bf16[16,56,224]{2,1,0:T(8,128)(2,1)}), bf16[16,56,224]{2,1,0:T(8,128)(2,1)S(1)}, u32[]{:S(2)}, u32[]{:S(2)}) async-start(bf16[16,56,224]{2,1,0:T(8,128)(2,1)} %bitcast.38), calls=%async_computation.7 | async-start | bytes 917504 | tf_op jit(solution)/shard_map/all_to_all | solution.py:68

commit v2 on v1

v2 whole, which is shorter than its diff:
```python
import jax
import jax.numpy as jnp
from jax import lax
from jax.sharding import Mesh
from jax.sharding import PartitionSpec as P
from jax.experimental import pallas as pl
from jax.experimental.pallas import tpu as pltpu

BLK = ("x", "y_hi", "core")
GRP = ("y_lo", "z")
PLANE = ("x", "y_hi")
BF16 = jnp.bfloat16
F32 = jnp.float32


def from_everyone(x, axis):
    count = lax.axis_size(axis)
    return lax.all_to_all(jnp.broadcast_to(x[None], (count, *x.shape)), axis, 0, 0, tiled=True)


def from_ahead(x, axis, offset):
    n = lax.axis_size(axis)
    return lax.ppermute(x, axis, [((i + offset) % n, i) for i in range(n)])


def steps_along(x, axis, order=None):
    n = lax.axis_size(axis)
    arrived = {o: from_ahead(x, axis, o) for o in (order or range(1, n))}
    return jnp.concatenate([x] + [arrived[o] for o in range(1, n)], axis=0)


def kernel_call(body, outs, args, flops=0, scratch=()):
    smem = pl.BlockSpec(memory_space=pltpu.SMEM)
    vmem = pl.BlockSpec(memory_space=pltpu.VMEM)
    moved = sum(a.size * a.dtype.itemsize for a in (*args, *outs))
    return pl.pallas_call(
        body,
        out_shape=outs,
        in_specs=[smem] + [vmem] * (len(args) - 1),
        out_specs=[vmem] * len(outs),
        scratch_shapes=list(scratch),
        cost_estimate=pl.CostEstimate(flops=flops, bytes_accessed=moved, transcendentals=0),
        compiler_params=pltpu.CompilerParams(vmem_limit_bytes=40 * 2**20),
    )(*args)


def placed_by_block(place, pieces, n_x, n_h):
    count = len(pieces)

    def body(place, *refs):
        out = refs[-1]
        for i in range(count):
            core, ox = i // n_x, i % n_x
            for oh in range(n_h):
                b = (
                    ((place[0] + ox) % n_x) * (2 * n_h)
                    + ((place[1] + oh) % n_h) * 2
                    + (place[2] + core) % 2
                )
                out[b] = refs[i][oh]

    shape = (count * n_h, *pieces[0].shape[1:])
    return kernel_call(body, [jax.ShapeDtypeStruct(shape, BF16)], [place, *pieces])[0]


def both_ways(pieces, place):
    n_l, pts, nv = pieces[0].shape
    rows = n_l * pts
    total = rows * len(pieces)

    def body(place, *refs):
        out, turned = refs[-2:]
        for i in range(0, len(pieces), 2):
            block = jnp.concatenate(
                [refs[i + j][...].reshape(rows, nv) for j in range(2)], axis=0
            )
            out[i * rows : (i + 2) * rows, :] = block
            turned[:, i * rows : (i + 2) * rows] = block.T

    outs = [jax.ShapeDtypeStruct((total, nv), BF16), jax.ShapeDtypeStruct((nv, total), BF16)]
    return kernel_call(body, outs, [place, *pieces])


def weighed(place, rows, turned, right, z_own, z_other, half, n_z, n_l):
    total, nv = rows.shape
    n_q = z_own.shape[1]
    pts = total // (2 * n_z * n_l)

    def body(place, rows, turned, right, z_own, z_other, out, weighted):
        for k in range(half):
            cols = slice(k * n_q, (k + 1) * n_q)
            for core, z in enumerate((z_own, z_other)):
                base = core * n_z * n_l * pts
                products = jnp.dot(
                    rows[base : base + n_z * n_l * pts, :],
                    right[:, cols],
                    preferred_element_type=F32,
                )
                for s in range(n_z * n_l):
                    oz, ol = s // n_l, s % n_l
                    g = ((place[1] + ol) % n_l) * n_z + (place[0] + oz) % n_z
                    zs = z[pl.ds(pl.multiple_of(g * pts, pts), pts), :]
                    weighted[base + s * pts : base + (s + 1) * pts, :] = (
                        zs * products[s * pts : (s + 1) * pts, :]
                    ).astype(BF16)
            out[:, cols] = jnp.dot(
                turned[...], weighted[...], preferred_element_type=F32
            ).astype(BF16)

    outs = [jax.ShapeDtypeStruct((nv, half * n_q), BF16)]
    flops = 4 * total * nv * half * n_q
    return kernel_call(
        body,
        outs,
        [place, rows, turned, right, z_own, z_other],
        flops,
        [pltpu.VMEM((total, n_q), BF16)],
    )[0]


def contract_last(a, b):
    return lax.dot_general(a, b, (((0,), (1,)), ((), ())), preferred_element_type=F32)


def in_core_order(own, other, axis):
    first = lax.axis_index("core") == 0
    return jnp.stack([jnp.where(first, own, other), jnp.where(first, other, own)], axis=axis)


def local(amplitudes, grid_factor, metric, virt_energy, pair_energy):
    n_c, n_k, n_d = amplitudes.shape
    _, nv = grid_factor.shape
    n_x, n_h = lax.axis_size("x"), lax.axis_size("y_hi")
    n_z, n_l = lax.axis_size("z"), lax.axis_size("y_lo")
    n_plane, n_grp = n_x * n_h, n_z * n_l
    my_x, my_h, my_core = lax.axis_index("x"), lax.axis_index("y_hi"), lax.axis_index("core")
    my_z, my_l = lax.axis_index("z"), lax.axis_index("y_lo")
    half = n_k // 2
    first = my_core == 0

    turned = amplitudes.transpose(2, 1, 0)
    low = turned[:, :half].reshape(n_d, half * n_c)
    high = turned[:, half:].reshape(n_d, half * n_c)
    other = from_ahead(jnp.where(first, high, low), "core", 1).reshape(n_d, half, n_c)
    own = jnp.where(first, low, high).reshape(n_d, half, n_c)
    turned = in_core_order(own, other, 2).reshape(n_d, half * 2 * n_c)
    turned = from_everyone(turned, GRP).reshape(nv, half * 2 * n_c)

    mine = steps_along(grid_factor[None], "y_hi")
    own = [mine] + [from_ahead(mine, "x", o) for o in range(1, n_x)]
    own += [from_ahead(piece, "core", 1) for piece in own]
    columns = placed_by_block(jnp.stack([my_x, my_h, my_core]), own, n_x, n_h).reshape(-1, nv)
    n_q = columns.shape[0]

    right = contract_last(turned, columns).astype(BF16)
    right = right.reshape(half, 2 * n_c, n_q).transpose(1, 0, 2).reshape(2 * n_c, half * n_q)
    right = from_everyone(right, PLANE).reshape(nv, half * n_q)

    pair = steps_along(grid_factor[None], "y_lo")
    own = {0: pair}
    up = down = pair
    for o in range(1, n_z // 2 + 1):
        up = from_ahead(up, "z", 1)
        if o < n_z - o:
            down = from_ahead(down, "z", -1)
            up, down = lax.optimization_barrier((up, down))
            own[n_z - o] = down
        own[o] = up
    own = [own[o] for o in range(n_z)]
    own += [from_ahead(piece, "core", 1) for piece in own]
    place = jnp.stack([my_z, my_l])
    rows, rows_turned = both_ways(own, place)
    z = metric.reshape(-1, n_q)
    z_other = from_ahead(z, "core", 1)
    back = weighed(place, rows, rows_turned, right, z, z_other, half, n_z, n_l)
    back = back.reshape(n_plane, 2 * n_c, half * n_q)
    back = lax.all_to_all(back, PLANE, 0, 0, tiled=True)
    back = back.astype(F32).sum(axis=0).astype(BF16)
    back = back.reshape(2 * n_c, half, n_q).transpose(1, 0, 2).reshape(half * 2 * n_c, n_q)
    ladder = contract_last(columns, back).astype(BF16).reshape(n_grp, n_d, half * 2 * n_c)
    ladder = lax.all_to_all(ladder, GRP, 0, 0, tiled=True)
    ladder = ladder.astype(F32).sum(axis=0).reshape(n_d, half, 2, n_c)
    keep = jnp.where(first, ladder[:, :, 0], ladder[:, :, 1])
    give = jnp.where(first, ladder[:, :, 1], ladder[:, :, 0])
    other = from_ahead(give.reshape(n_d, half * n_c), "core", 1).reshape(n_d, half, n_c)
    ladder = in_core_order(keep, other, 1).reshape(n_d, n_k, n_c).transpose(2, 1, 0)
    first_energy = lax.dynamic_slice_in_dim(virt_energy, lax.axis_index(BLK) * n_c, n_c)
    second_energy = lax.dynamic_slice_in_dim(virt_energy, lax.axis_index(GRP) * n_d, n_d)
    denominator = (
        first_energy[:, None, None] + second_energy[None, None, :] - pair_energy[None, :, None]
    )
    return denominator * amplitudes.astype(F32) + ladder


def solution(mesh):
    split = Mesh(mesh.devices.reshape(4, 2, 2, 2, 8), ("x", "y_hi", "core", "y_lo", "z"))
    in_specs = (P(BLK, None, GRP), P(BLK + GRP, None), P(BLK, GRP, None), P(), P())
    return jax.shard_map(
        local, mesh=split, in_specs=in_specs, out_specs=P(BLK, None, GRP), check_vma=False
    )
```

time: 185 us -> 149 us (0.81)
  waiting for transfers between devices: 73 us -> 26.4 us
  starting transfers between devices: 43.5 us -> 58.9 us
  other arithmetic: 11.8 us -> 1.27 us
  local copies, waits for them, and re-layouts: 11.8 us -> 21.6 us
  Pallas kernels: 0 us -> 8.2 us
  matrix products: 7.54 us -> 0.92 us
  blocking collectives: 34.8 us -> 30.7 us
    all_to_all x3 -> x2, waiting for transfers between devices: 36.6 us -> 0.01 us  [from_everyone(): lax.all_to_all(jnp.broadcast_to(x[None], (count, *x.shape)), axis, 0, 0,...]
    ppermute x5 -> x27, starting transfers between devices: 12.1 us -> 40.7 us  [from_ahead(): return lax.ppermute(x, axis, [((i + offset) % n, i) for i in range(n)])]
    all_to_all x3 -> x1, waiting for transfers between devices: 36.4 us -> 10 us  [local(): ladder = lax.all_to_all(ladder, GRP, 0, 0, tiled=True)]
    ppermute x5 -> x27, waiting for transfers between devices: 0.01 us -> 16.3 us  [from_ahead(): return lax.ppermute(x, axis, [((i + offset) % n, i) for i in range(n)])]
    unnamed x14 -> x38, local copies, waits for them, and re-layouts: 1.3 us -> 15.7 us
    pallas_call x0 -> x3, Pallas kernels: none -> 8.2 us  [kernel_call(): pl.pallas_call(body, out_shape=outs, in_specs=[smem] + [vmem] * (len(args...]
    all_to_all x3 -> x2, starting transfers between devices: 18.8 us -> 11.2 us  [from_everyone(): lax.all_to_all(jnp.broadcast_to(x[None], (count, *x.shape)), axis, 0, 0,...]
    dot_general x7 -> x2, matrix products: 7.54 us -> 0.92 us  [contract_last(): lax.dot_general(a, b, (((0,), (1,)), ((), ())), preferred_element_type=F32)]
  transfers between devices with their start and end apart: 11 -> 30, of which waited for: 6 -> 11; matrix products, arithmetic and copies ran while one was open for 13% -> 2% of each run, Pallas kernels for 0% -> 2%
where the time goes in v2:
time: 149 us; the launch traced here: 148 us
  starting transfers between devices  58.9 us (40%)
  blocking collectives  30.7 us (21%)
  waiting for transfers between devices  26.4 us (18%)
  local copies, waits for them, and re-layouts  21.6 us (14%)
  Pallas kernels  8.2 us (6%)
    ppermute x27, starting transfers between devices, from_ahead(): return lax.ppermute(x, axis, [((i + offset) % n, i) for i in range(n)])  40.7 us
    all_to_all x1, blocking collectives, local(): back = lax.all_to_all(back, PLANE, 0, 0, tiled=True)  30.7 us
    ppermute x27, waiting for transfers between devices, from_ahead(): return lax.ppermute(x, axis, [((i + offset) % n, i) for i in range(n)])  16.3 us
    unnamed x38, local copies, waits for them, and re-layouts  15.7 us
    all_to_all x2, starting transfers between devices, from_everyone(): lax.all_to_all(jnp.broadcast_to(x[None], (count, *x.shape)), axis, 0, 0,...  11.2 us
    all_to_all x1, waiting for transfers between devices, local(): ladder = lax.all_to_all(ladder, GRP, 0, 0, tiled=True)  10 us
    pallas_call x3, Pallas kernels, kernel_call(): pl.pallas_call(body, out_shape=outs, in_specs=[smem] + [vmem] * (len(args...  8.2 us
    all_to_all x1, starting transfers between devices, local(): ladder = lax.all_to_all(ladder, GRP, 0, 0, tiled=True)  6.99 us
  transfers between devices with their start and end apart: 30, of which 11 were waited for; matrix products, arithmetic and copies ran while one was open for 2% of the time, Pallas kernels for 2%

profile of v2, /device:TPU:1, one launch (start us, length us, event | category | flops | bytes accessed | tf_op | source)
XLA Modules:
  0.0 148.3 jit_solution(2379563044367405895)
XLA Ops:
  0.0 0.9 copy.11
  1.1 3.3 %collective-permute-start.24 = (bf16[56,112]{1,0:T(8,128)(2,1)S(1)}, bf16[56,112]{1,0:T(8,128)(2,1)S(1)}, u32[]{:S(2)}, u32[]{:S(2)}) collective-permute-start(bf16[56,112]{1,0:T(8,128)(2,1)S(1)} %select_n.93), channel_id=1, source_target_pairs={{16,0},{0,16},{17,1},{1,17},{18,2},{2,18},{19,3},{3,19},{20,4},{4,... | collective-permute-start | bytes 37640 | tf_op jit(solution)/shard_map/ppermute | solution.py:23
  4.4 0.8 collective-permute-done.24
  5.7 0.8 broadcast_in_dim.23
  6.5 7.6 %all-to-all-start = ((bf16[16,56,224]{2,1,0:T(8,128)(2,1)}), bf16[16,56,224]{2,1,0:T(8,128)(2,1)S(1)}, u32[]{:S(2)}, u32[]{:S(2)}) async-start(bf16[16,56,224]{2,1,0:T(8,128)(2,1)} %broadcast_in_dim.23), calls=%async_computation | async-start | bytes 917504 | tf_op jit(solution)/shard_map/all_to_all | solution.py:18
  14.1 2.7 %collective-permute-start = (bf16[1,32,896]{2,1,0:T(8,128)(2,1)S(1)}, bf16[1,32,896]{2,1,0:T(8,128)(2,1)S(1)}, u32[]{:S(2)}, u32[]{:S(2)}) collective-permute-start(bf16[1,32,896]{2,1,0:T(8,128)(2,1)S(1)} %bitcast.54), channel_id=1, source_target_pairs={{32,0},{0,32},{33,1},{1,33},{34,2},{2,34},{35,3},{3,35},{36,4},{4,... | collective-permute-start | bytes 172040 | tf_op jit(solution)/shard_map/ppermute | solution.py:23
  16.8 0.8 collective-permute-start.8
  17.5 1.3 collective-permute-done
  18.8 1.9 %collective-permute-done.8 = bf16[1,32,896]{2,1,0:T(8,128)(2,1)S(1)} collective-permute-done((bf16[1,32,896]{2,1,0:T(8,128)(2,1)S(1)}, bf16[1,32,896]{2,1,0:T(8,128)(2,1)S(1)}, u32[]{:S(2)}, u32[]{:S(2)}) %collective-permute-start.8) | collective-permute-done | bytes 57376 | tf_op jit(solution)/shard_map/ppermute | solution.py:23
  20.7 2.6 %collective-permute-start.1 = (bf16[2,32,896]{2,1,0:T(8,128)(2,1)S(1)}, bf16[2,32,896]{2,1,0:T(8,128)(2,1)S(1)}, u32[]{:S(2)}, u32[]{:S(2)}) collective-permute-start(bf16[2,32,896]{2,1,0:T(8,128)(2,1)S(1)} %get-tuple-element.27.refs_0_), channel_id=1, source_target_pairs={{64,0},{128,64},{192,128},{0,192},{65,1},{129,65},{193,129},{1,193... | collective-permute-start | bytes 344072 | tf_op jit(solution)/shard_map/ppermute | solution.py:23
  24.4 4.2 %collective-permute-start.4 = (bf16[2,32,896]{2,1,0:T(8,128)(2,1)S(1)}, bf16[2,32,896]{2,1,0:T(8,128)(2,1)S(1)}, u32[]{:S(2)}, u32[]{:S(2)}) collective-permute-start(bf16[2,32,896]{2,1,0:T(8,128)(2,1)S(1)} %get-tuple-element.27.refs_0_), channel_id=1, source_target_pairs={{16,0},{0,16},{17,1},{1,17},{18,2},{2,18},{19,3},{3,19},{20,4},{4,... | collective-permute-start | bytes 344072 | tf_op jit(solution)/shard_map/ppermute | solution.py:23
  29.3 4.0 %collective-permute-start.6 = (bf16[2,32,896]{2,1,0:T(8,128)(2,1)S(1)}, bf16[2,32,896]{2,1,0:T(8,128)(2,1)S(1)}, u32[]{:S(2)}, u32[]{:S(2)}) collective-permute-start(bf16[2,32,896]{2,1,0:T(8,128)(2,1)S(1)} %collective-permute-done.2.refs_2_), channel_id=1, source_target_pairs={{16,0},{0,16},{17,1},{1,17},{18,2},{2,18},{19,3},{3,19},{20,4},{4,... | collective-permute-start | bytes 344072 | tf_op jit(solution)/shard_map/ppermute | solution.py:23
  33.3 1.1 collective-permute-start.7
  34.5 0.9 collective-permute-done.7.refs_7_
  36.8 1.5 %broadcast_in_dim.25 = bf16[8,112,1024]{2,1,0:T(8,128)(2,1)} broadcast(bf16[112,1024]{1,0:T(8,128)(2,1)S(1)} %bitcast.47), dimensions={1,2} | broadcast | bytes 2064384 | tf_op jit(solution)/shard_map/broadcast_in_dim | solution.py:18
  38.3 3.6 %all-to-all-start.1 = ((bf16[8,112,1024]{2,1,0:T(8,128)(2,1)}), bf16[8,112,1024]{2,1,0:T(8,128)(2,1)S(1)}, u32[]{:S(2)}, u32[]{:S(2)}) async-start(bf16[8,112,1024]{2,1,0:T(8,128)(2,1)} %broadcast_in_dim.25), calls=%async_computation.1 | async-start | bytes 3670016 | tf_op jit(solution)/shard_map/all_to_all | solution.py:18
  41.9 2.3 %copy.21 = f32[512,1,512]{2,0,1:T(8,128)} copy(f32[512,1,512]{2,1,0:T(1,128)} %param.7) | data formatting | bytes 2097152
  44.6 1.2 collective-permute-start.10
  45.8 1.5 collective-permute-start.9
  47.3 3.1 %collective-permute-done.10.refs_7_ = bf16[2,32,896]{2,1,0:T(8,128)(2,1)S(1)} collective-permute-done((bf16[2,32,896]{2,1,0:T(8,128)(2,1)S(1)}, bf16[2,32,896]{2,1,0:T(8,128)(2,1)S(1)}, u32[]{:S(2)}, u32[]{:S(2)}) %collective-permute-start.10) | collective-permute-done | bytes 114720 | tf_op jit(solution)/shard_map/ppermute | solution.py:23
  50.3 2.4 %collective-permute-start.11 = (bf16[2,32,896]{2,1,0:T(8,128)(2,1)S(1)}, bf16[2,32,896]{2,1,0:T(8,128)(2,1)S(1)}, u32[]{:S(2)}, u32[]{:S(2)}) collective-permute-start(bf16[2,32,896]{2,1,0:T(8,128)(2,1)S(1)} %collective-permute-done.9.refs_1_), channel_id=1, source_target_pairs={{1,0},{2,1},{3,2},{4,3},{5,4},{6,5},{7,6},{0,7},{9,8},{10,9},{11,1... | collective-permute-start | bytes 344072 | tf_op jit(solution)/shard_map/ppermute | solution.py:23
  52.7 1.8 %collective-permute-done.11.refs_2_ = bf16[2,32,896]{2,1,0:T(8,128)(2,1)S(1)} collective-permute-done((bf16[2,32,896]{2,1,0:T(8,128)(2,1)S(1)}, bf16[2,32,896]{2,1,0:T(8,128)(2,1)S(1)}, u32[]{:S(2)}, u32[]{:S(2)}) %collective-permute-start.11) | collective-permute-done | bytes 114720 | tf_op jit(solution)/shard_map/ppermute | solution.py:23
  54.5 3.4 %collective-permute-done.12.refs_6_ = bf16[2,32,896]{2,1,0:T(8,128)(2,1)S(1)} collective-permute-done((bf16[2,32,896]{2,1,0:T(8,128)(2,1)S(1)}, bf16[2,32,896]{2,1,0:T(8,128)(2,1)S(1)}, u32[]{:S(2)}, u32[]{:S(2)}) %collective-permute-start.12) | collective-permute-done | bytes 114720 | tf_op jit(solution)/shard_map/ppermute | solution.py:23
  57.9 1.5 collective-permute-start.14
  59.3 3.0 %collective-permute-start.16 = (bf16[2,32,896]{2,1,0:T(8,128)(2,1)S(1)}, bf16[2,32,896]{2,1,0:T(8,128)(2,1)S(1)}, u32[]{:S(2)}, u32[]{:S(2)}) collective-permute-start(bf16[2,32,896]{2,1,0:T(8,128)(2,1)S(1)} %get-tuple-element.28.refs_0_), channel_id=1, source_target_pairs={{16,0},{0,16},{17,1},{1,17},{18,2},{2,18},{19,3},{3,19},{20,4},{4,... | collective-permute-start | bytes 344072 | tf_op jit(solution)/shard_map/ppermute | solution.py:23
  62.4 2.8 %collective-permute-start.23 = (bf16[2,32,896]{2,1,0:T(8,128)(2,1)S(1)}, bf16[2,32,896]{2,1,0:T(8,128)(2,1)S(1)}, u32[]{:S(2)}, u32[]{:S(2)}) collective-permute-start(bf16[2,32,896]{2,1,0:T(8,128)(2,1)S(1)} %collective-permute-done.10.refs_7_), channel_id=1, source_target_pairs={{16,0},{0,16},{17,1},{1,17},{18,2},{2,18},{19,3},{3,19},{20,4},{4,... | collective-permute-start | bytes 344072 | tf_op jit(solution)/shard_map/ppermute | solution.py:23
  65.1 1.2 collective-permute-start.18
  67.0 0.8 collective-permute-start.15
  70.5 1.3 collective-permute-done.15.refs_4_
  71.8 0.9 collective-permute-start.20
  72.7 1.2 collective-permute-done.20.refs_12_
  74.0 0.9 copy-done.1
  74.9 0.9 copy-done.3
  75.8 0.9 copy-done.5
  76.6 0.9 copy-done.7
  77.5 1.8 %shard_map.56 = (bf16[1024,896]{1,0:T(8,128)(2,1)S(1)}, bf16[896,1024]{1,0:T(8,128)(2,1)S(1)}) custom-call(s32[2]{0:T(128)S(1)} %pad_add_fusion.place, bf16[2,32,896]{2,1,0:T(8,128)(2,1)S(1)} %get-tuple-element.28.refs_0_, bf16[2,32,896]{2,1,0:T(8,128)(2,1)S(1)} %collective-permute-done.9.refs_1_, bf16[2,32,896]{2,1,0:T(8,128)(2,1)S(1)} %collective-permute-done.11.refs_2_, ...), custom_call_target="tpu_custom_call" | custom-call | bytes 5505032 | tf_op jit(solution)/shard_map/pallas_call | solution.py:36
  79.4 1.2 copy-done.10
  80.6 1.2 copy-done.12
  82.5 1.5 %copy-done.11 = bf16[1024,896]{1,0:T(8,128)(2,1)S(1)} copy-done((bf16[1024,896]{1,0:T(8,128)(2,1)S(1)}, bf16[1024,896]{1,0:T(8,128)(2,1)}, u32[]{:S(2)}) %copy-start.11) | copy-done | bytes 1835032
  84.0 1.5 %copy-done.13 = bf16[896,1024]{1,0:T(8,128)(2,1)S(1)} copy-done((bf16[896,1024]{1,0:T(8,128)(2,1)S(1)}, bf16[896,1024]{1,0:T(8,128)(2,1)}, u32[]{:S(2)}) %copy-start.13) | copy-done | bytes 1835032
  85.5 5.8 %shard_map.57 = bf16[896,1024]{1,0:T(8,128)(2,1)S(1)} custom-call(s32[2]{0:T(128)S(1)} %copy-done.9, bf16[1024,896]{1,0:T(8,128)(2,1)S(1)} %copy-done.11, bf16[896,1024]{1,0:T(8,128)(2,1)S(1)} %copy-done.13, bf16[896,1024]{1,0:T(8,128)(2,1)S(1)} %bitcast.40, f32[512,512]{1,0:T(8,128)} %bitcast.33.z_own, f32[512,512]{1,0:T(8,128)} %collective-permute-done.25.z_other), custom_call_target="tpu_custom_call" | custom-call | flops 3758096384 | bytes 9437192 | tf_op jit(solution)/shard_map/pallas_call | solution.py:36
  91.3 30.7 %all_to_all.20 = bf16[8,112,1024]{2,1,0:T(8,128)(2,1)S(1)} all-to-all(bf16[8,112,1024]{2,1,0:T(8,128)(2,1)S(1)} %bitcast.41), channel_id=1, replica_groups=mesh['x'=4,'y_hi'=2,'core'=2,'y_lo'=2,'z'=8] {'x','y_hi'}, dimensions={0} | all-to-all | bytes 3670016 | tf_op jit(solution)/shard_map/all_to_all | solution.py:177
  123.0 1.0 copy.15
  123.9 7.0 %all-to-all-start.3 = ((bf16[16,56,224]{2,1,0:T(8,128)(2,1)}), bf16[16,56,224]{2,1,0:T(8,128)(2,1)S(1)}, u32[]{:S(2)}, u32[]{:S(2)}) async-start(bf16[16,56,224]{2,1,0:T(8,128)(2,1)} %bitcast.17), calls=%async_computation.3 | async-start | bytes 917504 | tf_op jit(solution)/shard_map/all_to_all | solution.py:181
  130.9 0.8 fusion.3
  131.8 10.0 %all-to-all-done.3 = bf16[16,56,224]{2,1,0:T(8,128)(2,1)S(1)} async-done(((bf16[16,56,224]{2,1,0:T(8,128)(2,1)}), bf16[16,56,224]{2,1,0:T(8,128)(2,1)S(1)}, u32[]{:S(2)}, u32[]{:S(2)}) %all-to-all-start.3) | async-done | bytes 401440 | tf_op jit(solution)/shard_map/all_to_all | solution.py:181
  142.4 4.0 %collective-permute-start.26 = (f32[56,112]{1,0:T(8,128)S(1)}, f32[56,112]{1,0:T(8,128)S(1)}, u32[]{:S(2)}, u32[]{:S(2)}) collective-permute-start(f32[56,112]{1,0:T(8,128)S(1)} %select_n.99), channel_id=1, source_target_pairs={{16,0},{0,16},{17,1},{1,17},{18,2},{2,18},{19,3},{3,19},{20,4},{4,... | collective-permute-start | bytes 75272 | tf_op jit(solution)/shard_map/ppermute | solution.py:23
  147.5 0.7 copy.17
  (85 shorter events, 11.0 us)
Async XLA Ops:
  0.0 14.1 %copy-start.15 = (bf16[32,896]{1,0:T(8,128)(2,1)S(1)}, bf16[32,896]{1,0:T(8,128)(2,1)}, u32[]{:S(2)}) copy-start(bf16[32,896]{1,0:T(8,128)(2,1)} %param.6) | copy-start | bytes 172036
  1.1 4.1 %collective-permute-start.24 = (bf16[56,112]{1,0:T(8,128)(2,1)S(1)}, bf16[56,112]{1,0:T(8,128)(2,1)S(1)}, u32[]{:S(2)}, u32[]{:S(2)}) collective-permute-start(bf16[56,112]{1,0:T(8,128)(2,1)S(1)} %select_n.93), channel_id=1, source_target_pairs={{16,0},{0,16},{17,1},{1,17},{18,2},{2,18},{19,3},{3,19},{20,4},{4,... | collective-permute-start | bytes 37640 | tf_op jit(solution)/shard_map/ppermute | solution.py:23
  6.5 29.6 %all-to-all-start = ((bf16[16,56,224]{2,1,0:T(8,128)(2,1)}), bf16[16,56,224]{2,1,0:T(8,128)(2,1)S(1)}, u32[]{:S(2)}, u32[]{:S(2)}) async-start(bf16[16,56,224]{2,1,0:T(8,128)(2,1)} %broadcast_in_dim.23), calls=%async_computation | async-start | bytes 917504 | tf_op jit(solution)/shard_map/all_to_all | solution.py:18
  14.1 4.8 %collective-permute-start = (bf16[1,32,896]{2,1,0:T(8,128)(2,1)S(1)}, bf16[1,32,896]{2,1,0:T(8,128)(2,1)S(1)}, u32[]{:S(2)}, u32[]{:S(2)}) collective-permute-start(bf16[1,32,896]{2,1,0:T(8,128)(2,1)S(1)} %bitcast.54), channel_id=1, source_target_pairs={{32,0},{0,32},{33,1},{1,33},{34,2},{2,34},{35,3},{3,35},{36,4},{4,... | collective-permute-start | bytes 172040 | tf_op jit(solution)/shard_map/ppermute | solution.py:23
  16.8 3.9 %collective-permute-start.8 = (bf16[1,32,896]{2,1,0:T(8,128)(2,1)S(1)}, bf16[1,32,896]{2,1,0:T(8,128)(2,1)S(1)}, u32[]{:S(2)}, u32[]{:S(2)}) collective-permute-start(bf16[1,32,896]{2,1,0:T(8,128)(2,1)S(1)} %bitcast.55), channel_id=1, source_target_pairs={{8,0},{0,8},{9,1},{1,9},{10,2},{2,10},{11,3},{3,11},{12,4},{4,12},... | collective-permute-start | bytes 172040 | tf_op jit(solution)/shard_map/ppermute | solution.py:23
  20.7 7.9 %collective-permute-start.1 = (bf16[2,32,896]{2,1,0:T(8,128)(2,1)S(1)}, bf16[2,32,896]{2,1,0:T(8,128)(2,1)S(1)}, u32[]{:S(2)}, u32[]{:S(2)}) collective-permute-start(bf16[2,32,896]{2,1,0:T(8,128)(2,1)S(1)} %get-tuple-element.27.refs_0_), channel_id=1, source_target_pairs={{64,0},{128,64},{192,128},{0,192},{65,1},{129,65},{193,129},{1,193... | collective-permute-start | bytes 344072 | tf_op jit(solution)/shard_map/ppermute | solution.py:23
  23.3 6.0 %collective-permute-start.2 = (bf16[2,32,896]{2,1,0:T(8,128)(2,1)S(1)}, bf16[2,32,896]{2,1,0:T(8,128)(2,1)S(1)}, u32[]{:S(2)}, u32[]{:S(2)}) collective-permute-start(bf16[2,32,896]{2,1,0:T(8,128)(2,1)S(1)} %get-tuple-element.27.refs_0_), channel_id=1, source_target_pairs={{128,0},{192,64},{0,128},{64,192},{129,1},{193,65},{1,129},{65,193... | collective-permute-start | bytes 344072 | tf_op jit(solution)/shard_map/ppermute | solution.py:23
  23.8 9.5 %collective-permute-start.3 = (bf16[2,32,896]{2,1,0:T(8,128)(2,1)S(1)}, bf16[2,32,896]{2,1,0:T(8,128)(2,1)S(1)}, u32[]{:S(2)}, u32[]{:S(2)}) collective-permute-start(bf16[2,32,896]{2,1,0:T(8,128)(2,1)S(1)} %get-tuple-element.27.refs_0_), channel_id=1, source_target_pairs={{192,0},{0,64},{64,128},{128,192},{193,1},{1,65},{65,129},{129,193... | collective-permute-start | bytes 344072 | tf_op jit(solution)/shard_map/ppermute | solution.py:23
  24.4 10.1 %collective-permute-start.4 = (bf16[2,32,896]{2,1,0:T(8,128)(2,1)S(1)}, bf16[2,32,896]{2,1,0:T(8,128)(2,1)S(1)}, u32[]{:S(2)}, u32[]{:S(2)}) collective-permute-start(bf16[2,32,896]{2,1,0:T(8,128)(2,1)S(1)} %get-tuple-element.27.refs_0_), channel_id=1, source_target_pairs={{16,0},{0,16},{17,1},{1,17},{18,2},{2,18},{19,3},{3,19},{20,4},{4,... | collective-permute-start | bytes 344072 | tf_op jit(solution)/shard_map/ppermute | solution.py:23
  28.6 5.9 %collective-permute-start.5 = (bf16[2,32,896]{2,1,0:T(8,128)(2,1)S(1)}, bf16[2,32,896]{2,1,0:T(8,128)(2,1)S(1)}, u32[]{:S(2)}, u32[]{:S(2)}) collective-permute-start(bf16[2,32,896]{2,1,0:T(8,128)(2,1)S(1)} %collective-permute-done.1.refs_1_), channel_id=1, source_target_pairs={{16,0},{0,16},{17,1},{1,17},{18,2},{2,18},{19,3},{3,19},{20,4},{4,... | collective-permute-start | bytes 344072 | tf_op jit(solution)/shard_map/ppermute | solution.py:23
  29.3 5.2 %collective-permute-start.6 = (bf16[2,32,896]{2,1,0:T(8,128)(2,1)S(1)}, bf16[2,32,896]{2,1,0:T(8,128)(2,1)S(1)}, u32[]{:S(2)}, u32[]{:S(2)}) collective-permute-start(bf16[2,32,896]{2,1,0:T(8,128)(2,1)S(1)} %collective-permute-done.2.refs_2_), channel_id=1, source_target_pairs={{16,0},{0,16},{17,1},{1,17},{18,2},{2,18},{19,3},{3,19},{20,4},{4,... | collective-permute-start | bytes 344072 | tf_op jit(solution)/shard_map/ppermute | solution.py:23
  33.3 2.1 %collective-permute-start.7 = (bf16[2,32,896]{2,1,0:T(8,128)(2,1)S(1)}, bf16[2,32,896]{2,1,0:T(8,128)(2,1)S(1)}, u32[]{:S(2)}, u32[]{:S(2)}) collective-permute-start(bf16[2,32,896]{2,1,0:T(8,128)(2,1)S(1)} %collective-permute-done.3.refs_3_), channel_id=1, source_target_pairs={{16,0},{0,16},{17,1},{1,17},{18,2},{2,18},{19,3},{3,19},{20,4},{4,... | collective-permute-start | bytes 344072 | tf_op jit(solution)/shard_map/ppermute | solution.py:23
  38.3 43.5 %all-to-all-start.1 = ((bf16[8,112,1024]{2,1,0:T(8,128)(2,1)}), bf16[8,112,1024]{2,1,0:T(8,128)(2,1)S(1)}, u32[]{:S(2)}, u32[]{:S(2)}) async-start(bf16[8,112,1024]{2,1,0:T(8,128)(2,1)} %broadcast_in_dim.25), calls=%async_computation.1 | async-start | bytes 3670016 | tf_op jit(solution)/shard_map/all_to_all | solution.py:18
  44.2 37.6 %collective-permute-start.25 = (f32[512,512]{1,0:T(8,128)}, f32[512,512]{1,0:T(8,128)}, u32[]{:S(2)}, u32[]{:S(2)}) collective-permute-start(f32[512,512]{1,0:T(8,128)} %bitcast.33.z_own), channel_id=1, source_target_pairs={{16,0},{0,16},{17,1},{1,17},{18,2},{2,18},{19,3},{3,19},{20,4},{4,... | collective-permute-start | bytes 3145736 | tf_op jit(solution)/shard_map/ppermute | solution.py:23
  44.6 5.7 %collective-permute-start.10 = (bf16[2,32,896]{2,1,0:T(8,128)(2,1)S(1)}, bf16[2,32,896]{2,1,0:T(8,128)(2,1)S(1)}, u32[]{:S(2)}, u32[]{:S(2)}) collective-permute-start(bf16[2,32,896]{2,1,0:T(8,128)(2,1)S(1)} %get-tuple-element.28.refs_0_), channel_id=1, source_target_pairs={{7,0},{0,1},{1,2},{2,3},{3,4},{4,5},{5,6},{6,7},{15,8},{8,9},{9,10... | collective-permute-start | bytes 344072 | tf_op jit(solution)/shard_map/ppermute | solution.py:23
  45.8 4.5 %collective-permute-start.9 = (bf16[2,32,896]{2,1,0:T(8,128)(2,1)S(1)}, bf16[2,32,896]{2,1,0:T(8,128)(2,1)S(1)}, u32[]{:S(2)}, u32[]{:S(2)}) collective-permute-start(bf16[2,32,896]{2,1,0:T(8,128)(2,1)S(1)} %get-tuple-element.28.refs_0_), channel_id=1, source_target_pairs={{1,0},{2,1},{3,2},{4,3},{5,4},{6,5},{7,6},{0,7},{9,8},{10,9},{11,1... | collective-permute-start | bytes 344072 | tf_op jit(solution)/shard_map/ppermute | solution.py:23
  50.3 4.2 %collective-permute-start.11 = (bf16[2,32,896]{2,1,0:T(8,128)(2,1)S(1)}, bf16[2,32,896]{2,1,0:T(8,128)(2,1)S(1)}, u32[]{:S(2)}, u32[]{:S(2)}) collective-permute-start(bf16[2,32,896]{2,1,0:T(8,128)(2,1)S(1)} %collective-permute-done.9.refs_1_), channel_id=1, source_target_pairs={{1,0},{2,1},{3,2},{4,3},{5,4},{6,5},{7,6},{0,7},{9,8},{10,9},{11,1... | collective-permute-start | bytes 344072 | tf_op jit(solution)/shard_map/ppermute | solution.py:23
  52.7 5.1 %collective-permute-start.12 = (bf16[2,32,896]{2,1,0:T(8,128)(2,1)S(1)}, bf16[2,32,896]{2,1,0:T(8,128)(2,1)S(1)}, u32[]{:S(2)}, u32[]{:S(2)}) collective-permute-start(bf16[2,32,896]{2,1,0:T(8,128)(2,1)S(1)} %collective-permute-done.10.refs_7_), channel_id=1, source_target_pairs={{7,0},{0,1},{1,2},{2,3},{3,4},{4,5},{5,6},{6,7},{15,8},{8,9},{9,10... | collective-permute-start | bytes 344072 | tf_op jit(solution)/shard_map/ppermute | solution.py:23
  57.9 4.5 %collective-permute-start.13 = (bf16[2,32,896]{2,1,0:T(8,128)(2,1)S(1)}, bf16[2,32,896]{2,1,0:T(8,128)(2,1)S(1)}, u32[]{:S(2)}, u32[]{:S(2)}) collective-permute-start(bf16[2,32,896]{2,1,0:T(8,128)(2,1)S(1)} %collective-permute-done.11.refs_2_), channel_id=1, source_target_pairs={{1,0},{2,1},{3,2},{4,3},{5,4},{6,5},{7,6},{0,7},{9,8},{10,9},{11,1... | collective-permute-start | bytes 344072 | tf_op jit(solution)/shard_map/ppermute | solution.py:23
  57.9 7.2 %collective-permute-start.14 = (bf16[2,32,896]{2,1,0:T(8,128)(2,1)S(1)}, bf16[2,32,896]{2,1,0:T(8,128)(2,1)S(1)}, u32[]{:S(2)}, u32[]{:S(2)}) collective-permute-start(bf16[2,32,896]{2,1,0:T(8,128)(2,1)S(1)} %collective-permute-done.12.refs_6_), channel_id=1, source_target_pairs={{7,0},{0,1},{1,2},{2,3},{3,4},{4,5},{5,6},{6,7},{15,8},{8,9},{9,10... | collective-permute-start | bytes 344072 | tf_op jit(solution)/shard_map/ppermute | solution.py:23
  59.3 7.0 %collective-permute-start.16 = (bf16[2,32,896]{2,1,0:T(8,128)(2,1)S(1)}, bf16[2,32,896]{2,1,0:T(8,128)(2,1)S(1)}, u32[]{:S(2)}, u32[]{:S(2)}) collective-permute-start(bf16[2,32,896]{2,1,0:T(8,128)(2,1)S(1)} %get-tuple-element.28.refs_0_), channel_id=1, source_target_pairs={{16,0},{0,16},{17,1},{1,17},{18,2},{2,18},{19,3},{3,19},{20,4},{4,... | collective-permute-start | bytes 344072 | tf_op jit(solution)/shard_map/ppermute | solution.py:23
  62.3 5.4 %collective-permute-start.17 = (bf16[2,32,896]{2,1,0:T(8,128)(2,1)S(1)}, bf16[2,32,896]{2,1,0:T(8,128)(2,1)S(1)}, u32[]{:S(2)}, u32[]{:S(2)}) collective-permute-start(bf16[2,32,896]{2,1,0:T(8,128)(2,1)S(1)} %collective-permute-done.9.refs_1_), channel_id=1, source_target_pairs={{16,0},{0,16},{17,1},{1,17},{18,2},{2,18},{19,3},{3,19},{20,4},{4,... | collective-permute-start | bytes 344072 | tf_op jit(solution)/shard_map/ppermute | solution.py:23
  62.4 6.4 %collective-permute-start.23 = (bf16[2,32,896]{2,1,0:T(8,128)(2,1)S(1)}, bf16[2,32,896]{2,1,0:T(8,128)(2,1)S(1)}, u32[]{:S(2)}, u32[]{:S(2)}) collective-permute-start(bf16[2,32,896]{2,1,0:T(8,128)(2,1)S(1)} %collective-permute-done.10.refs_7_), channel_id=1, source_target_pairs={{16,0},{0,16},{17,1},{1,17},{18,2},{2,18},{19,3},{3,19},{20,4},{4,... | collective-permute-start | bytes 344072 | tf_op jit(solution)/shard_map/ppermute | solution.py:23
  65.1 4.5 %collective-permute-start.18 = (bf16[2,32,896]{2,1,0:T(8,128)(2,1)S(1)}, bf16[2,32,896]{2,1,0:T(8,128)(2,1)S(1)}, u32[]{:S(2)}, u32[]{:S(2)}) collective-permute-start(bf16[2,32,896]{2,1,0:T(8,128)(2,1)S(1)} %collective-permute-done.11.refs_2_), channel_id=1, source_target_pairs={{16,0},{0,16},{17,1},{1,17},{18,2},{2,18},{19,3},{3,19},{20,4},{4,... | collective-permute-start | bytes 344072 | tf_op jit(solution)/shard_map/ppermute | solution.py:23
  66.3 0.6 copy-start
  67.0 4.8 %collective-permute-start.15 = (bf16[2,32,896]{2,1,0:T(8,128)(2,1)S(1)}, bf16[2,32,896]{2,1,0:T(8,128)(2,1)}, u32[]{:S(2)}, u32[]{:S(2)}) collective-permute-start(bf16[2,32,896]{2,1,0:T(8,128)(2,1)S(1)} %collective-permute-done.13.refs_3_), channel_id=1, source_target_pairs={{1,0},{2,1},{3,2},{4,3},{5,4},{6,5},{7,6},{0,7},{9,8},{10,9},{11,1... | collective-permute-start | bytes 344072 | tf_op jit(solution)/shard_map/ppermute | solution.py:23
  67.8 0.6 copy-start.2
  68.4 4.3 %collective-permute-start.22 = (bf16[2,32,896]{2,1,0:T(8,128)(2,1)S(1)}, bf16[2,32,896]{2,1,0:T(8,128)(2,1)}, u32[]{:S(2)}, u32[]{:S(2)}) collective-permute-start(bf16[2,32,896]{2,1,0:T(8,128)(2,1)S(1)} %collective-permute-done.12.refs_6_), channel_id=1, source_target_pairs={{16,0},{0,16},{17,1},{1,17},{18,2},{2,18},{19,3},{3,19},{20,4},{4,... | collective-permute-start | bytes 344072 | tf_op jit(solution)/shard_map/ppermute | solution.py:23
  68.7 0.6 copy-start.4
  69.3 3.4 %collective-permute-start.19 = (bf16[2,32,896]{2,1,0:T(8,128)(2,1)S(1)}, bf16[2,32,896]{2,1,0:T(8,128)(2,1)}, u32[]{:S(2)}, u32[]{:S(2)}) collective-permute-start(bf16[2,32,896]{2,1,0:T(8,128)(2,1)S(1)} %collective-permute-done.13.refs_3_), channel_id=1, source_target_pairs={{16,0},{0,16},{17,1},{1,17},{18,2},{2,18},{19,3},{3,19},{20,4},{4,... | collective-permute-start | bytes 344072 | tf_op jit(solution)/shard_map/ppermute | solution.py:23
  69.6 0.7 copy-start.6
  70.2 2.5 %collective-permute-start.21 = (bf16[2,32,896]{2,1,0:T(8,128)(2,1)S(1)}, bf16[2,32,896]{2,1,0:T(8,128)(2,1)}, u32[]{:S(2)}, u32[]{:S(2)}) collective-permute-start(bf16[2,32,896]{2,1,0:T(8,128)(2,1)S(1)} %collective-permute-done.14.refs_5_), channel_id=1, source_target_pairs={{16,0},{0,16},{17,1},{1,17},{18,2},{2,18},{19,3},{3,19},{20,4},{4,... | collective-permute-start | bytes 344072 | tf_op jit(solution)/shard_map/ppermute | solution.py:23
  71.8 2.2 %collective-permute-start.20 = (bf16[2,32,896]{2,1,0:T(8,128)(2,1)}, bf16[2,32,896]{2,1,0:T(8,128)(2,1)}, u32[]{:S(2)}, u32[]{:S(2)}) collective-permute-start(bf16[2,32,896]{2,1,0:T(8,128)(2,1)} %collective-permute-done.15.refs_4_), channel_id=1, source_target_pairs={{16,0},{0,16},{17,1},{1,17},{18,2},{2,18},{19,3},{3,19},{20,4},{4,... | collective-permute-start | bytes 344072 | tf_op jit(solution)/shard_map/ppermute | solution.py:23
  72.7 6.6 %copy-start.8 = (s32[2]{0:T(128)}, s32[2]{0:T(128)S(1)}, u32[]{:S(2)}) copy-start(s32[2]{0:T(128)S(1)} %pad_add_fusion.place) | copy-start | bytes 28
  74.0 0.9 copy-start.1
  74.8 0.9 copy-start.3
  75.7 0.9 copy-start.5
  76.6 0.9 copy-start.7
  79.4 1.2 copy-start.10
  80.6 1.3 copy-start.12
  81.8 0.7 copy-start.9
  82.5 1.5 %copy-start.11 = (bf16[1024,896]{1,0:T(8,128)(2,1)S(1)}, bf16[1024,896]{1,0:T(8,128)(2,1)}, u32[]{:S(2)}) copy-start(bf16[1024,896]{1,0:T(8,128)(2,1)} %copy-done.10) | copy-start | bytes 5505028
  84.0 1.5 %copy-start.13 = (bf16[896,1024]{1,0:T(8,128)(2,1)S(1)}, bf16[896,1024]{1,0:T(8,128)(2,1)}, u32[]{:S(2)}) copy-start(bf16[896,1024]{1,0:T(8,128)(2,1)} %copy-done.12) | copy-start | bytes 5505028
  122.5 23.9 %copy-start.14 = (bf16[56,4,56]{2,1,0:T(4,128)(2,1)S(1)}, bf16[56,4,56]{2,1,0:T(4,128)(2,1)}, u32[]{:S(2)}) copy-start(bf16[56,4,56]{2,1,0:T(4,128)(2,1)} %param.5) | copy-start | bytes 75268
  122.9 24.5 %copy-start.16 = (f32[4]{0:T(128)S(1)}, f32[4]{0:T(128)}, u32[]{:S(2)}) copy-start(f32[4]{0:T(128)} %param.9) | copy-start | bytes 52
  123.9 17.9 %all-to-all-start.3 = ((bf16[16,56,224]{2,1,0:T(8,128)(2,1)}), bf16[16,56,224]{2,1,0:T(8,128)(2,1)S(1)}, u32[]{:S(2)}, u32[]{:S(2)}) async-start(bf16[16,56,224]{2,1,0:T(8,128)(2,1)} %bitcast.17), calls=%async_computation.3 | async-start | bytes 917504 | tf_op jit(solution)/shard_map/all_to_all | solution.py:181
  142.4 4.8 %collective-permute-start.26 = (f32[56,112]{1,0:T(8,128)S(1)}, f32[56,112]{1,0:T(8,128)S(1)}, u32[]{:S(2)}, u32[]{:S(2)}) collective-permute-start(f32[56,112]{1,0:T(8,128)S(1)} %select_n.99), channel_id=1, source_target_pairs={{16,0},{0,16},{17,1},{1,17},{18,2},{2,18},{19,3},{3,19},{20,4},{4,... | collective-permute-start | bytes 75272 | tf_op jit(solution)/shard_map/ppermute | solution.py:23

commit v3 on v2

v3 whole, which is shorter than its diff:
```python
import jax
import jax.numpy as jnp
from jax import lax
from jax.sharding import Mesh
from jax.sharding import PartitionSpec as P
from jax.experimental import pallas as pl
from jax.experimental.pallas import tpu as pltpu

BLK = ("x", "y_hi", "core")
GRP = ("y_lo", "z")
BF16 = jnp.bfloat16
F32 = jnp.float32


def from_ahead(x, axis, offset):
    n = lax.axis_size(axis)
    return lax.ppermute(x, axis, [((i + offset) % n, i) for i in range(n)])


def to_ahead(x, axis, offset):
    n = lax.axis_size(axis)
    return lax.ppermute(x, axis, [(i, (i + offset) % n) for i in range(n)])


def total(parts):
    return sum(p.astype(F32) for p in parts).astype(BF16)


def steps_along(x, axis, order=None):
    n = lax.axis_size(axis)
    arrived = {o: from_ahead(x, axis, o) for o in (order or range(1, n))}
    return jnp.concatenate([x] + [arrived[o] for o in range(1, n)], axis=0)


def kernel_call(body, outs, args, flops=0, scratch=(), far=()):
    smem = pl.BlockSpec(memory_space=pltpu.SMEM)
    vmem = pl.BlockSpec(memory_space=pltpu.VMEM)
    moved = sum(a.size * a.dtype.itemsize for a in (*args, *outs))
    return pl.pallas_call(
        body,
        out_shape=outs,
        in_specs=[smem]
        + [pl.BlockSpec(memory_space=pl.ANY) if i in far else vmem for i in range(1, len(args))],
        out_specs=[vmem] * len(outs),
        scratch_shapes=list(scratch),
        cost_estimate=pl.CostEstimate(flops=flops, bytes_accessed=moved, transcendentals=0),
        compiler_params=pltpu.CompilerParams(vmem_limit_bytes=40 * 2**20),
    )(*args)


def turned_copies(core, own, other, count):
    n_c, n_k, n_d = own.shape
    half = n_k // 2

    def body(core, own, other, out):
        mine = own[...].astype(F32)
        theirs = other[...].astype(F32)
        is_low = core[0] == 0
        blocks = []
        for k in range(half):
            a = jnp.where(is_low, mine[:, k], mine[:, half + k])
            b = jnp.where(is_low, theirs[:, k], theirs[:, half + k])
            blocks += [jnp.where(is_low, a, b), jnp.where(is_low, b, a)]
        whole = jnp.concatenate(blocks, axis=0).T.astype(BF16)
        for i in range(count):
            out[i] = whole

    shape = jax.ShapeDtypeStruct((count, n_d, half * 2 * n_c), BF16)
    return kernel_call(body, [shape], [core, own, other])[0]


def right_of(core, turned, columns, half):
    n_grp, n_d, width = turned.shape
    n_q = columns.shape[0]
    rows = width // half

    def body(core, turned, columns, *outs):
        left = turned[...].reshape(n_grp * n_d, width).T
        right = lax.dot_general(
            left, columns[...], (((1,), (1,)), ((), ())), preferred_element_type=F32
        ).astype(BF16)
        for k in range(half):
            outs[k][...] = right[k * rows : (k + 1) * rows]

    outs = [jax.ShapeDtypeStruct((rows, n_q), BF16)] * half
    return kernel_call(body, outs, [core, turned, columns], 2 * n_q * n_grp * n_d * width)


def placed_by_block(place, pieces, n_x, n_h):
    count = len(pieces)

    def body(place, *refs):
        out = refs[-1]
        for i in range(count):
            core, ox = i // n_x, i % n_x
            for oh in range(n_h):
                b = (
                    ((place[0] + ox) % n_x) * (2 * n_h)
                    + ((place[1] + oh) % n_h) * 2
                    + (place[2] + core) % 2
                )
                out[b] = refs[i][oh]

    shape = (count * n_h, *pieces[0].shape[1:])
    return kernel_call(body, [jax.ShapeDtypeStruct(shape, BF16)], [place, *pieces])[0]


def weighed(place, pieces, right, z_own, z_other, half, n_z, n_l, n_x, n_h):
    pts, nv = pieces[0].shape[1:]
    step = n_l * pts
    total = step * len(pieces)
    n_q = right[0].shape[2]
    lanes = z_own.shape[1]
    per_row = n_q // lanes
    n_plane = n_x * n_h
    share = nv // n_plane
    count = len(pieces)

    def body(place, *refs):
        parts, rights = refs[:count], refs[count : count + n_x + n_h]
        far_own, far_other = refs[count + n_x + n_h : count + n_x + n_h + 2]
        outs = refs[count + n_x + n_h + 2 : -7]
        rows, turned, weighted, right, z_own, z_other, done = refs[-7:]
        copies = [
            pltpu.make_async_copy(far_own, z_own, done.at[0]),
            pltpu.make_async_copy(far_other, z_other, done.at[1]),
        ]
        for copy in copies:
            copy.start()
        slots = []
        for j in range(n_plane):
            ox = (j // n_h + n_x - place[2]) % n_x
            oh = (j % n_h + n_h - place[3]) % n_h
            slots.append(ox * n_h + oh)
        for i in range(0, count, 2):
            block = jnp.concatenate(
                [parts[i + j][...].reshape(step, nv) for j in range(2)], axis=0
            )
            rows[i * step : (i + 2) * step, :] = block
            flipped = block.T
            for j in range(n_plane):
                turned[slots[j], :, i * step : (i + 2) * step] = flipped[
                    j * share : (j + 1) * share
                ]
        for k in range(half):
            for ox in range(n_x):
                for oh in range(n_h):
                    at = ((place[2] + ox) % n_x) * n_h + (place[3] + oh) % n_h
                    right[at] = rights[ox][oh] if k == 0 else rights[n_x + oh][ox]
            for core, z in enumerate((z_own, z_other)):
                base = core * n_z * step
                products = jnp.dot(
                    rows[base : base + n_z * step, :],
                    right[...].reshape(nv, n_q),
                    preferred_element_type=F32,
                )
                if k == 0:
                    copies[core].wait()
                for s in range(n_z * n_l):
                    oz, ol = s // n_l, s % n_l
                    g = ((place[1] + ol) % n_l) * n_z + (place[0] + oz) % n_z
                    first = g * (pts * per_row)
                    for j in range(per_row):
                        zs = z[pl.ds(first + j, pts, stride=per_row), :]
                        weighted[
                            base + s * pts : base + (s + 1) * pts, j * lanes : (j + 1) * lanes
                        ] = (
                            zs * products[s * pts : (s + 1) * pts, j * lanes : (j + 1) * lanes]
                        ).astype(BF16)
            back = jnp.dot(
                turned[...].reshape(nv, total), weighted[...], preferred_element_type=F32
            ).astype(BF16)
            for ox in range(n_x):
                for oh in range(n_h):
                    at = (ox * n_h + oh) * share
                    block = back[at : at + share]
                    if k == 0:
                        outs[ox][oh] = block
                    else:
                        outs[n_x + oh][ox] = block

    outs = [jax.ShapeDtypeStruct((n_h, share, n_q), BF16)] * n_x
    outs += [jax.ShapeDtypeStruct((n_x, share, n_q), BF16)] * n_h
    flops = 4 * total * nv * half * n_q
    scratch = [
        pltpu.VMEM((total, nv), BF16),
        pltpu.VMEM((n_plane, share, total), BF16),
        pltpu.VMEM((total, n_q), BF16),
        pltpu.VMEM((n_plane, share, n_q), BF16),
        pltpu.VMEM(z_own.shape, F32),
        pltpu.VMEM(z_own.shape, F32),
        pltpu.SemaphoreType.DMA((2,)),
    ]
    args = [place, *pieces, *right, z_own, z_other]
    return kernel_call(body, outs, args, flops, scratch, (len(args) - 2, len(args) - 1))


def contract_last(a, b):
    return lax.dot_general(a, b, (((0,), (1,)), ((), ())), preferred_element_type=F32)


def in_core_order(own, other, axis):
    first = lax.axis_index("core") == 0
    return jnp.stack([jnp.where(first, own, other), jnp.where(first, other, own)], axis=axis)


def local(amplitudes, grid_factor, metric, virt_energy, pair_energy):
    n_c, n_k, n_d = amplitudes.shape
    _, nv = grid_factor.shape
    n_x, n_h = lax.axis_size("x"), lax.axis_size("y_hi")
    n_z, n_l = lax.axis_size("z"), lax.axis_size("y_lo")
    n_grp = n_z * n_l
    half = n_k // 2
    my_x, my_h, my_core = lax.axis_index("x"), lax.axis_index("y_hi"), lax.axis_index("core")
    my_z, my_l = lax.axis_index("z"), lax.axis_index("y_lo")
    half = n_k // 2
    first = my_core == 0

    other = from_ahead(amplitudes, "core", 1)
    turned = turned_copies(my_core[None], amplitudes, other, n_z * n_l)
    turned = lax.all_to_all(turned, GRP, 0, 0, tiled=True)

    mine = steps_along(grid_factor[None], "y_hi")
    own = [mine] + [from_ahead(mine, "x", o) for o in range(1, n_x)]
    own += [from_ahead(piece, "core", 1) for piece in own]
    columns = placed_by_block(jnp.stack([my_x, my_h, my_core]), own, n_x, n_h).reshape(-1, nv)

    right = right_of(my_core[None], turned, columns, half)
    low = from_ahead(right[0], "y_hi", 1)
    high = [right[1]] + [from_ahead(right[1], "x", o) for o in (1, 3, 2)]
    low = jnp.stack([right[0], low])
    high = jnp.stack([high[o] for o in (0, 1, 3, 2)])
    low = {0: low, **{o: from_ahead(low, "x", o) for o in (1, 3, 2)}}
    right = [low[o] for o in range(n_x)] + [high, from_ahead(high, "y_hi", 1)]

    pair = steps_along(grid_factor[None], "y_lo")
    own = {0: pair}
    up = down = pair
    for o in range(1, n_z // 2 + 1):
        up = from_ahead(up, "z", 1)
        if o < n_z - o:
            down = from_ahead(down, "z", -1)
            up, down = lax.optimization_barrier((up, down))
            own[n_z - o] = down
        own[o] = up
    own = [own[o] for o in range(n_z)]
    own += [from_ahead(piece, "core", 1) for piece in own]
    z = metric.reshape(-1, 128)
    z_other = from_ahead(z, "core", 1)
    place = jnp.stack([my_z, my_l, my_x, my_h])
    sums = weighed(place, own, right, z, z_other, half, n_z, n_l, n_x, n_h)
    low, high = sums[:n_x], sums[n_x:]
    high_arrived = to_ahead(high[1], "y_hi", 1)
    low_arrived = [to_ahead(low[o], "x", o) for o in (1, 3, 2)]
    low = [total([low[0][h]] + [p[h] for p in low_arrived]) for h in range(n_h)]
    high = [total([high[0][o], high_arrived[o]]) for o in range(n_x)]
    low_arrived = to_ahead(low[1], "y_hi", 1)
    high_arrived = [to_ahead(high[o], "x", o) for o in (1, 3, 2)]
    back = jnp.concatenate([total([low[0], low_arrived]), total([high[0]] + high_arrived)], axis=0)
    ladder = contract_last(columns, back).astype(BF16).reshape(n_grp, n_d, half * 2 * n_c)
    ladder = lax.all_to_all(ladder, GRP, 0, 0, tiled=True)
    ladder = ladder.astype(F32).sum(axis=0).reshape(n_d, half, 2, n_c)
    keep = jnp.where(first, ladder[:, :, 0], ladder[:, :, 1])
    give = jnp.where(first, ladder[:, :, 1], ladder[:, :, 0])
    other = from_ahead(give.reshape(n_d, half * n_c), "core", 1).reshape(n_d, half, n_c)
    ladder = in_core_order(keep, other, 1).reshape(n_d, n_k, n_c).transpose(2, 1, 0)
    first_energy = lax.dynamic_slice_in_dim(virt_energy, lax.axis_index(BLK) * n_c, n_c)
    second_energy = lax.dynamic_slice_in_dim(virt_energy, lax.axis_index(GRP) * n_d, n_d)
    denominator = (
        first_energy[:, None, None] + second_energy[None, None, :] - pair_energy[None, :, None]
    )
    return denominator * amplitudes.astype(F32) + ladder


def solution(mesh):
    split = Mesh(mesh.devices.reshape(4, 2, 2, 2, 8), ("x", "y_hi", "core", "y_lo", "z"))
    in_specs = (P(BLK, None, GRP), P(BLK + GRP, None), P(BLK, GRP, None), P(), P())
    return jax.shard_map(
        local, mesh=split, in_specs=in_specs, out_specs=P(BLK, None, GRP), check_vma=False
    )
```

time: 149 us -> 146 us (0.980)
  blocking collectives: 30.7 us -> 0 us
  waiting for transfers between devices: 26.4 us -> 44.2 us
  starting transfers between devices: 58.9 us -> 75.7 us
  local copies, waits for them, and re-layouts: 21.6 us -> 14.6 us
    all_to_all x1 -> x0, blocking collectives: 30.7 us -> none  [local(): back = lax.all_to_all(back, PLANE, 0, 0, tiled=True)]
    ppermute x0 -> x8, waiting for transfers between devices: none -> 14.4 us  [to_ahead(): return lax.ppermute(x, axis, [(i, (i + offset) % n) for i in range(n)])]
    ppermute x27 -> x35, starting transfers between devices: 40.7 us -> 51.4 us  [from_ahead(): return lax.ppermute(x, axis, [((i + offset) % n, i) for i in range(n)])]
    ppermute x0 -> x8, starting transfers between devices: none -> 9.23 us  [to_ahead(): return lax.ppermute(x, axis, [(i, (i + offset) % n) for i in range(n)])]
    ppermute x27 -> x35, waiting for transfers between devices: 16.3 us -> 20.7 us  [from_ahead(): return lax.ppermute(x, axis, [((i + offset) % n, i) for i in range(n)])]
    unnamed x38 -> x45, local copies, waits for them, and re-layouts: 15.7 us -> 11.7 us
    all_to_all x2 -> x1, starting transfers between devices: 11.2 us -> 7.73 us  [local(): turned = lax.all_to_all(turned, GRP, 0, 0, tiled=True)]
    broadcast_in_dim x3 -> x0, local copies, waits for them, and re-layouts: 2.4 us -> none  [from_everyone(): jnp.broadcast_to(x[None], (count, *x.shape))]
  transfers between devices with their start and end apart: 30 -> 45, of which waited for: 11 -> 18; matrix products, arithmetic and copies ran while one was open for 2% -> 1% of each run, Pallas kernels for 2% -> 1%
where the time goes in v3:
time: 146 us; the launch traced here: 145 us
  starting transfers between devices  75.7 us (52%)
  waiting for transfers between devices  44.2 us (30%)
  local copies, waits for them, and re-layouts  14.6 us (10%)
  Pallas kernels  8.84 us (6%)
    ppermute x35, starting transfers between devices, from_ahead(): return lax.ppermute(x, axis, [((i + offset) % n, i) for i in range(n)])  51.4 us
    ppermute x35, waiting for transfers between devices, from_ahead(): return lax.ppermute(x, axis, [((i + offset) % n, i) for i in range(n)])  20.7 us
    ppermute x8, waiting for transfers between devices, to_ahead(): return lax.ppermute(x, axis, [(i, (i + offset) % n) for i in range(n)])  14.4 us
    unnamed x45, local copies, waits for them, and re-layouts  11.7 us
    ppermute x8, starting transfers between devices, to_ahead(): return lax.ppermute(x, axis, [(i, (i + offset) % n) for i in range(n)])  9.23 us
    all_to_all x1, waiting for transfers between devices, local(): ladder = lax.all_to_all(ladder, GRP, 0, 0, tiled=True)  9.2 us
    pallas_call x4, Pallas kernels, kernel_call(): pl.pallas_call(body, out_shape=outs, in_specs=[smem] + [pl.BlockSpec(memo...  8.84 us
    all_to_all x1, starting transfers between devices, local(): turned = lax.all_to_all(turned, GRP, 0, 0, tiled=True)  7.73 us
  transfers between devices with their start and end apart: 45, of which 18 were waited for; matrix products, arithmetic and copies ran while one was open for 1% of the time, Pallas kernels for 1%

profile of v3, /device:TPU:1, one launch (start us, length us, event | category | flops | bytes accessed | tf_op | source)
XLA Modules:
  0.0 145.3 jit_solution(14333304848521953629)
XLA Ops:
  0.0 3.2 %collective-permute-start.24 = (bf16[56,4,56]{2,1,0:T(4,128)(2,1)}, bf16[56,4,56]{2,1,0:T(4,128)(2,1)S(1)}, u32[]{:S(2)}, u32[]{:S(2)}) collective-permute-start(bf16[56,4,56]{2,1,0:T(4,128)(2,1)} %own.1), channel_id=1, source_target_pairs={{16,0},{0,16},{17,1},{1,17},{18,2},{2,18},{19,3},{3,19},{20,4},{4,... | collective-permute-start | bytes 75272 | tf_op jit(solution)/shard_map/ppermute | solution.py:17
  3.2 1.1 collective-permute-done.24.other
  5.1 1.0 shard_map.56
  6.1 7.7 %all-to-all-start = ((bf16[16,56,224]{2,1,0:T(8,128)(2,1)}), bf16[16,56,224]{2,1,0:T(8,128)(2,1)S(1)}, u32[]{:S(2)}, u32[]{:S(2)}) async-start(bf16[16,56,224]{2,1,0:T(8,128)(2,1)} %shard_map.56), calls=%async_computation | async-start | bytes 917504 | tf_op jit(solution)/shard_map/all_to_all | solution.py:221
  13.8 2.7 %collective-permute-start = (bf16[1,32,896]{2,1,0:T(8,128)(2,1)S(1)}, bf16[1,32,896]{2,1,0:T(8,128)(2,1)S(1)}, u32[]{:S(2)}, u32[]{:S(2)}) collective-permute-start(bf16[1,32,896]{2,1,0:T(8,128)(2,1)S(1)} %bitcast.57), channel_id=1, source_target_pairs={{32,0},{0,32},{33,1},{1,33},{34,2},{2,34},{35,3},{3,35},{36,4},{4,... | collective-permute-start | bytes 172040 | tf_op jit(solution)/shard_map/ppermute | solution.py:17
  17.3 1.3 collective-permute-done
  18.6 1.9 %collective-permute-done.8 = bf16[1,32,896]{2,1,0:T(8,128)(2,1)S(1)} collective-permute-done((bf16[1,32,896]{2,1,0:T(8,128)(2,1)S(1)}, bf16[1,32,896]{2,1,0:T(8,128)(2,1)S(1)}, u32[]{:S(2)}, u32[]{:S(2)}) %collective-permute-start.8) | collective-permute-done | bytes 57376 | tf_op jit(solution)/shard_map/ppermute | solution.py:17
  20.5 2.2 %collective-permute-start.10 = (bf16[2,32,896]{2,1,0:T(8,128)(2,1)S(1)}, bf16[2,32,896]{2,1,0:T(8,128)(2,1)S(1)}, u32[]{:S(2)}, u32[]{:S(2)}) collective-permute-start(bf16[2,32,896]{2,1,0:T(8,128)(2,1)S(1)} %get-tuple-element.40.refs_0_), channel_id=1, source_target_pairs={{7,0},{0,1},{1,2},{2,3},{3,4},{4,5},{5,6},{6,7},{15,8},{8,9},{9,10... | collective-permute-start | bytes 344072 | tf_op jit(solution)/shard_map/ppermute | solution.py:17
  22.7 1.1 collective-permute-start.9
  23.8 2.5 %collective-permute-start.1 = (bf16[2,32,896]{2,1,0:T(8,128)(2,1)S(1)}, bf16[2,32,896]{2,1,0:T(8,128)(2,1)S(1)}, u32[]{:S(2)}, u32[]{:S(2)}) collective-permute-start(bf16[2,32,896]{2,1,0:T(8,128)(2,1)S(1)} %get-tuple-element.41.refs_0_), channel_id=1, source_target_pairs={{64,0},{128,64},{192,128},{0,192},{65,1},{129,65},{193,129},{1,193... | collective-permute-start | bytes 344072 | tf_op jit(solution)/shard_map/ppermute | solution.py:17
  27.5 1.7 %collective-permute-done.10.refs_7_ = bf16[2,32,896]{2,1,0:T(8,128)(2,1)S(1)} collective-permute-done((bf16[2,32,896]{2,1,0:T(8,128)(2,1)S(1)}, bf16[2,32,896]{2,1,0:T(8,128)(2,1)S(1)}, u32[]{:S(2)}, u32[]{:S(2)}) %collective-permute-start.10) | collective-permute-done | bytes 114720 | tf_op jit(solution)/shard_map/ppermute | solution.py:17
  29.2 1.5 %collective-permute-start.11 = (bf16[2,32,896]{2,1,0:T(8,128)(2,1)}, bf16[2,32,896]{2,1,0:T(8,128)(2,1)}, u32[]{:S(2)}, u32[]{:S(2)}) collective-permute-start(bf16[2,32,896]{2,1,0:T(8,128)(2,1)} %collective-permute-done.9.refs_1_), channel_id=1, source_target_pairs={{1,0},{2,1},{3,2},{4,3},{5,4},{6,5},{7,6},{0,7},{9,8},{10,9},{11,1... | collective-permute-start | bytes 344072 | tf_op jit(solution)/shard_map/ppermute | solution.py:17
  30.7 3.1 %collective-permute-start.33 = (f32[2048,128]{1,0:T(8,128)S(1)}, f32[2048,128]{1,0:T(8,128)}, u32[]{:S(2)}, u32[]{:S(2)}) collective-permute-start(f32[2048,128]{1,0:T(8,128)S(1)} %bitcast.47), channel_id=1, source_target_pairs={{16,0},{0,16},{17,1},{1,17},{18,2},{2,18},{19,3},{3,19},{20,4},{4,... | collective-permute-start | bytes 3145736 | tf_op jit(solution)/shard_map/ppermute | solution.py:17
  33.7 2.6 %collective-permute-start.4 = (bf16[2,32,896]{2,1,0:T(8,128)(2,1)S(1)}, bf16[2,32,896]{2,1,0:T(8,128)(2,1)S(1)}, u32[]{:S(2)}, u32[]{:S(2)}) collective-permute-start(bf16[2,32,896]{2,1,0:T(8,128)(2,1)S(1)} %get-tuple-element.41.refs_0_), channel_id=1, source_target_pairs={{16,0},{0,16},{17,1},{1,17},{18,2},{2,18},{19,3},{3,19},{20,4},{4,... | collective-permute-start | bytes 344072 | tf_op jit(solution)/shard_map/ppermute | solution.py:17
  36.3 1.1 collective-permute-start.5
  37.5 1.9 %collective-permute-start.7 = (bf16[2,32,896]{2,1,0:T(8,128)(2,1)S(1)}, bf16[2,32,896]{2,1,0:T(8,128)(2,1)S(1)}, u32[]{:S(2)}, u32[]{:S(2)}) collective-permute-start(bf16[2,32,896]{2,1,0:T(8,128)(2,1)S(1)} %collective-permute-done.3.refs_3_), channel_id=1, source_target_pairs={{16,0},{0,16},{17,1},{1,17},{18,2},{2,18},{19,3},{3,19},{20,4},{4,... | collective-permute-start | bytes 344072 | tf_op jit(solution)/shard_map/ppermute | solution.py:17
  40.4 1.0 collective-permute-start.14
  43.7 2.5 %collective-permute-start.29 = (bf16[112,512]{1,0:T(8,128)(2,1)S(1)}, bf16[112,512]{1,0:T(8,128)(2,1)S(1)}, u32[]{:S(2)}, u32[]{:S(2)}) collective-permute-start(bf16[112,512]{1,0:T(8,128)(2,1)S(1)} %get-tuple-element.26), channel_id=1, source_target_pairs={{64,0},{128,64},{192,128},{0,192},{65,1},{129,65},{193,129},{1,193... | collective-permute-start | bytes 344072 | tf_op jit(solution)/shard_map/ppermute | solution.py:17
  46.1 1.4 collective-permute-start.30
  47.9 1.5 %collective-permute-start.18 = (bf16[2,32,896]{2,1,0:T(8,128)(2,1)}, bf16[2,32,896]{2,1,0:T(8,128)(2,1)S(1)}, u32[]{:S(2)}, u32[]{:S(2)}) collective-permute-start(bf16[2,32,896]{2,1,0:T(8,128)(2,1)} %collective-permute-done.11.refs_2_), channel_id=1, source_target_pairs={{16,0},{0,16},{17,1},{1,17},{18,2},{2,18},{19,3},{3,19},{20,4},{4,... | collective-permute-start | bytes 344072 | tf_op jit(solution)/shard_map/ppermute | solution.py:17
  49.7 2.3 %collective-permute-start.22 = (bf16[2,32,896]{2,1,0:T(8,128)(2,1)}, bf16[2,32,896]{2,1,0:T(8,128)(2,1)S(1)}, u32[]{:S(2)}, u32[]{:S(2)}) collective-permute-start(bf16[2,32,896]{2,1,0:T(8,128)(2,1)} %collective-permute-done.12.refs_6_), channel_id=1, source_target_pairs={{16,0},{0,16},{17,1},{1,17},{18,2},{2,18},{19,3},{3,19},{20,4},{4,... | collective-permute-start | bytes 344072 | tf_op jit(solution)/shard_map/ppermute | solution.py:17
  52.1 1.9 %collective-permute-start.15 = (bf16[2,32,896]{2,1,0:T(8,128)(2,1)}, bf16[2,32,896]{2,1,0:T(8,128)(2,1)S(1)}, u32[]{:S(2)}, u32[]{:S(2)}) collective-permute-start(bf16[2,32,896]{2,1,0:T(8,128)(2,1)} %collective-permute-done.13.refs_3_), channel_id=1, source_target_pairs={{1,0},{2,1},{3,2},{4,3},{5,4},{6,5},{7,6},{0,7},{9,8},{10,9},{11,1... | collective-permute-start | bytes 344072 | tf_op jit(solution)/shard_map/ppermute | solution.py:17
  54.7 1.4 collective-permute-start.25
  56.8 1.6 %collective-permute-start.32 = (bf16[4,112,512]{2,1,0:T(8,128)(2,1)S(1)}, bf16[4,112,512]{2,1,0:T(8,128)(2,1)S(1)}, u32[]{:S(2)}, u32[]{:S(2)}) collective-permute-start(bf16[4,112,512]{2,1,0:T(8,128)(2,1)S(1)} %pad_maximum_fusion.refs_20_), channel_id=1, source_target_pairs={{32,0},{0,32},{33,1},{1,33},{34,2},{2,34},{35,3},{3,35},{36,4},{4,... | collective-permute-start | bytes 1376264 | tf_op jit(solution)/shard_map/ppermute | solution.py:17
  58.4 1.9 %collective-permute-start.19 = (bf16[2,32,896]{2,1,0:T(8,128)(2,1)}, bf16[2,32,896]{2,1,0:T(8,128)(2,1)S(1)}, u32[]{:S(2)}, u32[]{:S(2)}) collective-permute-start(bf16[2,32,896]{2,1,0:T(8,128)(2,1)} %collective-permute-done.13.refs_3_), channel_id=1, source_target_pairs={{16,0},{0,16},{17,1},{1,17},{18,2},{2,18},{19,3},{3,19},{20,4},{4,... | collective-permute-start | bytes 344072 | tf_op jit(solution)/shard_map/ppermute | solution.py:17
  60.5 2.9 %collective-permute-start.20 = (bf16[2,32,896]{2,1,0:T(8,128)(2,1)S(1)}, bf16[2,32,896]{2,1,0:T(8,128)(2,1)S(1)}, u32[]{:S(2)}, u32[]{:S(2)}) collective-permute-start(bf16[2,32,896]{2,1,0:T(8,128)(2,1)S(1)} %collective-permute-done.15.refs_4_), channel_id=1, source_target_pairs={{16,0},{0,16},{17,1},{1,17},{18,2},{2,18},{19,3},{3,19},{20,4},{4,... | collective-permute-start | bytes 344072 | tf_op jit(solution)/shard_map/ppermute | solution.py:17
  64.1 1.3 collective-permute-start.26
  67.4 4.0 %collective-permute-done.26.refs_17_ = bf16[2,112,512]{2,1,0:T(8,128)(2,1)S(1)} collective-permute-done((bf16[2,112,512]{2,1,0:T(8,128)(2,1)S(1)}, bf16[2,112,512]{2,1,0:T(8,128)(2,1)S(1)}, u32[]{:S(2)}, u32[]{:S(2)}) %collective-permute-start.26) | collective-permute-done | bytes 229408 | tf_op jit(solution)/shard_map/ppermute | solution.py:17
  71.3 3.2 %collective-permute-done.27.refs_18_ = bf16[2,112,512]{2,1,0:T(8,128)(2,1)} collective-permute-done((bf16[2,112,512]{2,1,0:T(8,128)(2,1)S(1)}, bf16[2,112,512]{2,1,0:T(8,128)(2,1)}, u32[]{:S(2)}, u32[]{:S(2)}) %collective-permute-start.27) | collective-permute-done | bytes 229408 | tf_op jit(solution)/shard_map/ppermute | solution.py:17
  74.6 5.5 %collective-permute-done.28.refs_19_ = bf16[2,112,512]{2,1,0:T(8,128)(2,1)} collective-permute-done((bf16[2,112,512]{2,1,0:T(8,128)(2,1)S(1)}, bf16[2,112,512]{2,1,0:T(8,128)(2,1)}, u32[]{:S(2)}, u32[]{:S(2)}) %collective-permute-start.28) | collective-permute-done | bytes 229408 | tf_op jit(solution)/shard_map/ppermute | solution.py:17
  80.1 0.9 copy-done.5
  81.0 0.9 copy-done.7
  81.9 0.9 copy-done.9
  83.7 0.9 copy-done.13
  84.6 0.9 copy-done.15
  87.3 6.8 %shard_map.58 = (bf16[2,112,512]{2,1,0:T(8,128)(2,1)S(1)}, bf16[2,112,512]{2,1,0:T(8,128)(2,1)S(1)}, bf16[2,112,512]{2,1,0:T(8,128)(2,1)S(1)}, bf16[2,112,512]{2...) custom-call(s32[4]{0:T(128)S(1)} %pad_add_fusion.place, ...), custom_call_target="tpu_custom_call" | custom-call | flops 3758096384 | bytes 7602192 | tf_op jit(solution)/shard_map/pallas_call | solution.py:39
  94.1 2.7 %collective-permute-start.35 = (bf16[2,112,512]{2,1,0:T(8,128)(2,1)S(1)}, bf16[2,112,512]{2,1,0:T(8,128)(2,1)S(1)}, u32[]{:S(2)}, u32[]{:S(2)}) collective-permute-start(bf16[2,112,512]{2,1,0:T(8,128)(2,1)S(1)} %get-tuple-element.29), channel_id=1, source_target_pairs={{0,192},{64,0},{128,64},{192,128},{1,193},{65,1},{129,65},{193,129... | collective-permute-start | bytes 688136 | tf_op jit(solution)/shard_map/ppermute | solution.py:22
  96.8 1.1 collective-permute-start.38
  97.9 9.0 %collective-permute-done.34 = bf16[2,112,512]{2,1,0:T(8,128)(2,1)S(1)} collective-permute-done((bf16[2,112,512]{2,1,0:T(8,128)(2,1)S(1)}, bf16[2,112,512]{2,1,0:T(8,128)(2,1)S(1)}, u32[]{:S(2)}, u32[]{:S(2)}) %collective-permute-start.34) | collective-permute-done | bytes 229408 | tf_op jit(solution)/shard_map/ppermute | solution.py:22
  107.0 1.2 collective-permute-start.37
  108.2 1.2 collective-permute-done.38
  110.1 2.1 %collective-permute-start.40 = (bf16[112,512]{1,0:T(8,128)(2,1)S(1)}, bf16[112,512]{1,0:T(8,128)(2,1)S(1)}, u32[]{:S(2)}, u32[]{:S(2)}) collective-permute-start(bf16[112,512]{1,0:T(8,128)(2,1)S(1)} %get-tuple-element.35), channel_id=1, source_target_pairs={{0,192},{64,0},{128,64},{192,128},{1,193},{65,1},{129,65},{193,129... | collective-permute-start | bytes 344072 | tf_op jit(solution)/shard_map/ppermute | solution.py:22
  112.2 1.5 %collective-permute-start.41 = (bf16[112,512]{1,0:T(8,128)(2,1)S(1)}, bf16[112,512]{1,0:T(8,128)(2,1)S(1)}, u32[]{:S(2)}, u32[]{:S(2)}) collective-permute-start(bf16[112,512]{1,0:T(8,128)(2,1)S(1)} %get-tuple-element.34), channel_id=1, source_target_pairs={{0,128},{64,192},{128,0},{192,64},{1,129},{65,193},{129,1},{193,65... | collective-permute-start | bytes 344072 | tf_op jit(solution)/shard_map/ppermute | solution.py:22
  115.1 2.8 %collective-permute-done.41 = bf16[112,512]{1,0:T(8,128)(2,1)S(1)} collective-permute-done((bf16[112,512]{1,0:T(8,128)(2,1)S(1)}, bf16[112,512]{1,0:T(8,128)(2,1)S(1)}, u32[]{:S(2)}, u32[]{:S(2)}) %collective-permute-start.41) | collective-permute-done | bytes 114720 | tf_op jit(solution)/shard_map/ppermute | solution.py:22
  118.4 1.0 copy.8
  119.4 7.3 %all-to-all-start.1 = ((bf16[16,56,224]{2,1,0:T(8,128)(2,1)}), bf16[16,56,224]{2,1,0:T(8,128)(2,1)S(1)}, u32[]{:S(2)}, u32[]{:S(2)}) async-start(bf16[16,56,224]{2,1,0:T(8,128)(2,1)} %bitcast.20), calls=%async_computation.1 | async-start | bytes 917504 | tf_op jit(solution)/shard_map/all_to_all | solution.py:261
  127.6 9.2 %all-to-all-done.1 = bf16[16,56,224]{2,1,0:T(8,128)(2,1)S(1)} async-done(((bf16[16,56,224]{2,1,0:T(8,128)(2,1)}), bf16[16,56,224]{2,1,0:T(8,128)(2,1)S(1)}, u32[]{:S(2)}, u32[]{:S(2)}) %all-to-all-start.1) | async-done | bytes 401440 | tf_op jit(solution)/shard_map/all_to_all | solution.py:261
  137.4 5.4 %collective-permute-start.42 = (f32[56,112]{1,0:T(8,128)S(1)}, f32[56,112]{1,0:T(8,128)S(1)}, u32[]{:S(2)}, u32[]{:S(2)}) collective-permute-start(f32[56,112]{1,0:T(8,128)S(1)} %select_n.67), channel_id=1, source_target_pairs={{16,0},{0,16},{17,1},{1,17},{18,2},{2,18},{19,3},{3,19},{20,4},{4,... | collective-permute-start | bytes 75272 | tf_op jit(solution)/shard_map/ppermute | solution.py:17
  (114 shorter events, 20.3 us)
Async XLA Ops:
  0.0 4.3 %collective-permute-start.24 = (bf16[56,4,56]{2,1,0:T(4,128)(2,1)}, bf16[56,4,56]{2,1,0:T(4,128)(2,1)S(1)}, u32[]{:S(2)}, u32[]{:S(2)}) collective-permute-start(bf16[56,4,56]{2,1,0:T(4,128)(2,1)} %own.1), channel_id=1, source_target_pairs={{16,0},{0,16},{17,1},{1,17},{18,2},{2,18},{19,3},{3,19},{20,4},{4,... | collective-permute-start | bytes 75272 | tf_op jit(solution)/shard_map/ppermute | solution.py:17
  5.1 25.5 %copy-start.2 = (f32[512,1,512]{2,1,0:T(1,128)S(1)}, f32[512,1,512]{2,1,0:T(1,128)}, u32[]{:S(2)}) copy-start(f32[512,1,512]{2,1,0:T(1,128)} %param.7) | copy-start | bytes 3145732
  6.1 36.0 %all-to-all-start = ((bf16[16,56,224]{2,1,0:T(8,128)(2,1)}), bf16[16,56,224]{2,1,0:T(8,128)(2,1)S(1)}, u32[]{:S(2)}, u32[]{:S(2)}) async-start(bf16[16,56,224]{2,1,0:T(8,128)(2,1)} %shard_map.56), calls=%async_computation | async-start | bytes 917504 | tf_op jit(solution)/shard_map/all_to_all | solution.py:221
  13.8 4.8 %collective-permute-start = (bf16[1,32,896]{2,1,0:T(8,128)(2,1)S(1)}, bf16[1,32,896]{2,1,0:T(8,128)(2,1)S(1)}, u32[]{:S(2)}, u32[]{:S(2)}) collective-permute-start(bf16[1,32,896]{2,1,0:T(8,128)(2,1)S(1)} %bitcast.57), channel_id=1, source_target_pairs={{32,0},{0,32},{33,1},{1,33},{34,2},{2,34},{35,3},{3,35},{36,4},{4,... | collective-permute-start | bytes 172040 | tf_op jit(solution)/shard_map/ppermute | solution.py:17
  16.6 3.9 %collective-permute-start.8 = (bf16[1,32,896]{2,1,0:T(8,128)(2,1)S(1)}, bf16[1,32,896]{2,1,0:T(8,128)(2,1)S(1)}, u32[]{:S(2)}, u32[]{:S(2)}) collective-permute-start(bf16[1,32,896]{2,1,0:T(8,128)(2,1)S(1)} %bitcast.58), channel_id=1, source_target_pairs={{8,0},{0,8},{9,1},{1,9},{10,2},{2,10},{11,3},{3,11},{12,4},{4,12},... | collective-permute-start | bytes 172040 | tf_op jit(solution)/shard_map/ppermute | solution.py:17
  20.5 8.6 %collective-permute-start.10 = (bf16[2,32,896]{2,1,0:T(8,128)(2,1)S(1)}, bf16[2,32,896]{2,1,0:T(8,128)(2,1)S(1)}, u32[]{:S(2)}, u32[]{:S(2)}) collective-permute-start(bf16[2,32,896]{2,1,0:T(8,128)(2,1)S(1)} %get-tuple-element.40.refs_0_), channel_id=1, source_target_pairs={{7,0},{0,1},{1,2},{2,3},{3,4},{4,5},{5,6},{6,7},{15,8},{8,9},{9,10... | collective-permute-start | bytes 344072 | tf_op jit(solution)/shard_map/ppermute | solution.py:17
  22.7 6.4 %collective-permute-start.9 = (bf16[2,32,896]{2,1,0:T(8,128)(2,1)S(1)}, bf16[2,32,896]{2,1,0:T(8,128)(2,1)}, u32[]{:S(2)}, u32[]{:S(2)}) collective-permute-start(bf16[2,32,896]{2,1,0:T(8,128)(2,1)S(1)} %get-tuple-element.40.refs_0_), channel_id=1, source_target_pairs={{1,0},{2,1},{3,2},{4,3},{5,4},{6,5},{7,6},{0,7},{9,8},{10,9},{11,1... | collective-permute-start | bytes 344072 | tf_op jit(solution)/shard_map/ppermute | solution.py:17
  23.8 6.8 %collective-permute-start.1 = (bf16[2,32,896]{2,1,0:T(8,128)(2,1)S(1)}, bf16[2,32,896]{2,1,0:T(8,128)(2,1)S(1)}, u32[]{:S(2)}, u32[]{:S(2)}) collective-permute-start(bf16[2,32,896]{2,1,0:T(8,128)(2,1)S(1)} %get-tuple-element.41.refs_0_), channel_id=1, source_target_pairs={{64,0},{128,64},{192,128},{0,192},{65,1},{129,65},{193,129},{1,193... | collective-permute-start | bytes 344072 | tf_op jit(solution)/shard_map/ppermute | solution.py:17
  26.3 7.4 %collective-permute-start.2 = (bf16[2,32,896]{2,1,0:T(8,128)(2,1)S(1)}, bf16[2,32,896]{2,1,0:T(8,128)(2,1)S(1)}, u32[]{:S(2)}, u32[]{:S(2)}) collective-permute-start(bf16[2,32,896]{2,1,0:T(8,128)(2,1)S(1)} %get-tuple-element.41.refs_0_), channel_id=1, source_target_pairs={{128,0},{192,64},{0,128},{64,192},{129,1},{193,65},{1,129},{65,193... | collective-permute-start | bytes 344072 | tf_op jit(solution)/shard_map/ppermute | solution.py:17
  26.8 9.5 %collective-permute-start.3 = (bf16[2,32,896]{2,1,0:T(8,128)(2,1)S(1)}, bf16[2,32,896]{2,1,0:T(8,128)(2,1)S(1)}, u32[]{:S(2)}, u32[]{:S(2)}) collective-permute-start(bf16[2,32,896]{2,1,0:T(8,128)(2,1)S(1)} %get-tuple-element.41.refs_0_), channel_id=1, source_target_pairs={{192,0},{0,64},{64,128},{128,192},{193,1},{1,65},{65,129},{129,193... | collective-permute-start | bytes 344072 | tf_op jit(solution)/shard_map/ppermute | solution.py:17
  29.2 8.3 %copy-start.3 = (bf16[2,32,896]{2,1,0:T(8,128)(2,1)}, bf16[2,32,896]{2,1,0:T(8,128)(2,1)S(1)}, u32[]{:S(2)}) copy-start(bf16[2,32,896]{2,1,0:T(8,128)(2,1)S(1)} %collective-permute-done.10.refs_7_) | copy-start | bytes 344068
  29.2 8.3 %collective-permute-start.11 = (bf16[2,32,896]{2,1,0:T(8,128)(2,1)}, bf16[2,32,896]{2,1,0:T(8,128)(2,1)}, u32[]{:S(2)}, u32[]{:S(2)}) collective-permute-start(bf16[2,32,896]{2,1,0:T(8,128)(2,1)} %collective-permute-done.9.refs_1_), channel_id=1, source_target_pairs={{1,0},{2,1},{3,2},{4,3},{5,4},{6,5},{7,6},{0,7},{9,8},{10,9},{11,1... | collective-permute-start | bytes 344072 | tf_op jit(solution)/shard_map/ppermute | solution.py:17
  30.7 6.8 %collective-permute-start.12 = (bf16[2,32,896]{2,1,0:T(8,128)(2,1)S(1)}, bf16[2,32,896]{2,1,0:T(8,128)(2,1)}, u32[]{:S(2)}, u32[]{:S(2)}) collective-permute-start(bf16[2,32,896]{2,1,0:T(8,128)(2,1)S(1)} %collective-permute-done.10.refs_7_), channel_id=1, source_target_pairs={{7,0},{0,1},{1,2},{2,3},{3,4},{4,5},{5,6},{6,7},{15,8},{8,9},{9,10... | collective-permute-start | bytes 344072 | tf_op jit(solution)/shard_map/ppermute | solution.py:17
  30.7 36.7 %collective-permute-start.33 = (f32[2048,128]{1,0:T(8,128)S(1)}, f32[2048,128]{1,0:T(8,128)}, u32[]{:S(2)}, u32[]{:S(2)}) collective-permute-start(f32[2048,128]{1,0:T(8,128)S(1)} %bitcast.47), channel_id=1, source_target_pairs={{16,0},{0,16},{17,1},{1,17},{18,2},{2,18},{19,3},{3,19},{20,4},{4,... | collective-permute-start | bytes 3145736 | tf_op jit(solution)/shard_map/ppermute | solution.py:17
  33.7 5.6 %collective-permute-start.4 = (bf16[2,32,896]{2,1,0:T(8,128)(2,1)S(1)}, bf16[2,32,896]{2,1,0:T(8,128)(2,1)S(1)}, u32[]{:S(2)}, u32[]{:S(2)}) collective-permute-start(bf16[2,32,896]{2,1,0:T(8,128)(2,1)S(1)} %get-tuple-element.41.refs_0_), channel_id=1, source_target_pairs={{16,0},{0,16},{17,1},{1,17},{18,2},{2,18},{19,3},{3,19},{20,4},{4,... | collective-permute-start | bytes 344072 | tf_op jit(solution)/shard_map/ppermute | solution.py:17
  36.3 3.1 %collective-permute-start.5 = (bf16[2,32,896]{2,1,0:T(8,128)(2,1)S(1)}, bf16[2,32,896]{2,1,0:T(8,128)(2,1)S(1)}, u32[]{:S(2)}, u32[]{:S(2)}) collective-permute-start(bf16[2,32,896]{2,1,0:T(8,128)(2,1)S(1)} %collective-permute-done.1.refs_1_), channel_id=1, source_target_pairs={{16,0},{0,16},{17,1},{1,17},{18,2},{2,18},{19,3},{3,19},{20,4},{4,... | collective-permute-start | bytes 344072 | tf_op jit(solution)/shard_map/ppermute | solution.py:17
  37.5 2.5 %collective-permute-start.6 = (bf16[2,32,896]{2,1,0:T(8,128)(2,1)S(1)}, bf16[2,32,896]{2,1,0:T(8,128)(2,1)S(1)}, u32[]{:S(2)}, u32[]{:S(2)}) collective-permute-start(bf16[2,32,896]{2,1,0:T(8,128)(2,1)S(1)} %collective-permute-done.2.refs_2_), channel_id=1, source_target_pairs={{16,0},{0,16},{17,1},{1,17},{18,2},{2,18},{19,3},{3,19},{20,4},{4,... | collective-permute-start | bytes 344072 | tf_op jit(solution)/shard_map/ppermute | solution.py:17
  37.5 2.9 %collective-permute-start.7 = (bf16[2,32,896]{2,1,0:T(8,128)(2,1)S(1)}, bf16[2,32,896]{2,1,0:T(8,128)(2,1)S(1)}, u32[]{:S(2)}, u32[]{:S(2)}) collective-permute-start(bf16[2,32,896]{2,1,0:T(8,128)(2,1)S(1)} %collective-permute-done.3.refs_3_), channel_id=1, source_target_pairs={{16,0},{0,16},{17,1},{1,17},{18,2},{2,18},{19,3},{3,19},{20,4},{4,... | collective-permute-start | bytes 344072 | tf_op jit(solution)/shard_map/ppermute | solution.py:17
  39.4 3.2 %collective-permute-start.16 = (bf16[2,32,896]{2,1,0:T(8,128)(2,1)S(1)}, bf16[2,32,896]{2,1,0:T(8,128)(2,1)}, u32[]{:S(2)}, u32[]{:S(2)}) collective-permute-start(bf16[2,32,896]{2,1,0:T(8,128)(2,1)S(1)} %get-tuple-element.40.refs_0_), channel_id=1, source_target_pairs={{16,0},{0,16},{17,1},{1,17},{18,2},{2,18},{19,3},{3,19},{20,4},{4,... | collective-permute-start | bytes 344072 | tf_op jit(solution)/shard_map/ppermute | solution.py:17
  39.4 4.3 %collective-permute-start.17 = (bf16[2,32,896]{2,1,0:T(8,128)(2,1)}, bf16[2,32,896]{2,1,0:T(8,128)(2,1)}, u32[]{:S(2)}, u32[]{:S(2)}) collective-permute-start(bf16[2,32,896]{2,1,0:T(8,128)(2,1)} %collective-permute-done.9.refs_1_), channel_id=1, source_target_pairs={{16,0},{0,16},{17,1},{1,17},{18,2},{2,18},{19,3},{3,19},{20,4},{4,... | collective-permute-start | bytes 344072 | tf_op jit(solution)/shard_map/ppermute | solution.py:17
  39.9 6.2 %collective-permute-start.13 = (bf16[2,32,896]{2,1,0:T(8,128)(2,1)}, bf16[2,32,896]{2,1,0:T(8,128)(2,1)}, u32[]{:S(2)}, u32[]{:S(2)}) collective-permute-start(bf16[2,32,896]{2,1,0:T(8,128)(2,1)} %collective-permute-done.11.refs_2_), channel_id=1, source_target_pairs={{1,0},{2,1},{3,2},{4,3},{5,4},{6,5},{7,6},{0,7},{9,8},{10,9},{11,1... | collective-permute-start | bytes 344072 | tf_op jit(solution)/shard_map/ppermute | solution.py:17
  40.4 7.2 %collective-permute-start.14 = (bf16[2,32,896]{2,1,0:T(8,128)(2,1)}, bf16[2,32,896]{2,1,0:T(8,128)(2,1)}, u32[]{:S(2)}, u32[]{:S(2)}) collective-permute-start(bf16[2,32,896]{2,1,0:T(8,128)(2,1)} %collective-permute-done.12.refs_6_), channel_id=1, source_target_pairs={{7,0},{0,1},{1,2},{2,3},{3,4},{4,5},{5,6},{6,7},{15,8},{8,9},{9,10... | collective-permute-start | bytes 344072 | tf_op jit(solution)/shard_map/ppermute | solution.py:17
  43.0 4.9 %collective-permute-start.23 = (bf16[2,32,896]{2,1,0:T(8,128)(2,1)S(1)}, bf16[2,32,896]{2,1,0:T(8,128)(2,1)S(1)}, u32[]{:S(2)}, u32[]{:S(2)}) collective-permute-start(bf16[2,32,896]{2,1,0:T(8,128)(2,1)S(1)} %copy-done.4), channel_id=1, source_target_pairs={{16,0},{0,16},{17,1},{1,17},{18,2},{2,18},{19,3},{3,19},{20,4},{4,... | collective-permute-start | bytes 344072 | tf_op jit(solution)/shard_map/ppermute | solution.py:17
  43.7 6.1 %collective-permute-start.29 = (bf16[112,512]{1,0:T(8,128)(2,1)S(1)}, bf16[112,512]{1,0:T(8,128)(2,1)S(1)}, u32[]{:S(2)}, u32[]{:S(2)}) collective-permute-start(bf16[112,512]{1,0:T(8,128)(2,1)S(1)} %get-tuple-element.26), channel_id=1, source_target_pairs={{64,0},{128,64},{192,128},{0,192},{65,1},{129,65},{193,129},{1,193... | collective-permute-start | bytes 344072 | tf_op jit(solution)/shard_map/ppermute | solution.py:17
  46.1 5.9 %collective-permute-start.30 = (bf16[112,512]{1,0:T(8,128)(2,1)S(1)}, bf16[112,512]{1,0:T(8,128)(2,1)S(1)}, u32[]{:S(2)}, u32[]{:S(2)}) collective-permute-start(bf16[112,512]{1,0:T(8,128)(2,1)S(1)} %get-tuple-element.26), channel_id=1, source_target_pairs={{128,0},{192,64},{0,128},{64,192},{129,1},{193,65},{1,129},{65,193... | collective-permute-start | bytes 344072 | tf_op jit(solution)/shard_map/ppermute | solution.py:17
  47.6 7.1 %collective-permute-start.31 = (bf16[112,512]{1,0:T(8,128)(2,1)S(1)}, bf16[112,512]{1,0:T(8,128)(2,1)S(1)}, u32[]{:S(2)}, u32[]{:S(2)}) collective-permute-start(bf16[112,512]{1,0:T(8,128)(2,1)S(1)} %get-tuple-element.26), channel_id=1, source_target_pairs={{192,0},{0,64},{64,128},{128,192},{193,1},{1,65},{65,129},{129,193... | collective-permute-start | bytes 344072 | tf_op jit(solution)/shard_map/ppermute | solution.py:17
  47.9 8.2 %copy-start.6 = (bf16[2,32,896]{2,1,0:T(8,128)(2,1)}, bf16[2,32,896]{2,1,0:T(8,128)(2,1)S(1)}, u32[]{:S(2)}) copy-start(bf16[2,32,896]{2,1,0:T(8,128)(2,1)S(1)} %collective-permute-done.23.refs_15_) | copy-start | bytes 344068
  47.9 8.2 %collective-permute-start.18 = (bf16[2,32,896]{2,1,0:T(8,128)(2,1)}, bf16[2,32,896]{2,1,0:T(8,128)(2,1)S(1)}, u32[]{:S(2)}, u32[]{:S(2)}) collective-permute-start(bf16[2,32,896]{2,1,0:T(8,128)(2,1)} %collective-permute-done.11.refs_2_), channel_id=1, source_target_pairs={{16,0},{0,16},{17,1},{1,17},{18,2},{2,18},{19,3},{3,19},{20,4},{4,... | collective-permute-start | bytes 344072 | tf_op jit(solution)/shard_map/ppermute | solution.py:17
  49.7 8.7 %collective-permute-start.22 = (bf16[2,32,896]{2,1,0:T(8,128)(2,1)}, bf16[2,32,896]{2,1,0:T(8,128)(2,1)S(1)}, u32[]{:S(2)}, u32[]{:S(2)}) collective-permute-start(bf16[2,32,896]{2,1,0:T(8,128)(2,1)} %collective-permute-done.12.refs_6_), channel_id=1, source_target_pairs={{16,0},{0,16},{17,1},{1,17},{18,2},{2,18},{19,3},{3,19},{20,4},{4,... | collective-permute-start | bytes 344072 | tf_op jit(solution)/shard_map/ppermute | solution.py:17
  52.1 8.3 %collective-permute-start.15 = (bf16[2,32,896]{2,1,0:T(8,128)(2,1)}, bf16[2,32,896]{2,1,0:T(8,128)(2,1)S(1)}, u32[]{:S(2)}, u32[]{:S(2)}) collective-permute-start(bf16[2,32,896]{2,1,0:T(8,128)(2,1)} %collective-permute-done.13.refs_3_), channel_id=1, source_target_pairs={{1,0},{2,1},{3,2},{4,3},{5,4},{6,5},{7,6},{0,7},{9,8},{10,9},{11,1... | collective-permute-start | bytes 344072 | tf_op jit(solution)/shard_map/ppermute | solution.py:17
  54.7 5.8 %collective-permute-start.25 = (bf16[112,512]{1,0:T(8,128)(2,1)S(1)}, bf16[112,512]{1,0:T(8,128)(2,1)S(1)}, u32[]{:S(2)}, u32[]{:S(2)}) collective-permute-start(bf16[112,512]{1,0:T(8,128)(2,1)S(1)} %get-tuple-element.25), channel_id=1, source_target_pairs={{32,0},{0,32},{33,1},{1,33},{34,2},{2,34},{35,3},{3,35},{36,4},{4,... | collective-permute-start | bytes 344072 | tf_op jit(solution)/shard_map/ppermute | solution.py:17
  56.8 23.3 %collective-permute-start.32 = (bf16[4,112,512]{2,1,0:T(8,128)(2,1)S(1)}, bf16[4,112,512]{2,1,0:T(8,128)(2,1)S(1)}, u32[]{:S(2)}, u32[]{:S(2)}) collective-permute-start(bf16[4,112,512]{2,1,0:T(8,128)(2,1)S(1)} %pad_maximum_fusion.refs_20_), channel_id=1, source_target_pairs={{32,0},{0,32},{33,1},{1,33},{34,2},{2,34},{35,3},{3,35},{36,4},{4,... | collective-permute-start | bytes 1376264 | tf_op jit(solution)/shard_map/ppermute | solution.py:17
  58.4 5.0 %collective-permute-start.19 = (bf16[2,32,896]{2,1,0:T(8,128)(2,1)}, bf16[2,32,896]{2,1,0:T(8,128)(2,1)S(1)}, u32[]{:S(2)}, u32[]{:S(2)}) collective-permute-start(bf16[2,32,896]{2,1,0:T(8,128)(2,1)} %collective-permute-done.13.refs_3_), channel_id=1, source_target_pairs={{16,0},{0,16},{17,1},{1,17},{18,2},{2,18},{19,3},{3,19},{20,4},{4,... | collective-permute-start | bytes 344072 | tf_op jit(solution)/shard_map/ppermute | solution.py:17
  60.3 5.0 %collective-permute-start.21 = (bf16[2,32,896]{2,1,0:T(8,128)(2,1)}, bf16[2,32,896]{2,1,0:T(8,128)(2,1)S(1)}, u32[]{:S(2)}, u32[]{:S(2)}) collective-permute-start(bf16[2,32,896]{2,1,0:T(8,128)(2,1)} %collective-permute-done.14.refs_5_), channel_id=1, source_target_pairs={{16,0},{0,16},{17,1},{1,17},{18,2},{2,18},{19,3},{3,19},{20,4},{4,... | collective-permute-start | bytes 344072 | tf_op jit(solution)/shard_map/ppermute | solution.py:17
  60.5 5.7 %collective-permute-start.20 = (bf16[2,32,896]{2,1,0:T(8,128)(2,1)S(1)}, bf16[2,32,896]{2,1,0:T(8,128)(2,1)S(1)}, u32[]{:S(2)}, u32[]{:S(2)}) collective-permute-start(bf16[2,32,896]{2,1,0:T(8,128)(2,1)S(1)} %collective-permute-done.15.refs_4_), channel_id=1, source_target_pairs={{16,0},{0,16},{17,1},{1,17},{18,2},{2,18},{19,3},{3,19},{20,4},{4,... | collective-permute-start | bytes 344072 | tf_op jit(solution)/shard_map/ppermute | solution.py:17
  64.1 7.3 %collective-permute-start.26 = (bf16[2,112,512]{2,1,0:T(8,128)(2,1)S(1)}, bf16[2,112,512]{2,1,0:T(8,128)(2,1)S(1)}, u32[]{:S(2)}, u32[]{:S(2)}) collective-permute-start(bf16[2,112,512]{2,1,0:T(8,128)(2,1)S(1)} %pad_maximum_fusion.1.refs_16_), channel_id=1, source_target_pairs={{64,0},{128,64},{192,128},{0,192},{65,1},{129,65},{193,129},{1,193... | collective-permute-start | bytes 688136 | tf_op jit(solution)/shard_map/ppermute | solution.py:17
  66.0 8.5 %collective-permute-start.27 = (bf16[2,112,512]{2,1,0:T(8,128)(2,1)S(1)}, bf16[2,112,512]{2,1,0:T(8,128)(2,1)}, u32[]{:S(2)}, u32[]{:S(2)}) collective-permute-start(bf16[2,112,512]{2,1,0:T(8,128)(2,1)S(1)} %pad_maximum_fusion.1.refs_16_), channel_id=1, source_target_pairs={{128,0},{192,64},{0,128},{64,192},{129,1},{193,65},{1,129},{65,193... | collective-permute-start | bytes 688136 | tf_op jit(solution)/shard_map/ppermute | solution.py:17
  66.8 13.3 %collective-permute-start.28 = (bf16[2,112,512]{2,1,0:T(8,128)(2,1)S(1)}, bf16[2,112,512]{2,1,0:T(8,128)(2,1)}, u32[]{:S(2)}, u32[]{:S(2)}) collective-permute-start(bf16[2,112,512]{2,1,0:T(8,128)(2,1)S(1)} %pad_maximum_fusion.1.refs_16_), channel_id=1, source_target_pairs={{192,0},{0,64},{64,128},{128,192},{193,1},{1,65},{65,129},{129,193... | collective-permute-start | bytes 688136 | tf_op jit(solution)/shard_map/ppermute | solution.py:17
  94.0 12.9 %collective-permute-start.34 = (bf16[2,112,512]{2,1,0:T(8,128)(2,1)S(1)}, bf16[2,112,512]{2,1,0:T(8,128)(2,1)S(1)}, u32[]{:S(2)}, u32[]{:S(2)}) collective-permute-start(bf16[2,112,512]{2,1,0:T(8,128)(2,1)S(1)} %get-tuple-element.28), channel_id=1, source_target_pairs={{0,64},{64,128},{128,192},{192,0},{1,65},{65,129},{129,193},{193,1... | collective-permute-start | bytes 688136 | tf_op jit(solution)/shard_map/ppermute | solution.py:22
  94.1 12.8 %collective-permute-start.35 = (bf16[2,112,512]{2,1,0:T(8,128)(2,1)S(1)}, bf16[2,112,512]{2,1,0:T(8,128)(2,1)S(1)}, u32[]{:S(2)}, u32[]{:S(2)}) collective-permute-start(bf16[2,112,512]{2,1,0:T(8,128)(2,1)S(1)} %get-tuple-element.29), channel_id=1, source_target_pairs={{0,192},{64,0},{128,64},{192,128},{1,193},{65,1},{129,65},{193,129... | collective-permute-start | bytes 688136 | tf_op jit(solution)/shard_map/ppermute | solution.py:22
  96.8 10.1 %collective-permute-start.36 = (bf16[2,112,512]{2,1,0:T(8,128)(2,1)S(1)}, bf16[2,112,512]{2,1,0:T(8,128)(2,1)S(1)}, u32[]{:S(2)}, u32[]{:S(2)}) collective-permute-start(bf16[2,112,512]{2,1,0:T(8,128)(2,1)S(1)} %get-tuple-element.30), channel_id=1, source_target_pairs={{0,128},{64,192},{128,0},{192,64},{1,129},{65,193},{129,1},{193,65... | collective-permute-start | bytes 688136 | tf_op jit(solution)/shard_map/ppermute | solution.py:22
  96.8 12.5 %collective-permute-start.38 = (bf16[4,112,512]{2,1,0:T(8,128)(2,1)S(1)}, bf16[4,112,512]{2,1,0:T(8,128)(2,1)S(1)}, u32[]{:S(2)}, u32[]{:S(2)}) collective-permute-start(bf16[4,112,512]{2,1,0:T(8,128)(2,1)S(1)} %get-tuple-element.32), channel_id=1, source_target_pairs={{0,32},{32,0},{1,33},{33,1},{2,34},{34,2},{3,35},{35,3},{4,36},{36... | collective-permute-start | bytes 1376264 | tf_op jit(solution)/shard_map/ppermute | solution.py:22
  107.0 6.7 %collective-permute-start.37 = (bf16[112,512]{1,0:T(8,128)(2,1)S(1)}, bf16[112,512]{1,0:T(8,128)(2,1)S(1)}, u32[]{:S(2)}, u32[]{:S(2)}) collective-permute-start(bf16[112,512]{1,0:T(8,128)(2,1)S(1)} %fusion.8), channel_id=1, source_target_pairs={{0,32},{32,0},{1,33},{33,1},{2,34},{34,2},{3,35},{35,3},{4,36},{36... | collective-permute-start | bytes 344072 | tf_op jit(solution)/shard_map/ppermute | solution.py:22
  109.4 4.9 %collective-permute-start.39 = (bf16[112,512]{1,0:T(8,128)(2,1)S(1)}, bf16[112,512]{1,0:T(8,128)(2,1)S(1)}, u32[]{:S(2)}, u32[]{:S(2)}) collective-permute-start(bf16[112,512]{1,0:T(8,128)(2,1)S(1)} %get-tuple-element.33), channel_id=1, source_target_pairs={{0,64},{64,128},{128,192},{192,0},{1,65},{65,129},{129,193},{193,1... | collective-permute-start | bytes 344072 | tf_op jit(solution)/shard_map/ppermute | solution.py:22
  110.1 5.1 %collective-permute-start.40 = (bf16[112,512]{1,0:T(8,128)(2,1)S(1)}, bf16[112,512]{1,0:T(8,128)(2,1)S(1)}, u32[]{:S(2)}, u32[]{:S(2)}) collective-permute-start(bf16[112,512]{1,0:T(8,128)(2,1)S(1)} %get-tuple-element.35), channel_id=1, source_target_pairs={{0,192},{64,0},{128,64},{192,128},{1,193},{65,1},{129,65},{193,129... | collective-permute-start | bytes 344072 | tf_op jit(solution)/shard_map/ppermute | solution.py:22
  112.2 5.7 %collective-permute-start.41 = (bf16[112,512]{1,0:T(8,128)(2,1)S(1)}, bf16[112,512]{1,0:T(8,128)(2,1)S(1)}, u32[]{:S(2)}, u32[]{:S(2)}) collective-permute-start(bf16[112,512]{1,0:T(8,128)(2,1)S(1)} %get-tuple-element.34), channel_id=1, source_target_pairs={{0,128},{64,192},{128,0},{192,64},{1,129},{65,193},{129,1},{193,65... | collective-permute-start | bytes 344072 | tf_op jit(solution)/shard_map/ppermute | solution.py:22
  119.4 17.4 %all-to-all-start.1 = ((bf16[16,56,224]{2,1,0:T(8,128)(2,1)}), bf16[16,56,224]{2,1,0:T(8,128)(2,1)S(1)}, u32[]{:S(2)}, u32[]{:S(2)}) async-start(bf16[16,56,224]{2,1,0:T(8,128)(2,1)} %bitcast.20), calls=%async_computation.1 | async-start | bytes 917504 | tf_op jit(solution)/shard_map/all_to_all | solution.py:261
  137.4 6.2 %collective-permute-start.42 = (f32[56,112]{1,0:T(8,128)S(1)}, f32[56,112]{1,0:T(8,128)S(1)}, u32[]{:S(2)}, u32[]{:S(2)}) collective-permute-start(f32[56,112]{1,0:T(8,128)S(1)} %select_n.67), channel_id=1, source_target_pairs={{16,0},{0,16},{17,1},{1,17},{18,2},{2,18},{19,3},{3,19},{20,4},{4,... | collective-permute-start | bytes 75272 | tf_op jit(solution)/shard_map/ppermute | solution.py:17
  (19 other events, 33.5 us)

commit v4 on v3

--- a/solution.py
+++ b/solution.py
@@ -10,6 +10,7 @@
 GRP = ("y_lo", "z")
 BF16 = jnp.bfloat16
 F32 = jnp.float32
+FIRST_PART = 640
 
 
 def from_ahead(x, axis, offset):
@@ -69,7 +70,7 @@
     return kernel_call(body, [shape], [core, own, other])[0]
 
 
-def right_of(core, turned, columns, half):
+def right_of(core, turned, columns, half, first_part):
     n_grp, n_d, width = turned.shape
     n_q = columns.shape[0]
     rows = width // half
@@ -79,11 +80,35 @@
         right = lax.dot_general(
             left, columns[...], (((1,), (1,)), ((), ())), preferred_element_type=F32
         ).astype(BF16)
-        for k in range(half):
-            outs[k][...] = right[k * rows : (k + 1) * rows]
-
-    outs = [jax.ShapeDtypeStruct((rows, n_q), BF16)] * half
+        whole = jnp.concatenate([right[k * rows : (k + 1) * rows] for k in range(half)], axis=1)
+        outs[0][...] = whole[:, :first_part]
+        outs[1][...] = whole[:, first_part:]
+
+    widths = (first_part, half * n_q - first_part)
+    outs = [jax.ShapeDtypeStruct((rows, w), BF16) for w in widths]
     return kernel_call(body, outs, [core, turned, columns], 2 * n_q * n_grp * n_d * width)
+
+
+def ladder_of(core, parts, columns, n_grp):
+    n_q, nv = columns.shape
+    rows = parts[0][0].shape[0]
+    half = len(parts)
+    count = [len(p) for p in parts]
+
+    def body(core, *refs):
+        columns, out = refs[-2:]
+        at, sums = 0, []
+        for n in count:
+            sums.append(sum(r[...].astype(F32) for r in refs[at : at + n]).astype(BF16))
+            at += n
+        whole = jnp.dot(
+            jnp.concatenate(sums, axis=0), columns[...], preferred_element_type=F32
+        )
+        out[...] = whole.T.astype(BF16).reshape(n_grp, nv // n_grp, half * rows)
+
+    shape = jax.ShapeDtypeStruct((n_grp, nv // n_grp, half * rows), BF16)
+    args = [core, *[x for p in parts for x in p], columns]
+    return kernel_call(body, [shape], args, 2 * n_q * nv * half * rows)[0]
 
 
 def placed_by_block(place, pieces, n_x, n_h):
@@ -109,7 +134,8 @@
     pts, nv = pieces[0].shape[1:]
     step = n_l * pts
     total = step * len(pieces)
-    n_q = right[0].shape[2]
+    n_q = (right[0].shape[2] + right[-1].shape[2]) // half
+    cut = right[0].shape[2]
     lanes = z_own.shape[1]
     per_row = n_q // lanes
     n_plane = n_x * n_h
@@ -142,30 +168,38 @@
                 turned[slots[j], :, i * step : (i + 2) * step] = flipped[
                     j * share : (j + 1) * share
                 ]
+        for ox in range(n_x):
+            for oh in range(n_h):
+                at = ((place[2] + ox) % n_x) * n_h + (place[3] + oh) % n_h
+                for k in range(half):
+                    low, high = k * n_q, (k + 1) * n_q
+                    if low < cut:
+                        end = min(high, cut)
+                        right[k, at, :, : end - low] = rights[ox][oh, :, low:end]
+                    if high > cut:
+                        start = max(low, cut)
+                        right[k, at, :, start - low :] = rights[n_x + oh][
+                            ox, :, start - cut : high - cut
+                        ]
         for k in range(half):
-            for ox in range(n_x):
-                for oh in range(n_h):
-                    at = ((place[2] + ox) % n_x) * n_h + (place[3] + oh) % n_h
-                    right[at] = rights[ox][oh] if k == 0 else rights[n_x + oh][ox]
+            products = jnp.dot(
+                rows[...],
+                right[k].reshape(nv, n_q),
+                preferred_element_type=F32,
+            )
             for core, z in enumerate((z_own, z_other)):
-                base = core * n_z * step
-                products = jnp.dot(
-                    rows[base : base + n_z * step, :],
-                    right[...].reshape(nv, n_q),
-                    preferred_element_type=F32,
-                )
                 if k == 0:
                     copies[core].wait()
                 for s in range(n_z * n_l):
                     oz, ol = s // n_l, s % n_l
                     g = ((place[1] + ol) % n_l) * n_z + (place[0] + oz) % n_z
                     first = g * (pts * per_row)
+                    at = core * n_z * step + s * pts
                     for j in range(per_row):
                         zs = z[pl.ds(first + j, pts, stride=per_row), :]
-                        weighted[
-                            base + s * pts : base + (s + 1) * pts, j * lanes : (j + 1) * lanes
-                        ] = (
-                            zs * products[s * pts : (s + 1) * pts, j * lanes : (j + 1) * lanes]
+                        cols = slice(j * lanes, (j + 1) * lanes)
+                        weighted[at : at + pts, cols] = (
+                            zs * products[at : at + pts, cols]
                         ).astype(BF16)
             back = jnp.dot(
                 turned[...].reshape(nv, total), weighted[...], preferred_element_type=F32
@@ -186,17 +220,13 @@
         pltpu.VMEM((total, nv), BF16),
         pltpu.VMEM((n_plane, share, total), BF16),
         pltpu.VMEM((total, n_q), BF16),
-        pltpu.VMEM((n_plane, share, n_q), BF16),
+        pltpu.VMEM((half, n_plane, share, n_q), BF16),
         pltpu.VMEM(z_own.shape, F32),
         pltpu.VMEM(z_own.shape, F32),
         pltpu.SemaphoreType.DMA((2,)),
     ]
     args = [place, *pieces, *right, z_own, z_other]
     return kernel_call(body, outs, args, flops, scratch, (len(args) - 2, len(args) - 1))
-
-
-def contract_last(a, b):
-    return lax.dot_general(a, b, (((0,), (1,)), ((), ())), preferred_element_type=F32)
 
 
 def in_core_order(own, other, axis):
@@ -225,7 +255,7 @@
     own += [from_ahead(piece, "core", 1) for piece in own]
     columns = placed_by_block(jnp.stack([my_x, my_h, my_core]), own, n_x, n_h).reshape(-1, nv)
 
-    right = right_of(my_core[None], turned, columns, half)
+    right = right_of(my_core[None], turned, columns, half, FIRST_PART)
     low = from_ahead(right[0], "y_hi", 1)
     high = [right[1]] + [from_ahead(right[1], "x", o) for o in (1, 3, 2)]
     low = jnp.stack([right[0], low])
@@ -235,16 +265,16 @@
 
     pair = steps_along(grid_factor[None], "y_lo")
     own = {0: pair}
-    up = down = pair
-    for o in range(1, n_z // 2 + 1):
-        up = from_ahead(up, "z", 1)
-        if o < n_z - o:
-            down = from_ahead(down, "z", -1)
-            up, down = lax.optimization_barrier((up, down))
-            own[n_z - o] = down
-        own[o] = up
+    own[1], own[n_z - 1] = from_ahead(pair, "z", 1), from_ahead(pair, "z", -1)
+    own[n_z // 2] = from_ahead(pair, "z", n_z // 2)
+    for o in range(2, n_z // 2):
+        up, down = lax.optimization_barrier((own[o - 1], own[n_z - o + 1]))
+        own[o], own[n_z - o] = from_ahead(up, "z", 1), from_ahead(down, "z", -1)
     own = [own[o] for o in range(n_z)]
-    own += [from_ahead(piece, "core", 1) for piece in own]
+    others = []
+    for o in range(n_z):
+        others.append(from_ahead(own[o], "core", 1))
+    own += others
     z = metric.reshape(-1, 128)
     z_other = from_ahead(z, "core", 1)
     place = jnp.stack([my_z, my_l, my_x, my_h])
@@ -256,8 +286,8 @@
     high = [total([high[0][o], high_arrived[o]]) for o in range(n_x)]
     low_arrived = to_ahead(low[1], "y_hi", 1)
     high_arrived = [to_ahead(high[o], "x", o) for o in (1, 3, 2)]
-    back = jnp.concatenate([total([low[0], low_arrived]), total([high[0]] + high_arrived)], axis=0)
-    ladder = contract_last(columns, back).astype(BF16).reshape(n_grp, n_d, half * 2 * n_c)
+    parts = [[low[0], low_arrived], [high[0], *high_arrived]]
+    ladder = ladder_of(my_core[None], parts, columns, n_grp)
     ladder = lax.all_to_all(ladder, GRP, 0, 0, tiled=True)
     ladder = ladder.astype(F32).sum(axis=0).reshape(n_d, half, 2, n_c)
     keep = jnp.where(first, ladder[:, :, 0], ladder[:, :, 1])

time: 146 us -> 156 us (1.068)
  waiting for transfers between devices: 44.2 us -> 50.9 us
  Pallas kernels: 8.84 us -> 10.4 us
    ppermute x35, waiting for transfers between devices: 20.7 us -> 27.1 us  [from_ahead(): return lax.ppermute(x, axis, [((i + offset) % n, i) for i in range(n)])]
    ppermute x35, starting transfers between devices: 51.4 us -> 55.4 us  [from_ahead(): return lax.ppermute(x, axis, [((i + offset) % n, i) for i in range(n)])]
    all_to_all x1, starting transfers between devices: 7.33 us -> 4.69 us  [local(): ladder = lax.all_to_all(ladder, GRP, 0, 0, tiled=True)]
    unnamed x45 -> x49, local copies, waits for them, and re-layouts: 11.7 us -> 13.7 us
    pallas_call x4 -> x5, Pallas kernels: 8.84 us -> 10.4 us  [kernel_call(): pl.pallas_call(body, out_shape=outs, in_specs=[smem] + [pl.BlockSpec(memo...]
  transfers between devices with their start and end apart: 45 -> 45, of which waited for: 18 -> 16; matrix products, arithmetic and copies ran while one was open for 1% -> 1% of each run, Pallas kernels for 1% -> 1%
where the time goes in v4:
time: 156 us; the launch traced here: 155 us
  starting transfers between devices  76.8 us (49%)
  waiting for transfers between devices  50.9 us (33%)
  local copies, waits for them, and re-layouts  15.7 us (10%)
  Pallas kernels  10.4 us (7%)
    ppermute x35, starting transfers between devices, from_ahead(): return lax.ppermute(x, axis, [((i + offset) % n, i) for i in range(n)])  55.4 us
    ppermute x35, waiting for transfers between devices, from_ahead(): return lax.ppermute(x, axis, [((i + offset) % n, i) for i in range(n)])  27.1 us
    ppermute x8, waiting for transfers between devices, to_ahead(): return lax.ppermute(x, axis, [(i, (i + offset) % n) for i in range(n)])  14.6 us
    unnamed x49, local copies, waits for them, and re-layouts  13.7 us
    pallas_call x5, Pallas kernels, kernel_call(): pl.pallas_call(body, out_shape=outs, in_specs=[smem] + [pl.BlockSpec(memo...  10.4 us
    all_to_all x1, waiting for transfers between devices, local(): ladder = lax.all_to_all(ladder, GRP, 0, 0, tiled=True)  9.2 us
    ppermute x8, starting transfers between devices, to_ahead(): return lax.ppermute(x, axis, [(i, (i + offset) % n) for i in range(n)])  9.02 us
    all_to_all x1, starting transfers between devices, local(): turned = lax.all_to_all(turned, GRP, 0, 0, tiled=True)  7.73 us
  transfers between devices with their start and end apart: 45, of which 16 were waited for; matrix products, arithmetic and copies ran while one was open for 1% of the time, Pallas kernels for 1%

profile of v4, /device:TPU:1, one launch (start us, length us, event | category | flops | bytes accessed | tf_op | source)
XLA Modules:
  0.0 155.1 jit_solution(7380244565818104755)
XLA Ops:
  0.0 3.2 %collective-permute-start.16 = (bf16[56,4,56]{2,1,0:T(4,128)(2,1)}, bf16[56,4,56]{2,1,0:T(4,128)(2,1)S(1)}, u32[]{:S(2)}, u32[]{:S(2)}) collective-permute-start(bf16[56,4,56]{2,1,0:T(4,128)(2,1)} %own.1), channel_id=1, source_target_pairs={{16,0},{0,16},{17,1},{1,17},{18,2},{2,18},{19,3},{3,19},{20,4},{4,... | collective-permute-start | bytes 75272 | tf_op jit(solution)/shard_map/ppermute | solution.py:18
  3.2 1.1 collective-permute-done.16.other
  5.1 1.0 shard_map.55
  6.1 7.7 %all-to-all-start = ((bf16[16,56,224]{2,1,0:T(8,128)(2,1)}), bf16[16,56,224]{2,1,0:T(8,128)(2,1)S(1)}, u32[]{:S(2)}, u32[]{:S(2)}) async-start(bf16[16,56,224]{2,1,0:T(8,128)(2,1)} %shard_map.55), calls=%async_computation | async-start | bytes 917504 | tf_op jit(solution)/shard_map/all_to_all | solution.py:251
  13.9 1.5 collective-permute-start
  15.3 2.6 %collective-permute-start.17 = (bf16[1,32,896]{2,1,0:T(8,128)(2,1)S(1)}, bf16[1,32,896]{2,1,0:T(8,128)(2,1)S(1)}, u32[]{:S(2)}, u32[]{:S(2)}) collective-permute-start(bf16[1,32,896]{2,1,0:T(8,128)(2,1)S(1)} %bitcast.50), channel_id=1, source_target_pairs={{32,0},{0,32},{33,1},{1,33},{34,2},{2,34},{35,3},{3,35},{36,4},{4,... | collective-permute-start | bytes 172040 | tf_op jit(solution)/shard_map/ppermute | solution.py:18
  17.9 3.0 %collective-permute-done.17 = bf16[1,32,896]{2,1,0:T(8,128)(2,1)S(1)} collective-permute-done((bf16[1,32,896]{2,1,0:T(8,128)(2,1)S(1)}, bf16[1,32,896]{2,1,0:T(8,128)(2,1)S(1)}, u32[]{:S(2)}, u32[]{:S(2)}) %collective-permute-start.17) | collective-permute-done | bytes 57376 | tf_op jit(solution)/shard_map/ppermute | solution.py:18
  20.9 2.6 %collective-permute-start.18 = (bf16[2,32,896]{2,1,0:T(8,128)(2,1)S(1)}, bf16[2,32,896]{2,1,0:T(8,128)(2,1)S(1)}, u32[]{:S(2)}, u32[]{:S(2)}) collective-permute-start(bf16[2,32,896]{2,1,0:T(8,128)(2,1)S(1)} %get-tuple-element.39.refs_0_), channel_id=1, source_target_pairs={{64,0},{128,64},{192,128},{0,192},{65,1},{129,65},{193,129},{1,193... | collective-permute-start | bytes 344072 | tf_op jit(solution)/shard_map/ppermute | solution.py:18
  24.0 3.9 %collective-permute-start.1 = (bf16[2,32,896]{2,1,0:T(8,128)(2,1)S(1)}, bf16[2,32,896]{2,1,0:T(8,128)(2,1)}, u32[]{:S(2)}, u32[]{:S(2)}) collective-permute-start(bf16[2,32,896]{2,1,0:T(8,128)(2,1)S(1)} %get-tuple-element.40.refs_0_), channel_id=1, source_target_pairs={{1,0},{2,1},{3,2},{4,3},{5,4},{6,5},{7,6},{0,7},{9,8},{10,9},{11,1... | collective-permute-start | bytes 344072 | tf_op jit(solution)/shard_map/ppermute | solution.py:18
  27.9 2.2 %collective-permute-start.33 = (f32[2048,128]{1,0:T(8,128)S(1)}, f32[2048,128]{1,0:T(8,128)}, u32[]{:S(2)}, u32[]{:S(2)}) collective-permute-start(f32[2048,128]{1,0:T(8,128)S(1)} %bitcast.39), channel_id=1, source_target_pairs={{16,0},{0,16},{17,1},{1,17},{18,2},{2,18},{19,3},{3,19},{20,4},{4,... | collective-permute-start | bytes 3145736 | tf_op jit(solution)/shard_map/ppermute | solution.py:18
  30.7 1.1 collective-permute-start.21
  31.8 6.3 %collective-permute-start.6 = (bf16[2,32,896]{2,1,0:T(8,128)(2,1)S(1)}, bf16[2,32,896]{2,1,0:T(8,128)(2,1)}, u32[]{:S(2)}, u32[]{:S(2)}) collective-permute-start(bf16[2,32,896]{2,1,0:T(8,128)(2,1)S(1)} %get-tuple-element.40.refs_0_), channel_id=1, source_target_pairs={{4,0},{5,1},{6,2},{7,3},{0,4},{1,5},{2,6},{3,7},{12,8},{13,9},{14,... | collective-permute-start | bytes 344072 | tf_op jit(solution)/shard_map/ppermute | solution.py:18
  38.9 2.4 %collective-permute-done.6.refs_4_ = bf16[2,32,896]{2,1,0:T(8,128)(2,1)} collective-permute-done((bf16[2,32,896]{2,1,0:T(8,128)(2,1)S(1)}, bf16[2,32,896]{2,1,0:T(8,128)(2,1)}, u32[]{:S(2)}, u32[]{:S(2)}) %collective-permute-start.6) | collective-permute-done | bytes 114720 | tf_op jit(solution)/shard_map/ppermute | solution.py:18
  41.3 2.6 %collective-permute-start.24 = (bf16[2,32,896]{2,1,0:T(8,128)(2,1)S(1)}, bf16[2,32,896]{2,1,0:T(8,128)(2,1)S(1)}, u32[]{:S(2)}, u32[]{:S(2)}) collective-permute-start(bf16[2,32,896]{2,1,0:T(8,128)(2,1)S(1)} %collective-permute-done.20.refs_3_), channel_id=1, source_target_pairs={{16,0},{0,16},{17,1},{1,17},{18,2},{2,18},{19,3},{3,19},{20,4},{4,... | collective-permute-start | bytes 344072 | tf_op jit(solution)/shard_map/ppermute | solution.py:18
  44.5 2.6 %collective-permute-start.3 = (bf16[2,32,896]{2,1,0:T(8,128)(2,1)}, bf16[2,32,896]{2,1,0:T(8,128)(2,1)S(1)}, u32[]{:S(2)}, u32[]{:S(2)}) collective-permute-start(bf16[2,32,896]{2,1,0:T(8,128)(2,1)} %collective-permute-done.1.refs_1_), channel_id=1, source_target_pairs={{1,0},{2,1},{3,2},{4,3},{5,4},{6,5},{7,6},{0,7},{9,8},{10,9},{11,1... | collective-permute-start | bytes 344072 | tf_op jit(solution)/shard_map/ppermute | solution.py:18
  48.4 3.2 %collective-permute-done.3.refs_2_ = bf16[2,32,896]{2,1,0:T(8,128)(2,1)S(1)} collective-permute-done((bf16[2,32,896]{2,1,0:T(8,128)(2,1)}, bf16[2,32,896]{2,1,0:T(8,128)(2,1)S(1)}, u32[]{:S(2)}, u32[]{:S(2)}) %collective-permute-start.3) | collective-permute-done | bytes 114720 | tf_op jit(solution)/shard_map/ppermute | solution.py:18
  53.4 1.9 %collective-permute-start.29 = (bf16[112,384]{1,0:T(8,128)(2,1)S(1)}, bf16[112,384]{1,0:T(8,128)(2,1)S(1)}, u32[]{:S(2)}, u32[]{:S(2)}) collective-permute-start(bf16[112,384]{1,0:T(8,128)(2,1)S(1)} %get-tuple-element.22), channel_id=1, source_target_pairs={{64,0},{128,64},{192,128},{0,192},{65,1},{129,65},{193,129},{1,193... | collective-permute-start | bytes 258056 | tf_op jit(solution)/shard_map/ppermute | solution.py:18
  55.3 1.5 collective-permute-start.30
  58.3 2.3 %collective-permute-start.5 = (bf16[2,32,896]{2,1,0:T(8,128)(2,1)S(1)}, bf16[2,32,896]{2,1,0:T(8,128)(2,1)S(1)}, u32[]{:S(2)}, u32[]{:S(2)}) collective-permute-start(bf16[2,32,896]{2,1,0:T(8,128)(2,1)S(1)} %copy-done.8), channel_id=1, source_target_pairs={{1,0},{2,1},{3,2},{4,3},{5,4},{6,5},{7,6},{0,7},{9,8},{10,9},{11,1... | collective-permute-start | bytes 344072 | tf_op jit(solution)/shard_map/ppermute | solution.py:18
  60.6 1.7 %collective-permute-done.31 = bf16[112,384]{1,0:T(8,128)(2,1)S(1)} collective-permute-done((bf16[112,384]{1,0:T(8,128)(2,1)S(1)}, bf16[112,384]{1,0:T(8,128)(2,1)S(1)}, u32[]{:S(2)}, u32[]{:S(2)}) %collective-permute-start.31) | collective-permute-done | bytes 86048 | tf_op jit(solution)/shard_map/ppermute | solution.py:18
  62.3 1.6 %collective-permute-start.10 = (bf16[2,32,896]{2,1,0:T(8,128)(2,1)S(1)}, bf16[2,32,896]{2,1,0:T(8,128)(2,1)S(1)}, u32[]{:S(2)}, u32[]{:S(2)}) collective-permute-start(bf16[2,32,896]{2,1,0:T(8,128)(2,1)S(1)} %copy-done.8), channel_id=1, source_target_pairs={{16,0},{0,16},{17,1},{1,17},{18,2},{2,18},{19,3},{3,19},{20,4},{4,... | collective-permute-start | bytes 344072 | tf_op jit(solution)/shard_map/ppermute | solution.py:18
  64.0 1.3 collective-permute-start.14
  65.8 3.2 %collective-permute-start.11 = (bf16[2,32,896]{2,1,0:T(8,128)(2,1)S(1)}, bf16[2,32,896]{2,1,0:T(8,128)(2,1)S(1)}, u32[]{:S(2)}, u32[]{:S(2)}) collective-permute-start(bf16[2,32,896]{2,1,0:T(8,128)(2,1)S(1)} %collective-permute-done.5.refs_3_), channel_id=1, source_target_pairs={{16,0},{0,16},{17,1},{1,17},{18,2},{2,18},{19,3},{3,19},{20,4},{4,... | collective-permute-start | bytes 344072 | tf_op jit(solution)/shard_map/ppermute | solution.py:18
  69.7 2.2 %collective-permute-start.32 = (bf16[4,112,384]{2,1,0:T(8,128)(2,1)S(1)}, bf16[4,112,384]{2,1,0:T(8,128)(2,1)S(1)}, u32[]{:S(2)}, u32[]{:S(2)}) collective-permute-start(bf16[4,112,384]{2,1,0:T(8,128)(2,1)S(1)} %pad_maximum_fusion.refs_20_), channel_id=1, source_target_pairs={{32,0},{0,32},{33,1},{1,33},{34,2},{2,34},{35,3},{3,35},{36,4},{4,... | collective-permute-start | bytes 1032200 | tf_op jit(solution)/shard_map/ppermute | solution.py:18
  72.6 1.6 %collective-permute-start.26 = (bf16[2,112,640]{2,1,0:T(8,128)(2,1)S(1)}, bf16[2,112,640]{2,1,0:T(8,128)(2,1)S(1)}, u32[]{:S(2)}, u32[]{:S(2)}) collective-permute-start(bf16[2,112,640]{2,1,0:T(8,128)(2,1)S(1)} %pad_maximum_fusion.1.refs_16_), channel_id=1, source_target_pairs={{64,0},{128,64},{192,128},{0,192},{65,1},{129,65},{193,129},{1,193... | collective-permute-start | bytes 860168 | tf_op jit(solution)/shard_map/ppermute | solution.py:18
  76.2 4.1 %collective-permute-done.32.refs_21_ = bf16[4,112,384]{2,1,0:T(8,128)(2,1)S(1)} collective-permute-done((bf16[4,112,384]{2,1,0:T(8,128)(2,1)S(1)}, bf16[4,112,384]{2,1,0:T(8,128)(2,1)S(1)}, u32[]{:S(2)}, u32[]{:S(2)}) %collective-permute-start.32) | collective-permute-done | bytes 344096 | tf_op jit(solution)/shard_map/ppermute | solution.py:18
  81.1 2.8 %collective-permute-done.27.refs_18_ = bf16[2,112,640]{2,1,0:T(8,128)(2,1)} collective-permute-done((bf16[2,112,640]{2,1,0:T(8,128)(2,1)S(1)}, bf16[2,112,640]{2,1,0:T(8,128)(2,1)}, u32[]{:S(2)}, u32[]{:S(2)}) %collective-permute-start.27) | collective-permute-done | bytes 286752 | tf_op jit(solution)/shard_map/ppermute | solution.py:18
  83.9 7.5 %collective-permute-done.28.refs_19_ = bf16[2,112,640]{2,1,0:T(8,128)(2,1)} collective-permute-done((bf16[2,112,640]{2,1,0:T(8,128)(2,1)S(1)}, bf16[2,112,640]{2,1,0:T(8,128)(2,1)}, u32[]{:S(2)}, u32[]{:S(2)}) %collective-permute-start.28) | collective-permute-done | bytes 286752 | tf_op jit(solution)/shard_map/ppermute | solution.py:18
  91.4 1.0 copy-done.4
  92.4 0.9 copy-done.6
  93.3 0.9 copy-done.9
  94.2 0.9 copy-done.11
  95.1 0.9 copy-done.13
  96.0 0.9 copy-done.15
  96.9 0.9 copy-done.17
  99.6 7.1 %shard_map.58 = (bf16[2,112,512]{2,1,0:T(8,128)(2,1)S(1)}, bf16[2,112,512]{2,1,0:T(8,128)(2,1)S(1)}, bf16[2,112,512]{2,1,0:T(8,128)(2,1)S(1)}, bf16[2,112,512]{2...) custom-call(s32[4]{0:T(128)S(1)} %pad_add_fusion.place, ...), custom_call_target="tpu_custom_call" | custom-call | flops 3758096384 | bytes 7602192 | tf_op jit(solution)/shard_map/pallas_call | solution.py:40
  106.8 2.7 %collective-permute-start.35 = (bf16[2,112,512]{2,1,0:T(8,128)(2,1)S(1)}, bf16[2,112,512]{2,1,0:T(8,128)(2,1)S(1)}, u32[]{:S(2)}, u32[]{:S(2)}) collective-permute-start(bf16[2,112,512]{2,1,0:T(8,128)(2,1)S(1)} %get-tuple-element.25), channel_id=1, source_target_pairs={{0,192},{64,0},{128,64},{192,128},{1,193},{65,1},{129,65},{193,129... | collective-permute-start | bytes 688136 | tf_op jit(solution)/shard_map/ppermute | solution.py:23
  109.4 1.0 collective-permute-start.38
  110.4 9.1 %collective-permute-done.34 = bf16[2,112,512]{2,1,0:T(8,128)(2,1)S(1)} collective-permute-done((bf16[2,112,512]{2,1,0:T(8,128)(2,1)S(1)}, bf16[2,112,512]{2,1,0:T(8,128)(2,1)S(1)}, u32[]{:S(2)}, u32[]{:S(2)}) %collective-permute-start.34) | collective-permute-done | bytes 229408 | tf_op jit(solution)/shard_map/ppermute | solution.py:23
  119.7 1.1 collective-permute-start.37
  120.7 1.2 collective-permute-done.38
  122.7 2.1 %collective-permute-start.40 = (bf16[112,512]{1,0:T(8,128)(2,1)S(1)}, bf16[112,512]{1,0:T(8,128)(2,1)S(1)}, u32[]{:S(2)}, u32[]{:S(2)}) collective-permute-start(bf16[112,512]{1,0:T(8,128)(2,1)S(1)} %get-tuple-element.30), channel_id=1, source_target_pairs={{0,192},{64,0},{128,64},{192,128},{1,193},{65,1},{129,65},{193,129... | collective-permute-start | bytes 344072 | tf_op jit(solution)/shard_map/ppermute | solution.py:23
  124.8 1.5 collective-permute-start.41
  127.8 2.8 %collective-permute-done.41.refs_5_ = bf16[112,512]{1,0:T(8,128)(2,1)S(1)} collective-permute-done((bf16[112,512]{1,0:T(8,128)(2,1)S(1)}, bf16[112,512]{1,0:T(8,128)(2,1)S(1)}, u32[]{:S(2)}, u32[]{:S(2)}) %collective-permute-start.41) | collective-permute-done | bytes 114720 | tf_op jit(solution)/shard_map/ppermute | solution.py:23
  130.5 1.3 shard_map.59
  131.8 4.7 %all-to-all-start.1 = ((bf16[16,56,224]{2,1,0:T(8,128)(2,1)}), bf16[16,56,224]{2,1,0:T(8,128)(2,1)S(1)}, u32[]{:S(2)}, u32[]{:S(2)}) async-start(bf16[16,56,224]{2,1,0:T(8,128)(2,1)} %shard_map.59), calls=%async_computation.1 | async-start | bytes 917504 | tf_op jit(solution)/shard_map/all_to_all | solution.py:291
  137.4 9.2 %all-to-all-done.1 = bf16[16,56,224]{2,1,0:T(8,128)(2,1)S(1)} async-done(((bf16[16,56,224]{2,1,0:T(8,128)(2,1)}), bf16[16,56,224]{2,1,0:T(8,128)(2,1)S(1)}, u32[]{:S(2)}, u32[]{:S(2)}) %all-to-all-start.1) | async-done | bytes 401440 | tf_op jit(solution)/shard_map/all_to_all | solution.py:291
  147.2 5.4 %collective-permute-start.42 = (f32[56,112]{1,0:T(8,128)S(1)}, f32[56,112]{1,0:T(8,128)S(1)}, u32[]{:S(2)}, u32[]{:S(2)}) collective-permute-start(f32[56,112]{1,0:T(8,128)S(1)} %select_n.67), channel_id=1, source_target_pairs={{16,0},{0,16},{17,1},{1,17},{18,2},{2,18},{19,3},{3,19},{20,4},{4,... | collective-permute-start | bytes 75272 | tf_op jit(solution)/shard_map/ppermute | solution.py:18
  (115 shorter events, 20.8 us)
Async XLA Ops:
  0.0 4.3 %collective-permute-start.16 = (bf16[56,4,56]{2,1,0:T(4,128)(2,1)}, bf16[56,4,56]{2,1,0:T(4,128)(2,1)S(1)}, u32[]{:S(2)}, u32[]{:S(2)}) collective-permute-start(bf16[56,4,56]{2,1,0:T(4,128)(2,1)} %own.1), channel_id=1, source_target_pairs={{16,0},{0,16},{17,1},{1,17},{18,2},{2,18},{19,3},{3,19},{20,4},{4,... | collective-permute-start | bytes 75272 | tf_op jit(solution)/shard_map/ppermute | solution.py:18
  5.1 22.8 %copy-start.2 = (f32[512,1,512]{2,1,0:T(1,128)S(1)}, f32[512,1,512]{2,1,0:T(1,128)}, u32[]{:S(2)}) copy-start(f32[512,1,512]{2,1,0:T(1,128)} %param.7) | copy-start | bytes 3145732
  6.1 7.7 %copy-start.22 = (bf16[32,896]{1,0:T(8,128)(2,1)S(1)}, bf16[32,896]{1,0:T(8,128)(2,1)}, u32[]{:S(2)}) copy-start(bf16[32,896]{1,0:T(8,128)(2,1)} %param.6) | copy-start | bytes 172036
  6.1 46.8 %all-to-all-start = ((bf16[16,56,224]{2,1,0:T(8,128)(2,1)}), bf16[16,56,224]{2,1,0:T(8,128)(2,1)S(1)}, u32[]{:S(2)}, u32[]{:S(2)}) async-start(bf16[16,56,224]{2,1,0:T(8,128)(2,1)} %shard_map.55), calls=%async_computation | async-start | bytes 917504 | tf_op jit(solution)/shard_map/all_to_all | solution.py:251
  13.9 4.1 %collective-permute-start = (bf16[1,32,896]{2,1,0:T(8,128)(2,1)S(1)}, bf16[1,32,896]{2,1,0:T(8,128)(2,1)S(1)}, u32[]{:S(2)}, u32[]{:S(2)}) collective-permute-start(bf16[1,32,896]{2,1,0:T(8,128)(2,1)S(1)} %bitcast.49), channel_id=1, source_target_pairs={{8,0},{0,8},{9,1},{1,9},{10,2},{2,10},{11,3},{3,11},{12,4},{4,12},... | collective-permute-start | bytes 172040 | tf_op jit(solution)/shard_map/ppermute | solution.py:18
  15.3 5.6 %collective-permute-start.17 = (bf16[1,32,896]{2,1,0:T(8,128)(2,1)S(1)}, bf16[1,32,896]{2,1,0:T(8,128)(2,1)S(1)}, u32[]{:S(2)}, u32[]{:S(2)}) collective-permute-start(bf16[1,32,896]{2,1,0:T(8,128)(2,1)S(1)} %bitcast.50), channel_id=1, source_target_pairs={{32,0},{0,32},{33,1},{1,33},{34,2},{2,34},{35,3},{3,35},{36,4},{4,... | collective-permute-start | bytes 172040 | tf_op jit(solution)/shard_map/ppermute | solution.py:18
  20.9 9.2 %collective-permute-start.18 = (bf16[2,32,896]{2,1,0:T(8,128)(2,1)S(1)}, bf16[2,32,896]{2,1,0:T(8,128)(2,1)S(1)}, u32[]{:S(2)}, u32[]{:S(2)}) collective-permute-start(bf16[2,32,896]{2,1,0:T(8,128)(2,1)S(1)} %get-tuple-element.39.refs_0_), channel_id=1, source_target_pairs={{64,0},{128,64},{192,128},{0,192},{65,1},{129,65},{193,129},{1,193... | collective-permute-start | bytes 344072 | tf_op jit(solution)/shard_map/ppermute | solution.py:18
  23.5 7.2 %collective-permute-start.19 = (bf16[2,32,896]{2,1,0:T(8,128)(2,1)S(1)}, bf16[2,32,896]{2,1,0:T(8,128)(2,1)S(1)}, u32[]{:S(2)}, u32[]{:S(2)}) collective-permute-start(bf16[2,32,896]{2,1,0:T(8,128)(2,1)S(1)} %get-tuple-element.39.refs_0_), channel_id=1, source_target_pairs={{128,0},{192,64},{0,128},{64,192},{129,1},{193,65},{1,129},{65,193... | collective-permute-start | bytes 344072 | tf_op jit(solution)/shard_map/ppermute | solution.py:18
  24.0 7.8 %collective-permute-start.1 = (bf16[2,32,896]{2,1,0:T(8,128)(2,1)S(1)}, bf16[2,32,896]{2,1,0:T(8,128)(2,1)}, u32[]{:S(2)}, u32[]{:S(2)}) collective-permute-start(bf16[2,32,896]{2,1,0:T(8,128)(2,1)S(1)} %get-tuple-element.40.refs_0_), channel_id=1, source_target_pairs={{1,0},{2,1},{3,2},{4,3},{5,4},{6,5},{7,6},{0,7},{9,8},{10,9},{11,1... | collective-permute-start | bytes 344072 | tf_op jit(solution)/shard_map/ppermute | solution.py:18
  27.9 10.2 %collective-permute-start.2 = (bf16[2,32,896]{2,1,0:T(8,128)(2,1)S(1)}, bf16[2,32,896]{2,1,0:T(8,128)(2,1)}, u32[]{:S(2)}, u32[]{:S(2)}) collective-permute-start(bf16[2,32,896]{2,1,0:T(8,128)(2,1)S(1)} %get-tuple-element.40.refs_0_), channel_id=1, source_target_pairs={{7,0},{0,1},{1,2},{2,3},{3,4},{4,5},{5,6},{6,7},{15,8},{8,9},{9,10... | collective-permute-start | bytes 344072 | tf_op jit(solution)/shard_map/ppermute | solution.py:18
  27.9 48.4 %collective-permute-start.33 = (f32[2048,128]{1,0:T(8,128)S(1)}, f32[2048,128]{1,0:T(8,128)}, u32[]{:S(2)}, u32[]{:S(2)}) collective-permute-start(f32[2048,128]{1,0:T(8,128)S(1)} %bitcast.39), channel_id=1, source_target_pairs={{16,0},{0,16},{17,1},{1,17},{18,2},{2,18},{19,3},{3,19},{20,4},{4,... | collective-permute-start | bytes 3145736 | tf_op jit(solution)/shard_map/ppermute | solution.py:18
  30.1 8.3 %collective-permute-start.20 = (bf16[2,32,896]{2,1,0:T(8,128)(2,1)S(1)}, bf16[2,32,896]{2,1,0:T(8,128)(2,1)S(1)}, u32[]{:S(2)}, u32[]{:S(2)}) collective-permute-start(bf16[2,32,896]{2,1,0:T(8,128)(2,1)S(1)} %get-tuple-element.39.refs_0_), channel_id=1, source_target_pairs={{192,0},{0,64},{64,128},{128,192},{193,1},{1,65},{65,129},{129,193... | collective-permute-start | bytes 344072 | tf_op jit(solution)/shard_map/ppermute | solution.py:18
  30.7 7.9 %collective-permute-start.21 = (bf16[2,32,896]{2,1,0:T(8,128)(2,1)S(1)}, bf16[2,32,896]{2,1,0:T(8,128)(2,1)S(1)}, u32[]{:S(2)}, u32[]{:S(2)}) collective-permute-start(bf16[2,32,896]{2,1,0:T(8,128)(2,1)S(1)} %get-tuple-element.39.refs_0_), channel_id=1, source_target_pairs={{16,0},{0,16},{17,1},{1,17},{18,2},{2,18},{19,3},{3,19},{20,4},{4,... | collective-permute-start | bytes 344072 | tf_op jit(solution)/shard_map/ppermute | solution.py:18
  31.8 9.5 %collective-permute-start.6 = (bf16[2,32,896]{2,1,0:T(8,128)(2,1)S(1)}, bf16[2,32,896]{2,1,0:T(8,128)(2,1)}, u32[]{:S(2)}, u32[]{:S(2)}) collective-permute-start(bf16[2,32,896]{2,1,0:T(8,128)(2,1)S(1)} %get-tuple-element.40.refs_0_), channel_id=1, source_target_pairs={{4,0},{5,1},{6,2},{7,3},{0,4},{1,5},{2,6},{3,7},{12,8},{13,9},{14,... | collective-permute-start | bytes 344072 | tf_op jit(solution)/shard_map/ppermute | solution.py:18
  38.1 5.9 %collective-permute-start.8 = (bf16[2,32,896]{2,1,0:T(8,128)(2,1)S(1)}, bf16[2,32,896]{2,1,0:T(8,128)(2,1)S(1)}, u32[]{:S(2)}, u32[]{:S(2)}) collective-permute-start(bf16[2,32,896]{2,1,0:T(8,128)(2,1)S(1)} %get-tuple-element.40.refs_0_), channel_id=1, source_target_pairs={{16,0},{0,16},{17,1},{1,17},{18,2},{2,18},{19,3},{3,19},{20,4},{4,... | collective-permute-start | bytes 344072 | tf_op jit(solution)/shard_map/ppermute | solution.py:18
  38.4 8.8 %collective-permute-start.22 = (bf16[2,32,896]{2,1,0:T(8,128)(2,1)S(1)}, bf16[2,32,896]{2,1,0:T(8,128)(2,1)S(1)}, u32[]{:S(2)}, u32[]{:S(2)}) collective-permute-start(bf16[2,32,896]{2,1,0:T(8,128)(2,1)S(1)} %collective-permute-done.18.refs_1_), channel_id=1, source_target_pairs={{16,0},{0,16},{17,1},{1,17},{18,2},{2,18},{19,3},{3,19},{20,4},{4,... | collective-permute-start | bytes 344072 | tf_op jit(solution)/shard_map/ppermute | solution.py:18
  38.6 9.3 %collective-permute-start.23 = (bf16[2,32,896]{2,1,0:T(8,128)(2,1)S(1)}, bf16[2,32,896]{2,1,0:T(8,128)(2,1)S(1)}, u32[]{:S(2)}, u32[]{:S(2)}) collective-permute-start(bf16[2,32,896]{2,1,0:T(8,128)(2,1)S(1)} %collective-permute-done.19.refs_2_), channel_id=1, source_target_pairs={{16,0},{0,16},{17,1},{1,17},{18,2},{2,18},{19,3},{3,19},{20,4},{4,... | collective-permute-start | bytes 344072 | tf_op jit(solution)/shard_map/ppermute | solution.py:18
  41.3 6.8 %collective-permute-start.24 = (bf16[2,32,896]{2,1,0:T(8,128)(2,1)S(1)}, bf16[2,32,896]{2,1,0:T(8,128)(2,1)S(1)}, u32[]{:S(2)}, u32[]{:S(2)}) collective-permute-start(bf16[2,32,896]{2,1,0:T(8,128)(2,1)S(1)} %collective-permute-done.20.refs_3_), channel_id=1, source_target_pairs={{16,0},{0,16},{17,1},{1,17},{18,2},{2,18},{19,3},{3,19},{20,4},{4,... | collective-permute-start | bytes 344072 | tf_op jit(solution)/shard_map/ppermute | solution.py:18
  44.5 7.0 %collective-permute-start.3 = (bf16[2,32,896]{2,1,0:T(8,128)(2,1)}, bf16[2,32,896]{2,1,0:T(8,128)(2,1)S(1)}, u32[]{:S(2)}, u32[]{:S(2)}) collective-permute-start(bf16[2,32,896]{2,1,0:T(8,128)(2,1)} %collective-permute-done.1.refs_1_), channel_id=1, source_target_pairs={{1,0},{2,1},{3,2},{4,3},{5,4},{6,5},{7,6},{0,7},{9,8},{10,9},{11,1... | collective-permute-start | bytes 344072 | tf_op jit(solution)/shard_map/ppermute | solution.py:18
  47.2 6.2 %collective-permute-start.4 = (bf16[2,32,896]{2,1,0:T(8,128)(2,1)}, bf16[2,32,896]{2,1,0:T(8,128)(2,1)}, u32[]{:S(2)}, u32[]{:S(2)}) collective-permute-start(bf16[2,32,896]{2,1,0:T(8,128)(2,1)} %collective-permute-done.2.refs_7_), channel_id=1, source_target_pairs={{7,0},{0,1},{1,2},{2,3},{3,4},{4,5},{5,6},{6,7},{15,8},{8,9},{9,10... | collective-permute-start | bytes 344072 | tf_op jit(solution)/shard_map/ppermute | solution.py:18
  47.8 7.5 %collective-permute-start.15 = (bf16[2,32,896]{2,1,0:T(8,128)(2,1)}, bf16[2,32,896]{2,1,0:T(8,128)(2,1)}, u32[]{:S(2)}, u32[]{:S(2)}) collective-permute-start(bf16[2,32,896]{2,1,0:T(8,128)(2,1)} %collective-permute-done.2.refs_7_), channel_id=1, source_target_pairs={{16,0},{0,16},{17,1},{1,17},{18,2},{2,18},{19,3},{3,19},{20,4},{4,... | collective-permute-start | bytes 344072 | tf_op jit(solution)/shard_map/ppermute | solution.py:18
  48.1 8.7 %collective-permute-start.9 = (bf16[2,32,896]{2,1,0:T(8,128)(2,1)}, bf16[2,32,896]{2,1,0:T(8,128)(2,1)}, u32[]{:S(2)}, u32[]{:S(2)}) collective-permute-start(bf16[2,32,896]{2,1,0:T(8,128)(2,1)} %collective-permute-done.1.refs_1_), channel_id=1, source_target_pairs={{16,0},{0,16},{17,1},{1,17},{18,2},{2,18},{19,3},{3,19},{20,4},{4,... | collective-permute-start | bytes 344072 | tf_op jit(solution)/shard_map/ppermute | solution.py:18
  51.6 6.1 %collective-permute-start.12 = (bf16[2,32,896]{2,1,0:T(8,128)(2,1)}, bf16[2,32,896]{2,1,0:T(8,128)(2,1)}, u32[]{:S(2)}, u32[]{:S(2)}) collective-permute-start(bf16[2,32,896]{2,1,0:T(8,128)(2,1)} %collective-permute-done.6.refs_4_), channel_id=1, source_target_pairs={{16,0},{0,16},{17,1},{1,17},{18,2},{2,18},{19,3},{3,19},{20,4},{4,... | collective-permute-start | bytes 344072 | tf_op jit(solution)/shard_map/ppermute | solution.py:18
  53.4 4.9 %collective-permute-start.29 = (bf16[112,384]{1,0:T(8,128)(2,1)S(1)}, bf16[112,384]{1,0:T(8,128)(2,1)S(1)}, u32[]{:S(2)}, u32[]{:S(2)}) collective-permute-start(bf16[112,384]{1,0:T(8,128)(2,1)S(1)} %get-tuple-element.22), channel_id=1, source_target_pairs={{64,0},{128,64},{192,128},{0,192},{65,1},{129,65},{193,129},{1,193... | collective-permute-start | bytes 258056 | tf_op jit(solution)/shard_map/ppermute | solution.py:18
  55.3 5.3 %collective-permute-start.30 = (bf16[112,384]{1,0:T(8,128)(2,1)S(1)}, bf16[112,384]{1,0:T(8,128)(2,1)S(1)}, u32[]{:S(2)}, u32[]{:S(2)}) collective-permute-start(bf16[112,384]{1,0:T(8,128)(2,1)S(1)} %get-tuple-element.22), channel_id=1, source_target_pairs={{128,0},{192,64},{0,128},{64,192},{129,1},{193,65},{1,129},{65,193... | collective-permute-start | bytes 258056 | tf_op jit(solution)/shard_map/ppermute | solution.py:18
  56.8 5.5 %collective-permute-start.31 = (bf16[112,384]{1,0:T(8,128)(2,1)S(1)}, bf16[112,384]{1,0:T(8,128)(2,1)S(1)}, u32[]{:S(2)}, u32[]{:S(2)}) collective-permute-start(bf16[112,384]{1,0:T(8,128)(2,1)S(1)} %get-tuple-element.22), channel_id=1, source_target_pairs={{192,0},{0,64},{64,128},{128,192},{193,1},{1,65},{65,129},{129,193... | collective-permute-start | bytes 258056 | tf_op jit(solution)/shard_map/ppermute | solution.py:18
  57.7 12.1 %collective-permute-start.25 = (bf16[112,640]{1,0:T(8,128)(2,1)S(1)}, bf16[112,640]{1,0:T(8,128)(2,1)S(1)}, u32[]{:S(2)}, u32[]{:S(2)}) collective-permute-start(bf16[112,640]{1,0:T(8,128)(2,1)S(1)} %get-tuple-element.21), channel_id=1, source_target_pairs={{32,0},{0,32},{33,1},{1,33},{34,2},{2,34},{35,3},{3,35},{36,4},{4,... | collective-permute-start | bytes 430088 | tf_op jit(solution)/shard_map/ppermute | solution.py:18
  58.3 5.7 %collective-permute-start.5 = (bf16[2,32,896]{2,1,0:T(8,128)(2,1)S(1)}, bf16[2,32,896]{2,1,0:T(8,128)(2,1)S(1)}, u32[]{:S(2)}, u32[]{:S(2)}) collective-permute-start(bf16[2,32,896]{2,1,0:T(8,128)(2,1)S(1)} %copy-done.8), channel_id=1, source_target_pairs={{1,0},{2,1},{3,2},{4,3},{5,4},{6,5},{7,6},{0,7},{9,8},{10,9},{11,1... | collective-permute-start | bytes 344072 | tf_op jit(solution)/shard_map/ppermute | solution.py:18
  60.6 5.2 %collective-permute-start.7 = (bf16[2,32,896]{2,1,0:T(8,128)(2,1)}, bf16[2,32,896]{2,1,0:T(8,128)(2,1)S(1)}, u32[]{:S(2)}, u32[]{:S(2)}) collective-permute-start(bf16[2,32,896]{2,1,0:T(8,128)(2,1)} %collective-permute-done.4.refs_6_), channel_id=1, source_target_pairs={{7,0},{0,1},{1,2},{2,3},{3,4},{4,5},{5,6},{6,7},{15,8},{8,9},{9,10... | collective-permute-start | bytes 344072 | tf_op jit(solution)/shard_map/ppermute | solution.py:18
  62.3 6.7 %collective-permute-start.10 = (bf16[2,32,896]{2,1,0:T(8,128)(2,1)S(1)}, bf16[2,32,896]{2,1,0:T(8,128)(2,1)S(1)}, u32[]{:S(2)}, u32[]{:S(2)}) collective-permute-start(bf16[2,32,896]{2,1,0:T(8,128)(2,1)S(1)} %copy-done.8), channel_id=1, source_target_pairs={{16,0},{0,16},{17,1},{1,17},{18,2},{2,18},{19,3},{3,19},{20,4},{4,... | collective-permute-start | bytes 344072 | tf_op jit(solution)/shard_map/ppermute | solution.py:18
  64.0 8.0 %copy-start.10 = (bf16[2,32,896]{2,1,0:T(8,128)(2,1)}, bf16[2,32,896]{2,1,0:T(8,128)(2,1)S(1)}, u32[]{:S(2)}) copy-start(bf16[2,32,896]{2,1,0:T(8,128)(2,1)S(1)} %collective-permute-done.5.refs_3_) | copy-start | bytes 344068
  64.0 8.0 %collective-permute-start.14 = (bf16[2,32,896]{2,1,0:T(8,128)(2,1)}, bf16[2,32,896]{2,1,0:T(8,128)(2,1)S(1)}, u32[]{:S(2)}, u32[]{:S(2)}) collective-permute-start(bf16[2,32,896]{2,1,0:T(8,128)(2,1)} %collective-permute-done.4.refs_6_), channel_id=1, source_target_pairs={{16,0},{0,16},{17,1},{1,17},{18,2},{2,18},{19,3},{3,19},{20,4},{4,... | collective-permute-start | bytes 344072 | tf_op jit(solution)/shard_map/ppermute | solution.py:18
  65.8 8.4 %collective-permute-start.11 = (bf16[2,32,896]{2,1,0:T(8,128)(2,1)S(1)}, bf16[2,32,896]{2,1,0:T(8,128)(2,1)S(1)}, u32[]{:S(2)}, u32[]{:S(2)}) collective-permute-start(bf16[2,32,896]{2,1,0:T(8,128)(2,1)S(1)} %collective-permute-done.5.refs_3_), channel_id=1, source_target_pairs={{16,0},{0,16},{17,1},{1,17},{18,2},{2,18},{19,3},{3,19},{20,4},{4,... | collective-permute-start | bytes 344072 | tf_op jit(solution)/shard_map/ppermute | solution.py:18
  69.7 5.7 %collective-permute-start.13 = (bf16[2,32,896]{2,1,0:T(8,128)(2,1)S(1)}, bf16[2,32,896]{2,1,0:T(8,128)(2,1)S(1)}, u32[]{:S(2)}, u32[]{:S(2)}) collective-permute-start(bf16[2,32,896]{2,1,0:T(8,128)(2,1)S(1)} %collective-permute-done.7.refs_5_), channel_id=1, source_target_pairs={{16,0},{0,16},{17,1},{1,17},{18,2},{2,18},{19,3},{3,19},{20,4},{4,... | collective-permute-start | bytes 344072 | tf_op jit(solution)/shard_map/ppermute | solution.py:18
  69.7 10.6 %collective-permute-start.32 = (bf16[4,112,384]{2,1,0:T(8,128)(2,1)S(1)}, bf16[4,112,384]{2,1,0:T(8,128)(2,1)S(1)}, u32[]{:S(2)}, u32[]{:S(2)}) collective-permute-start(bf16[4,112,384]{2,1,0:T(8,128)(2,1)S(1)} %pad_maximum_fusion.refs_20_), channel_id=1, source_target_pairs={{32,0},{0,32},{33,1},{1,33},{34,2},{2,34},{35,3},{3,35},{36,4},{4,... | collective-permute-start | bytes 1032200 | tf_op jit(solution)/shard_map/ppermute | solution.py:18
  72.6 7.8 %collective-permute-start.26 = (bf16[2,112,640]{2,1,0:T(8,128)(2,1)S(1)}, bf16[2,112,640]{2,1,0:T(8,128)(2,1)S(1)}, u32[]{:S(2)}, u32[]{:S(2)}) collective-permute-start(bf16[2,112,640]{2,1,0:T(8,128)(2,1)S(1)} %pad_maximum_fusion.1.refs_16_), channel_id=1, source_target_pairs={{64,0},{128,64},{192,128},{0,192},{65,1},{129,65},{193,129},{1,193... | collective-permute-start | bytes 860168 | tf_op jit(solution)/shard_map/ppermute | solution.py:18
  74.9 9.0 %collective-permute-start.27 = (bf16[2,112,640]{2,1,0:T(8,128)(2,1)S(1)}, bf16[2,112,640]{2,1,0:T(8,128)(2,1)}, u32[]{:S(2)}, u32[]{:S(2)}) collective-permute-start(bf16[2,112,640]{2,1,0:T(8,128)(2,1)S(1)} %pad_maximum_fusion.1.refs_16_), channel_id=1, source_target_pairs={{128,0},{192,64},{0,128},{64,192},{129,1},{193,65},{1,129},{65,193... | collective-permute-start | bytes 860168 | tf_op jit(solution)/shard_map/ppermute | solution.py:18
  76.1 15.4 %collective-permute-start.28 = (bf16[2,112,640]{2,1,0:T(8,128)(2,1)S(1)}, bf16[2,112,640]{2,1,0:T(8,128)(2,1)}, u32[]{:S(2)}, u32[]{:S(2)}) collective-permute-start(bf16[2,112,640]{2,1,0:T(8,128)(2,1)S(1)} %pad_maximum_fusion.1.refs_16_), channel_id=1, source_target_pairs={{192,0},{0,64},{64,128},{128,192},{193,1},{1,65},{65,129},{129,193... | collective-permute-start | bytes 860168 | tf_op jit(solution)/shard_map/ppermute | solution.py:18
  106.7 12.9 %collective-permute-start.34 = (bf16[2,112,512]{2,1,0:T(8,128)(2,1)S(1)}, bf16[2,112,512]{2,1,0:T(8,128)(2,1)S(1)}, u32[]{:S(2)}, u32[]{:S(2)}) collective-permute-start(bf16[2,112,512]{2,1,0:T(8,128)(2,1)S(1)} %get-tuple-element.24), channel_id=1, source_target_pairs={{0,64},{64,128},{128,192},{192,0},{1,65},{65,129},{129,193},{193,1... | collective-permute-start | bytes 688136 | tf_op jit(solution)/shard_map/ppermute | solution.py:23
  106.8 12.8 %collective-permute-start.35 = (bf16[2,112,512]{2,1,0:T(8,128)(2,1)S(1)}, bf16[2,112,512]{2,1,0:T(8,128)(2,1)S(1)}, u32[]{:S(2)}, u32[]{:S(2)}) collective-permute-start(bf16[2,112,512]{2,1,0:T(8,128)(2,1)S(1)} %get-tuple-element.25), channel_id=1, source_target_pairs={{0,192},{64,0},{128,64},{192,128},{1,193},{65,1},{129,65},{193,129... | collective-permute-start | bytes 688136 | tf_op jit(solution)/shard_map/ppermute | solution.py:23
  109.4 10.1 %collective-permute-start.36 = (bf16[2,112,512]{2,1,0:T(8,128)(2,1)S(1)}, bf16[2,112,512]{2,1,0:T(8,128)(2,1)S(1)}, u32[]{:S(2)}, u32[]{:S(2)}) collective-permute-start(bf16[2,112,512]{2,1,0:T(8,128)(2,1)S(1)} %get-tuple-element.26), channel_id=1, source_target_pairs={{0,128},{64,192},{128,0},{192,64},{1,129},{65,193},{129,1},{193,65... | collective-permute-start | bytes 688136 | tf_op jit(solution)/shard_map/ppermute | solution.py:23
  109.4 12.5 %collective-permute-start.38 = (bf16[4,112,512]{2,1,0:T(8,128)(2,1)S(1)}, bf16[4,112,512]{2,1,0:T(8,128)(2,1)S(1)}, u32[]{:S(2)}, u32[]{:S(2)}) collective-permute-start(bf16[4,112,512]{2,1,0:T(8,128)(2,1)S(1)} %get-tuple-element.28), channel_id=1, source_target_pairs={{0,32},{32,0},{1,33},{33,1},{2,34},{34,2},{3,35},{35,3},{4,36},{36... | collective-permute-start | bytes 1376264 | tf_op jit(solution)/shard_map/ppermute | solution.py:23
  119.7 6.6 %collective-permute-start.37 = (bf16[112,512]{1,0:T(8,128)(2,1)S(1)}, bf16[112,512]{1,0:T(8,128)(2,1)S(1)}, u32[]{:S(2)}, u32[]{:S(2)}) collective-permute-start(bf16[112,512]{1,0:T(8,128)(2,1)S(1)} %get-tuple-element.33), channel_id=1, source_target_pairs={{0,32},{32,0},{1,33},{33,1},{2,34},{34,2},{3,35},{35,3},{4,36},{36... | collective-permute-start | bytes 344072 | tf_op jit(solution)/shard_map/ppermute | solution.py:23
  122.1 4.9 %collective-permute-start.39 = (bf16[112,512]{1,0:T(8,128)(2,1)S(1)}, bf16[112,512]{1,0:T(8,128)(2,1)S(1)}, u32[]{:S(2)}, u32[]{:S(2)}) collective-permute-start(bf16[112,512]{1,0:T(8,128)(2,1)S(1)} %get-tuple-element.31), channel_id=1, source_target_pairs={{0,64},{64,128},{128,192},{192,0},{1,65},{65,129},{129,193},{193,1... | collective-permute-start | bytes 344072 | tf_op jit(solution)/shard_map/ppermute | solution.py:23
  122.7 5.1 %collective-permute-start.40 = (bf16[112,512]{1,0:T(8,128)(2,1)S(1)}, bf16[112,512]{1,0:T(8,128)(2,1)S(1)}, u32[]{:S(2)}, u32[]{:S(2)}) collective-permute-start(bf16[112,512]{1,0:T(8,128)(2,1)S(1)} %get-tuple-element.30), channel_id=1, source_target_pairs={{0,192},{64,0},{128,64},{192,128},{1,193},{65,1},{129,65},{193,129... | collective-permute-start | bytes 344072 | tf_op jit(solution)/shard_map/ppermute | solution.py:23
  124.8 5.7 %collective-permute-start.41 = (bf16[112,512]{1,0:T(8,128)(2,1)S(1)}, bf16[112,512]{1,0:T(8,128)(2,1)S(1)}, u32[]{:S(2)}, u32[]{:S(2)}) collective-permute-start(bf16[112,512]{1,0:T(8,128)(2,1)S(1)} %get-tuple-element.29), channel_id=1, source_target_pairs={{0,128},{64,192},{128,0},{192,64},{1,129},{65,193},{129,1},{193,65... | collective-permute-start | bytes 344072 | tf_op jit(solution)/shard_map/ppermute | solution.py:23
  131.8 14.8 %all-to-all-start.1 = ((bf16[16,56,224]{2,1,0:T(8,128)(2,1)}), bf16[16,56,224]{2,1,0:T(8,128)(2,1)S(1)}, u32[]{:S(2)}, u32[]{:S(2)}) async-start(bf16[16,56,224]{2,1,0:T(8,128)(2,1)} %shard_map.59), calls=%async_computation.1 | async-start | bytes 917504 | tf_op jit(solution)/shard_map/all_to_all | solution.py:291
  147.2 6.2 %collective-permute-start.42 = (f32[56,112]{1,0:T(8,128)S(1)}, f32[56,112]{1,0:T(8,128)S(1)}, u32[]{:S(2)}, u32[]{:S(2)}) collective-permute-start(f32[56,112]{1,0:T(8,128)S(1)} %select_n.67), channel_id=1, source_target_pairs={{16,0},{0,16},{17,1},{1,17},{18,2},{2,18},{19,3},{3,19},{20,4},{4,... | collective-permute-start | bytes 75272 | tf_op jit(solution)/shard_map/ppermute | solution.py:18
  (21 other events, 31.3 us)

commit v5 on v4

--- a/solution.py
+++ b/solution.py
@@ -10,7 +10,7 @@
 GRP = ("y_lo", "z")
 BF16 = jnp.bfloat16
 F32 = jnp.float32
-FIRST_PART = 640
+FIRST_PART = 512
 
 
 def from_ahead(x, axis, offset):
@@ -131,9 +131,10 @@
 
 
 def weighed(place, pieces, right, z_own, z_other, half, n_z, n_l, n_x, n_h):
+    keys, pieces = [k for k, _ in pieces], [p for _, p in pieces]
     pts, nv = pieces[0].shape[1:]
     step = n_l * pts
-    total = step * len(pieces)
+    total = 2 * n_z * step
     n_q = (right[0].shape[2] + right[-1].shape[2]) // half
     cut = right[0].shape[2]
     lanes = z_own.shape[1]
@@ -158,16 +159,15 @@
             ox = (j // n_h + n_x - place[2]) % n_x
             oh = (j % n_h + n_h - place[3]) % n_h
             slots.append(ox * n_h + oh)
-        for i in range(0, count, 2):
-            block = jnp.concatenate(
-                [parts[i + j][...].reshape(step, nv) for j in range(2)], axis=0
-            )
-            rows[i * step : (i + 2) * step, :] = block
-            flipped = block.T
+        offsets = []
+        for key, part in zip(keys, parts):
+            at = len(offsets) * step
+            rows[at : at + len(key) * step, :] = part[...].reshape(len(key) * step, nv)
+            offsets += key
+        for i in range(0, total, 128):
+            flipped = rows[i : i + 128, :].T
             for j in range(n_plane):
-                turned[slots[j], :, i * step : (i + 2) * step] = flipped[
-                    j * share : (j + 1) * share
-                ]
+                turned[slots[j], :, i : i + 128] = flipped[j * share : (j + 1) * share]
         for ox in range(n_x):
             for oh in range(n_h):
                 at = ((place[2] + ox) % n_x) * n_h + (place[3] + oh) % n_h
@@ -187,14 +187,15 @@
                 right[k].reshape(nv, n_q),
                 preferred_element_type=F32,
             )
-            for core, z in enumerate((z_own, z_other)):
-                if k == 0:
-                    copies[core].wait()
-                for s in range(n_z * n_l):
-                    oz, ol = s // n_l, s % n_l
+            if k == 0:
+                for copy in copies:
+                    copy.wait()
+            for i, oz in enumerate(offsets):
+                z = z_own if i < n_z else z_other
+                for ol in range(n_l):
                     g = ((place[1] + ol) % n_l) * n_z + (place[0] + oz) % n_z
                     first = g * (pts * per_row)
-                    at = core * n_z * step + s * pts
+                    at = i * step + ol * pts
                     for j in range(per_row):
                         zs = z[pl.ds(first + j, pts, stride=per_row), :]
                         cols = slice(j * lanes, (j + 1) * lanes)
@@ -267,14 +268,15 @@
     own = {0: pair}
     own[1], own[n_z - 1] = from_ahead(pair, "z", 1), from_ahead(pair, "z", -1)
     own[n_z // 2] = from_ahead(pair, "z", n_z // 2)
-    for o in range(2, n_z // 2):
-        up, down = lax.optimization_barrier((own[o - 1], own[n_z - o + 1]))
-        own[o], own[n_z - o] = from_ahead(up, "z", 1), from_ahead(down, "z", -1)
-    own = [own[o] for o in range(n_z)]
-    others = []
-    for o in range(n_z):
-        others.append(from_ahead(own[o], "core", 1))
-    own += others
+    up = from_ahead(jnp.concatenate([pair, own[1]], axis=0), "z", 2)
+    down = from_ahead(jnp.concatenate([pair, own[n_z - 1]], axis=0), "z", -2)
+    pieces = {(0,): pair, (1,): own[1], (n_z - 1,): own[n_z - 1], (n_z // 2,): own[n_z // 2]}
+    order = [*pieces, (2, 3), (n_z - 2, n_z - 3)]
+    pieces = {**pieces, order[-2]: up, order[-1]: down}
+    others = {}
+    for key in order:
+        others[key] = from_ahead(pieces[key], "core", 1)
+    own = [(key, pieces[key]) for key in order] + [(key, others[key]) for key in order]
     z = metric.reshape(-1, 128)
     z_other = from_ahead(z, "core", 1)
     place = jnp.stack([my_z, my_l, my_x, my_h])

time: 156 us -> 150 us (0.962)
  local copies, waits for them, and re-layouts: 15.7 us -> 10.6 us
    unnamed x49 -> x29, local copies, waits for them, and re-layouts: 13.7 us -> 8.63 us
    ppermute x35 -> x31, starting transfers between devices: 55.4 us -> 51.8 us  [from_ahead(): return lax.ppermute(x, axis, [((i + offset) % n, i) for i in range(n)])]
    all_to_all x1, starting transfers between devices: 4.69 us -> 6.36 us  [local(): ladder = lax.all_to_all(ladder, GRP, 0, 0, tiled=True)]
    ppermute x35 -> x31, waiting for transfers between devices: 27.1 us -> 28.3 us  [from_ahead(): return lax.ppermute(x, axis, [((i + offset) % n, i) for i in range(n)])]
  transfers between devices with their start and end apart: 45 -> 41, of which waited for: 16 -> 17; matrix products, arithmetic and copies ran while one was open for 1% -> 2% of each run, Pallas kernels for 1% -> 1%
where the time goes in v5:
time: 150 us
  starting transfers between devices  76.1 us (51%)
  waiting for transfers between devices  50.2 us (33%)
  local copies, waits for them, and re-layouts  10.6 us (7%)
  Pallas kernels  10.6 us (7%)
  other arithmetic  1.84 us (1%)
    ppermute x31, starting transfers between devices, from_ahead(): return lax.ppermute(x, axis, [((i + offset) % n, i) for i in range(n)])  51.8 us
    ppermute x31, waiting for transfers between devices, from_ahead(): return lax.ppermute(x, axis, [((i + offset) % n, i) for i in range(n)])  28.3 us
    ppermute x8, waiting for transfers between devices, to_ahead(): return lax.ppermute(x, axis, [(i, (i + offset) % n) for i in range(n)])  13.2 us
    pallas_call x5, Pallas kernels, kernel_call(): pl.pallas_call(body, out_shape=outs, in_specs=[smem] + [pl.BlockSpec(memo...  10.6 us
    ppermute x8, starting transfers between devices, to_ahead(): return lax.ppermute(x, axis, [(i, (i + offset) % n) for i in range(n)])  10.2 us
    all_to_all x1, waiting for transfers between devices, local(): ladder = lax.all_to_all(ladder, GRP, 0, 0, tiled=True)  8.74 us
    unnamed x29, local copies, waits for them, and re-layouts  8.63 us
    all_to_all x1, starting transfers between devices, local(): turned = lax.all_to_all(turned, GRP, 0, 0, tiled=True)  7.73 us
  transfers between devices with their start and end apart: 41, of which 17 were waited for; matrix products, arithmetic and copies ran while one was open for 2% of the time, Pallas kernels for 1%

profile of v5, /device:TPU:1, one launch (start us, length us, event | category | flops | bytes accessed | tf_op | source)
XLA Modules:
  0.0 149.7 jit_solution(4831428964281994073)
XLA Ops:
  0.0 3.2 %collective-permute-start.12 = (bf16[56,4,56]{2,1,0:T(4,128)(2,1)}, bf16[56,4,56]{2,1,0:T(4,128)(2,1)S(1)}, u32[]{:S(2)}, u32[]{:S(2)}) collective-permute-start(bf16[56,4,56]{2,1,0:T(4,128)(2,1)} %own.1), channel_id=1, source_target_pairs={{16,0},{0,16},{17,1},{1,17},{18,2},{2,18},{19,3},{3,19},{20,4},{4,... | collective-permute-start | bytes 75272 | tf_op jit(solution)/shard_map/ppermute | solution.py:18
  3.2 1.1 collective-permute-done.12.other
  4.3 0.8 copy-done
  5.1 1.0 shard_map.55
  6.1 7.7 %all-to-all-start = ((bf16[16,56,224]{2,1,0:T(8,128)(2,1)}), bf16[16,56,224]{2,1,0:T(8,128)(2,1)S(1)}, u32[]{:S(2)}, u32[]{:S(2)}) async-start(bf16[16,56,224]{2,1,0:T(8,128)(2,1)} %shard_map.55), calls=%async_computation | async-start | bytes 917504 | tf_op jit(solution)/shard_map/all_to_all | solution.py:252
  13.9 1.5 collective-permute-start
  15.3 2.6 %collective-permute-start.13 = (bf16[1,32,896]{2,1,0:T(8,128)(2,1)S(1)}, bf16[1,32,896]{2,1,0:T(8,128)(2,1)S(1)}, u32[]{:S(2)}, u32[]{:S(2)}) collective-permute-start(bf16[1,32,896]{2,1,0:T(8,128)(2,1)S(1)} %bitcast.40), channel_id=1, source_target_pairs={{32,0},{0,32},{33,1},{1,33},{34,2},{2,34},{35,3},{3,35},{36,4},{4,... | collective-permute-start | bytes 172040 | tf_op jit(solution)/shard_map/ppermute | solution.py:18
  17.9 3.0 %collective-permute-done.13 = bf16[1,32,896]{2,1,0:T(8,128)(2,1)S(1)} collective-permute-done((bf16[1,32,896]{2,1,0:T(8,128)(2,1)S(1)}, bf16[1,32,896]{2,1,0:T(8,128)(2,1)S(1)}, u32[]{:S(2)}, u32[]{:S(2)}) %collective-permute-start.13) | collective-permute-done | bytes 57376 | tf_op jit(solution)/shard_map/ppermute | solution.py:18
  20.9 2.6 %collective-permute-start.14 = (bf16[2,32,896]{2,1,0:T(8,128)(2,1)S(1)}, bf16[2,32,896]{2,1,0:T(8,128)(2,1)S(1)}, u32[]{:S(2)}, u32[]{:S(2)}) collective-permute-start(bf16[2,32,896]{2,1,0:T(8,128)(2,1)S(1)} %get-tuple-element.33.refs_0_), channel_id=1, source_target_pairs={{64,0},{128,64},{192,128},{0,192},{65,1},{129,65},{193,129},{1,193... | collective-permute-start | bytes 344072 | tf_op jit(solution)/shard_map/ppermute | solution.py:18
  24.6 2.6 %collective-permute-start.17 = (bf16[2,32,896]{2,1,0:T(8,128)(2,1)S(1)}, bf16[2,32,896]{2,1,0:T(8,128)(2,1)S(1)}, u32[]{:S(2)}, u32[]{:S(2)}) collective-permute-start(bf16[2,32,896]{2,1,0:T(8,128)(2,1)S(1)} %get-tuple-element.33.refs_0_), channel_id=1, source_target_pairs={{16,0},{0,16},{17,1},{1,17},{18,2},{2,18},{19,3},{3,19},{20,4},{4,... | collective-permute-start | bytes 344072 | tf_op jit(solution)/shard_map/ppermute | solution.py:18
  27.2 3.5 %collective-permute-start.1 = (bf16[2,32,896]{2,1,0:T(8,128)(2,1)S(1)}, bf16[2,32,896]{2,1,0:T(8,128)(2,1)S(1)}, u32[]{:S(2)}, u32[]{:S(2)}) collective-permute-start(bf16[2,32,896]{2,1,0:T(8,128)(2,1)S(1)} %get-tuple-element.34.refs_0_), channel_id=1, source_target_pairs={{1,0},{2,1},{3,2},{4,3},{5,4},{6,5},{7,6},{0,7},{9,8},{10,9},{11,1... | collective-permute-start | bytes 344072 | tf_op jit(solution)/shard_map/ppermute | solution.py:18
  30.7 1.2 collective-permute-start.29
  31.9 6.6 %collective-permute-start.3 = (bf16[2,32,896]{2,1,0:T(8,128)(2,1)S(1)}, bf16[2,32,896]{2,1,0:T(8,128)(2,1)S(1)}, u32[]{:S(2)}, u32[]{:S(2)}) collective-permute-start(bf16[2,32,896]{2,1,0:T(8,128)(2,1)S(1)} %get-tuple-element.34.refs_0_), channel_id=1, source_target_pairs={{4,0},{5,1},{6,2},{7,3},{0,4},{1,5},{2,6},{3,7},{12,8},{13,9},{14,... | collective-permute-start | bytes 344072 | tf_op jit(solution)/shard_map/ppermute | solution.py:18
  38.5 1.5 %collective-permute-start.18 = (bf16[2,32,896]{2,1,0:T(8,128)(2,1)S(1)}, bf16[2,32,896]{2,1,0:T(8,128)(2,1)S(1)}, u32[]{:S(2)}, u32[]{:S(2)}) collective-permute-start(bf16[2,32,896]{2,1,0:T(8,128)(2,1)S(1)} %collective-permute-done.14.refs_1_), channel_id=1, source_target_pairs={{16,0},{0,16},{17,1},{1,17},{18,2},{2,18},{19,3},{3,19},{20,4},{4,... | collective-permute-start | bytes 344072 | tf_op jit(solution)/shard_map/ppermute | solution.py:18
  40.5 0.8 pad_maximum_fusion.3
  41.7 2.4 %collective-permute-start.4 = (bf16[4,32,896]{2,1,0:T(8,128)(2,1)}, bf16[4,32,896]{2,1,0:T(8,128)(2,1)S(1)}, u32[]{:S(2)}, u32[]{:S(2)}) collective-permute-start(bf16[4,32,896]{2,1,0:T(8,128)(2,1)} %get-tuple-element.32), channel_id=1, source_target_pairs={{2,0},{3,1},{4,2},{5,3},{6,4},{7,5},{0,6},{1,7},{10,8},{11,9},{12,... | collective-permute-start | bytes 688136 | tf_op jit(solution)/shard_map/ppermute | solution.py:18
  44.1 4.9 %collective-permute-start.6 = (bf16[2,32,896]{2,1,0:T(8,128)(2,1)S(1)}, bf16[2,32,896]{2,1,0:T(8,128)(2,1)S(1)}, u32[]{:S(2)}, u32[]{:S(2)}) collective-permute-start(bf16[2,32,896]{2,1,0:T(8,128)(2,1)S(1)} %get-tuple-element.34.refs_0_), channel_id=1, source_target_pairs={{16,0},{0,16},{17,1},{1,17},{18,2},{2,18},{19,3},{3,19},{20,4},{4,... | collective-permute-start | bytes 344072 | tf_op jit(solution)/shard_map/ppermute | solution.py:18
  51.3 2.5 %collective-permute-start.25 = (bf16[112,512]{1,0:T(8,128)(2,1)S(1)}, bf16[112,512]{1,0:T(8,128)(2,1)S(1)}, u32[]{:S(2)}, u32[]{:S(2)}) collective-permute-start(bf16[112,512]{1,0:T(8,128)(2,1)S(1)} %get-tuple-element.14), channel_id=1, source_target_pairs={{64,0},{128,64},{192,128},{0,192},{65,1},{129,65},{193,129},{1,193... | collective-permute-start | bytes 344072 | tf_op jit(solution)/shard_map/ppermute | solution.py:18
  54.4 1.4 collective-permute-done.4.refs_4_
  55.8 6.4 %collective-permute-done.5.refs_5_ = bf16[4,32,896]{2,1,0:T(8,128)(2,1)S(1)} collective-permute-done((bf16[4,32,896]{2,1,0:T(8,128)(2,1)}, bf16[4,32,896]{2,1,0:T(8,128)(2,1)S(1)}, u32[]{:S(2)}, u32[]{:S(2)}) %collective-permute-start.5) | collective-permute-done | bytes 229408 | tf_op jit(solution)/shard_map/ppermute | solution.py:18
  64.4 2.4 %collective-permute-start.28 = (bf16[4,112,512]{2,1,0:T(8,128)(2,1)S(1)}, bf16[4,112,512]{2,1,0:T(8,128)(2,1)S(1)}, u32[]{:S(2)}, u32[]{:S(2)}) collective-permute-start(bf16[4,112,512]{2,1,0:T(8,128)(2,1)S(1)} %pad_maximum_fusion.refs_16_), channel_id=1, source_target_pairs={{32,0},{0,32},{33,1},{1,33},{34,2},{2,34},{35,3},{3,35},{36,4},{4,... | collective-permute-start | bytes 1376264 | tf_op jit(solution)/shard_map/ppermute | solution.py:18
  66.9 1.5 collective-permute-done.21
  68.3 3.1 %collective-permute-start.9 = (bf16[2,32,896]{2,1,0:T(8,128)(2,1)S(1)}, bf16[2,32,896]{2,1,0:T(8,128)(2,1)S(1)}, u32[]{:S(2)}, u32[]{:S(2)}) collective-permute-start(bf16[2,32,896]{2,1,0:T(8,128)(2,1)S(1)} %collective-permute-done.3.refs_3_), channel_id=1, source_target_pairs={{16,0},{0,16},{17,1},{1,17},{18,2},{2,18},{19,3},{3,19},{20,4},{4,... | collective-permute-start | bytes 344072 | tf_op jit(solution)/shard_map/ppermute | solution.py:18
  71.5 0.9 collective-permute-done.9.refs_9_
  73.1 1.3 collective-permute-start.22
  75.0 5.0 %collective-permute-done.22.refs_13_ = bf16[2,112,512]{2,1,0:T(8,128)(2,1)S(1)} collective-permute-done((bf16[2,112,512]{2,1,0:T(8,128)(2,1)S(1)}, bf16[2,112,512]{2,1,0:T(8,128)(2,1)S(1)}, u32[]{:S(2)}, u32[]{:S(2)}) %collective-permute-start.22) | collective-permute-done | bytes 229408 | tf_op jit(solution)/shard_map/ppermute | solution.py:18
  80.0 2.6 %collective-permute-done.23.refs_14_ = bf16[2,112,512]{2,1,0:T(8,128)(2,1)} collective-permute-done((bf16[2,112,512]{2,1,0:T(8,128)(2,1)S(1)}, bf16[2,112,512]{2,1,0:T(8,128)(2,1)}, u32[]{:S(2)}, u32[]{:S(2)}) %collective-permute-start.23) | collective-permute-done | bytes 229408 | tf_op jit(solution)/shard_map/ppermute | solution.py:18
  82.5 5.4 %collective-permute-done.24.refs_15_ = bf16[2,112,512]{2,1,0:T(8,128)(2,1)} collective-permute-done((bf16[2,112,512]{2,1,0:T(8,128)(2,1)S(1)}, bf16[2,112,512]{2,1,0:T(8,128)(2,1)}, u32[]{:S(2)}, u32[]{:S(2)}) %collective-permute-start.24) | collective-permute-done | bytes 229408 | tf_op jit(solution)/shard_map/ppermute | solution.py:18
  88.0 0.9 copy-done.3
  88.9 0.9 copy-done.5
  89.8 0.9 copy-done.7
  90.7 0.9 copy-done.9
  91.6 0.9 copy-done.11
  92.5 7.3 %shard_map.58 = (bf16[2,112,512]{2,1,0:T(8,128)(2,1)S(1)}, bf16[2,112,512]{2,1,0:T(8,128)(2,1)S(1)}, bf16[2,112,512]{2,1,0:T(8,128)(2,1)S(1)}, bf16[2,112,512]{2...) custom-call(s32[4]{0:T(128)S(1)} %pad_add_fusion.place, ...), custom_call_target="tpu_custom_call" | custom-call | flops 3758096384 | bytes 7602192 | tf_op jit(solution)/shard_map/pallas_call | solution.py:40
  100.0 2.7 %collective-permute-start.31 = (bf16[2,112,512]{2,1,0:T(8,128)(2,1)S(1)}, bf16[2,112,512]{2,1,0:T(8,128)(2,1)S(1)}, u32[]{:S(2)}, u32[]{:S(2)}) collective-permute-start(bf16[2,112,512]{2,1,0:T(8,128)(2,1)S(1)} %get-tuple-element.17), channel_id=1, source_target_pairs={{0,192},{64,0},{128,64},{192,128},{1,193},{65,1},{129,65},{193,129... | collective-permute-start | bytes 688136 | tf_op jit(solution)/shard_map/ppermute | solution.py:23
  102.7 1.4 collective-permute-start.34
  104.1 8.5 %collective-permute-done.30 = bf16[2,112,512]{2,1,0:T(8,128)(2,1)S(1)} collective-permute-done((bf16[2,112,512]{2,1,0:T(8,128)(2,1)S(1)}, bf16[2,112,512]{2,1,0:T(8,128)(2,1)S(1)}, u32[]{:S(2)}, u32[]{:S(2)}) %collective-permute-start.30) | collective-permute-done | bytes 229408 | tf_op jit(solution)/shard_map/ppermute | solution.py:23
  112.7 1.6 %collective-permute-start.33 = (bf16[112,512]{1,0:T(8,128)(2,1)S(1)}, bf16[112,512]{1,0:T(8,128)(2,1)S(1)}, u32[]{:S(2)}, u32[]{:S(2)}) collective-permute-start(bf16[112,512]{1,0:T(8,128)(2,1)S(1)} %get-tuple-element.25), channel_id=1, source_target_pairs={{0,32},{32,0},{1,33},{33,1},{2,34},{34,2},{3,35},{35,3},{4,36},{36... | collective-permute-start | bytes 344072 | tf_op jit(solution)/shard_map/ppermute | solution.py:23
  115.8 2.1 %collective-permute-start.36 = (bf16[112,512]{1,0:T(8,128)(2,1)S(1)}, bf16[112,512]{1,0:T(8,128)(2,1)S(1)}, u32[]{:S(2)}, u32[]{:S(2)}) collective-permute-start(bf16[112,512]{1,0:T(8,128)(2,1)S(1)} %get-tuple-element.22), channel_id=1, source_target_pairs={{0,192},{64,0},{128,64},{192,128},{1,193},{65,1},{129,65},{193,129... | collective-permute-start | bytes 344072 | tf_op jit(solution)/shard_map/ppermute | solution.py:23
  117.9 1.5 collective-permute-start.37
  119.4 0.9 collective-permute-done.35.refs_3_
  120.9 2.6 %collective-permute-done.37.refs_5_ = bf16[112,512]{1,0:T(8,128)(2,1)S(1)} collective-permute-done((bf16[112,512]{1,0:T(8,128)(2,1)S(1)}, bf16[112,512]{1,0:T(8,128)(2,1)S(1)}, u32[]{:S(2)}, u32[]{:S(2)}) %collective-permute-start.37) | collective-permute-done | bytes 114720 | tf_op jit(solution)/shard_map/ppermute | solution.py:23
  123.4 1.3 shard_map.59
  124.7 6.4 %all-to-all-start.1 = ((bf16[16,56,224]{2,1,0:T(8,128)(2,1)}), bf16[16,56,224]{2,1,0:T(8,128)(2,1)S(1)}, u32[]{:S(2)}, u32[]{:S(2)}) async-start(bf16[16,56,224]{2,1,0:T(8,128)(2,1)} %shard_map.59), calls=%async_computation.1 | async-start | bytes 917504 | tf_op jit(solution)/shard_map/all_to_all | solution.py:293
  131.1 0.8 fusion.7
  131.9 8.7 %all-to-all-done.1 = bf16[16,56,224]{2,1,0:T(8,128)(2,1)S(1)} async-done(((bf16[16,56,224]{2,1,0:T(8,128)(2,1)}), bf16[16,56,224]{2,1,0:T(8,128)(2,1)S(1)}, u32[]{:S(2)}, u32[]{:S(2)}) %all-to-all-start.1) | async-done | bytes 401440 | tf_op jit(solution)/shard_map/all_to_all | solution.py:293
  141.3 5.9 %collective-permute-start.38 = (f32[56,112]{1,0:T(8,128)S(1)}, f32[56,112]{1,0:T(8,128)S(1)}, u32[]{:S(2)}, u32[]{:S(2)}) collective-permute-start(f32[56,112]{1,0:T(8,128)S(1)} %select_n.67), channel_id=1, source_target_pairs={{16,0},{0,16},{17,1},{1,17},{18,2},{2,18},{19,3},{3,19},{20,4},{4,... | collective-permute-start | bytes 75272 | tf_op jit(solution)/shard_map/ppermute | solution.py:18
  148.9 0.7 copy.8
  (88 shorter events, 13.2 us)
Async XLA Ops:
  0.0 4.3 %collective-permute-start.12 = (bf16[56,4,56]{2,1,0:T(4,128)(2,1)}, bf16[56,4,56]{2,1,0:T(4,128)(2,1)S(1)}, u32[]{:S(2)}, u32[]{:S(2)}) collective-permute-start(bf16[56,4,56]{2,1,0:T(4,128)(2,1)} %own.1), channel_id=1, source_target_pairs={{16,0},{0,16},{17,1},{1,17},{18,2},{2,18},{19,3},{3,19},{20,4},{4,... | collective-permute-start | bytes 75272 | tf_op jit(solution)/shard_map/ppermute | solution.py:18
  6.1 7.7 %copy-start.12 = (bf16[32,896]{1,0:T(8,128)(2,1)S(1)}, bf16[32,896]{1,0:T(8,128)(2,1)}, u32[]{:S(2)}) copy-start(bf16[32,896]{1,0:T(8,128)(2,1)} %param.6) | copy-start | bytes 172036
  6.1 44.0 %all-to-all-start = ((bf16[16,56,224]{2,1,0:T(8,128)(2,1)}), bf16[16,56,224]{2,1,0:T(8,128)(2,1)S(1)}, u32[]{:S(2)}, u32[]{:S(2)}) async-start(bf16[16,56,224]{2,1,0:T(8,128)(2,1)} %shard_map.55), calls=%async_computation | async-start | bytes 917504 | tf_op jit(solution)/shard_map/all_to_all | solution.py:252
  13.9 4.1 %collective-permute-start = (bf16[1,32,896]{2,1,0:T(8,128)(2,1)S(1)}, bf16[1,32,896]{2,1,0:T(8,128)(2,1)S(1)}, u32[]{:S(2)}, u32[]{:S(2)}) collective-permute-start(bf16[1,32,896]{2,1,0:T(8,128)(2,1)S(1)} %bitcast.39), channel_id=1, source_target_pairs={{8,0},{0,8},{9,1},{1,9},{10,2},{2,10},{11,3},{3,11},{12,4},{4,12},... | collective-permute-start | bytes 172040 | tf_op jit(solution)/shard_map/ppermute | solution.py:18
  15.3 5.6 %collective-permute-start.13 = (bf16[1,32,896]{2,1,0:T(8,128)(2,1)S(1)}, bf16[1,32,896]{2,1,0:T(8,128)(2,1)S(1)}, u32[]{:S(2)}, u32[]{:S(2)}) collective-permute-start(bf16[1,32,896]{2,1,0:T(8,128)(2,1)S(1)} %bitcast.40), channel_id=1, source_target_pairs={{32,0},{0,32},{33,1},{1,33},{34,2},{2,34},{35,3},{3,35},{36,4},{4,... | collective-permute-start | bytes 172040 | tf_op jit(solution)/shard_map/ppermute | solution.py:18
  20.9 9.8 %collective-permute-start.14 = (bf16[2,32,896]{2,1,0:T(8,128)(2,1)S(1)}, bf16[2,32,896]{2,1,0:T(8,128)(2,1)S(1)}, u32[]{:S(2)}, u32[]{:S(2)}) collective-permute-start(bf16[2,32,896]{2,1,0:T(8,128)(2,1)S(1)} %get-tuple-element.33.refs_0_), channel_id=1, source_target_pairs={{64,0},{128,64},{192,128},{0,192},{65,1},{129,65},{193,129},{1,193... | collective-permute-start | bytes 344072 | tf_op jit(solution)/shard_map/ppermute | solution.py:18
  23.5 7.2 %collective-permute-start.15 = (bf16[2,32,896]{2,1,0:T(8,128)(2,1)S(1)}, bf16[2,32,896]{2,1,0:T(8,128)(2,1)S(1)}, u32[]{:S(2)}, u32[]{:S(2)}) collective-permute-start(bf16[2,32,896]{2,1,0:T(8,128)(2,1)S(1)} %get-tuple-element.33.refs_0_), channel_id=1, source_target_pairs={{128,0},{192,64},{0,128},{64,192},{129,1},{193,65},{1,129},{65,193... | collective-permute-start | bytes 344072 | tf_op jit(solution)/shard_map/ppermute | solution.py:18
  24.0 7.9 %collective-permute-start.16 = (bf16[2,32,896]{2,1,0:T(8,128)(2,1)S(1)}, bf16[2,32,896]{2,1,0:T(8,128)(2,1)S(1)}, u32[]{:S(2)}, u32[]{:S(2)}) collective-permute-start(bf16[2,32,896]{2,1,0:T(8,128)(2,1)S(1)} %get-tuple-element.33.refs_0_), channel_id=1, source_target_pairs={{192,0},{0,64},{64,128},{128,192},{193,1},{1,65},{65,129},{129,193... | collective-permute-start | bytes 344072 | tf_op jit(solution)/shard_map/ppermute | solution.py:18
  24.6 13.9 %collective-permute-start.17 = (bf16[2,32,896]{2,1,0:T(8,128)(2,1)S(1)}, bf16[2,32,896]{2,1,0:T(8,128)(2,1)S(1)}, u32[]{:S(2)}, u32[]{:S(2)}) collective-permute-start(bf16[2,32,896]{2,1,0:T(8,128)(2,1)S(1)} %get-tuple-element.33.refs_0_), channel_id=1, source_target_pairs={{16,0},{0,16},{17,1},{1,17},{18,2},{2,18},{19,3},{3,19},{20,4},{4,... | collective-permute-start | bytes 344072 | tf_op jit(solution)/shard_map/ppermute | solution.py:18
  27.2 12.8 %collective-permute-start.1 = (bf16[2,32,896]{2,1,0:T(8,128)(2,1)S(1)}, bf16[2,32,896]{2,1,0:T(8,128)(2,1)S(1)}, u32[]{:S(2)}, u32[]{:S(2)}) collective-permute-start(bf16[2,32,896]{2,1,0:T(8,128)(2,1)S(1)} %get-tuple-element.34.refs_0_), channel_id=1, source_target_pairs={{1,0},{2,1},{3,2},{4,3},{5,4},{6,5},{7,6},{0,7},{9,8},{10,9},{11,1... | collective-permute-start | bytes 344072 | tf_op jit(solution)/shard_map/ppermute | solution.py:18
  30.7 9.4 %collective-permute-start.2 = (bf16[2,32,896]{2,1,0:T(8,128)(2,1)S(1)}, bf16[2,32,896]{2,1,0:T(8,128)(2,1)S(1)}, u32[]{:S(2)}, u32[]{:S(2)}) collective-permute-start(bf16[2,32,896]{2,1,0:T(8,128)(2,1)S(1)} %get-tuple-element.34.refs_0_), channel_id=1, source_target_pairs={{7,0},{0,1},{1,2},{2,3},{3,4},{4,5},{5,6},{6,7},{15,8},{8,9},{9,10... | collective-permute-start | bytes 344072 | tf_op jit(solution)/shard_map/ppermute | solution.py:18
  30.7 44.3 %collective-permute-start.29 = (f32[2048,128]{1,0:T(8,128)}, f32[2048,128]{1,0:T(8,128)}, u32[]{:S(2)}, u32[]{:S(2)}) collective-permute-start(f32[2048,128]{1,0:T(8,128)} %bitcast.13.refs_18_), channel_id=1, source_target_pairs={{16,0},{0,16},{17,1},{1,17},{18,2},{2,18},{19,3},{3,19},{20,4},{4,... | collective-permute-start | bytes 3145736 | tf_op jit(solution)/shard_map/ppermute | solution.py:18
  31.9 9.8 %collective-permute-start.3 = (bf16[2,32,896]{2,1,0:T(8,128)(2,1)S(1)}, bf16[2,32,896]{2,1,0:T(8,128)(2,1)S(1)}, u32[]{:S(2)}, u32[]{:S(2)}) collective-permute-start(bf16[2,32,896]{2,1,0:T(8,128)(2,1)S(1)} %get-tuple-element.34.refs_0_), channel_id=1, source_target_pairs={{4,0},{5,1},{6,2},{7,3},{0,4},{1,5},{2,6},{3,7},{12,8},{13,9},{14,... | collective-permute-start | bytes 344072 | tf_op jit(solution)/shard_map/ppermute | solution.py:18
  38.5 5.6 %collective-permute-start.18 = (bf16[2,32,896]{2,1,0:T(8,128)(2,1)S(1)}, bf16[2,32,896]{2,1,0:T(8,128)(2,1)S(1)}, u32[]{:S(2)}, u32[]{:S(2)}) collective-permute-start(bf16[2,32,896]{2,1,0:T(8,128)(2,1)S(1)} %collective-permute-done.14.refs_1_), channel_id=1, source_target_pairs={{16,0},{0,16},{17,1},{1,17},{18,2},{2,18},{19,3},{3,19},{20,4},{4,... | collective-permute-start | bytes 344072 | tf_op jit(solution)/shard_map/ppermute | solution.py:18
  40.0 9.0 %collective-permute-start.19 = (bf16[2,32,896]{2,1,0:T(8,128)(2,1)S(1)}, bf16[2,32,896]{2,1,0:T(8,128)(2,1)S(1)}, u32[]{:S(2)}, u32[]{:S(2)}) collective-permute-start(bf16[2,32,896]{2,1,0:T(8,128)(2,1)S(1)} %collective-permute-done.15.refs_2_), channel_id=1, source_target_pairs={{16,0},{0,16},{17,1},{1,17},{18,2},{2,18},{19,3},{3,19},{20,4},{4,... | collective-permute-start | bytes 344072 | tf_op jit(solution)/shard_map/ppermute | solution.py:18
  40.1 8.9 %collective-permute-start.20 = (bf16[2,32,896]{2,1,0:T(8,128)(2,1)S(1)}, bf16[2,32,896]{2,1,0:T(8,128)(2,1)S(1)}, u32[]{:S(2)}, u32[]{:S(2)}) collective-permute-start(bf16[2,32,896]{2,1,0:T(8,128)(2,1)S(1)} %collective-permute-done.16.refs_3_), channel_id=1, source_target_pairs={{16,0},{0,16},{17,1},{1,17},{18,2},{2,18},{19,3},{3,19},{20,4},{4,... | collective-permute-start | bytes 344072 | tf_op jit(solution)/shard_map/ppermute | solution.py:18
  41.7 26.6 %copy-start.2 = (bf16[2,32,896]{2,1,0:T(8,128)(2,1)}, bf16[2,32,896]{2,1,0:T(8,128)(2,1)S(1)}, u32[]{:S(2)}) copy-start(bf16[2,32,896]{2,1,0:T(8,128)(2,1)S(1)} %collective-permute-done.3.refs_3_) | copy-start | bytes 344068
  41.7 14.1 %collective-permute-start.4 = (bf16[4,32,896]{2,1,0:T(8,128)(2,1)}, bf16[4,32,896]{2,1,0:T(8,128)(2,1)S(1)}, u32[]{:S(2)}, u32[]{:S(2)}) collective-permute-start(bf16[4,32,896]{2,1,0:T(8,128)(2,1)} %get-tuple-element.32), channel_id=1, source_target_pairs={{2,0},{3,1},{4,2},{5,3},{6,4},{7,5},{0,6},{1,7},{10,8},{11,9},{12,... | collective-permute-start | bytes 688136 | tf_op jit(solution)/shard_map/ppermute | solution.py:18
  44.1 6.5 %collective-permute-start.6 = (bf16[2,32,896]{2,1,0:T(8,128)(2,1)S(1)}, bf16[2,32,896]{2,1,0:T(8,128)(2,1)S(1)}, u32[]{:S(2)}, u32[]{:S(2)}) collective-permute-start(bf16[2,32,896]{2,1,0:T(8,128)(2,1)S(1)} %get-tuple-element.34.refs_0_), channel_id=1, source_target_pairs={{16,0},{0,16},{17,1},{1,17},{18,2},{2,18},{19,3},{3,19},{20,4},{4,... | collective-permute-start | bytes 344072 | tf_op jit(solution)/shard_map/ppermute | solution.py:18
  49.0 13.2 %collective-permute-start.5 = (bf16[4,32,896]{2,1,0:T(8,128)(2,1)}, bf16[4,32,896]{2,1,0:T(8,128)(2,1)S(1)}, u32[]{:S(2)}, u32[]{:S(2)}) collective-permute-start(bf16[4,32,896]{2,1,0:T(8,128)(2,1)} %get-tuple-element.31), channel_id=1, source_target_pairs={{6,0},{7,1},{0,2},{1,3},{2,4},{3,5},{4,6},{5,7},{14,8},{15,9},{8,1... | collective-permute-start | bytes 688136 | tf_op jit(solution)/shard_map/ppermute | solution.py:18
  49.1 4.7 %collective-permute-start.7 = (bf16[2,32,896]{2,1,0:T(8,128)(2,1)S(1)}, bf16[2,32,896]{2,1,0:T(8,128)(2,1)S(1)}, u32[]{:S(2)}, u32[]{:S(2)}) collective-permute-start(bf16[2,32,896]{2,1,0:T(8,128)(2,1)S(1)} %collective-permute-done.1.refs_1_), channel_id=1, source_target_pairs={{16,0},{0,16},{17,1},{1,17},{18,2},{2,18},{19,3},{3,19},{20,4},{4,... | collective-permute-start | bytes 344072 | tf_op jit(solution)/shard_map/ppermute | solution.py:18
  51.3 11.4 %collective-permute-start.25 = (bf16[112,512]{1,0:T(8,128)(2,1)S(1)}, bf16[112,512]{1,0:T(8,128)(2,1)S(1)}, u32[]{:S(2)}, u32[]{:S(2)}) collective-permute-start(bf16[112,512]{1,0:T(8,128)(2,1)S(1)} %get-tuple-element.14), channel_id=1, source_target_pairs={{64,0},{128,64},{192,128},{0,192},{65,1},{129,65},{193,129},{1,193... | collective-permute-start | bytes 344072 | tf_op jit(solution)/shard_map/ppermute | solution.py:18
  54.4 8.3 %collective-permute-start.26 = (bf16[112,512]{1,0:T(8,128)(2,1)S(1)}, bf16[112,512]{1,0:T(8,128)(2,1)S(1)}, u32[]{:S(2)}, u32[]{:S(2)}) collective-permute-start(bf16[112,512]{1,0:T(8,128)(2,1)S(1)} %get-tuple-element.14), channel_id=1, source_target_pairs={{128,0},{192,64},{0,128},{64,192},{129,1},{193,65},{1,129},{65,193... | collective-permute-start | bytes 344072 | tf_op jit(solution)/shard_map/ppermute | solution.py:18
  55.8 7.4 %collective-permute-start.27 = (bf16[112,512]{1,0:T(8,128)(2,1)S(1)}, bf16[112,512]{1,0:T(8,128)(2,1)S(1)}, u32[]{:S(2)}, u32[]{:S(2)}) collective-permute-start(bf16[112,512]{1,0:T(8,128)(2,1)S(1)} %get-tuple-element.14), channel_id=1, source_target_pairs={{192,0},{0,64},{64,128},{128,192},{193,1},{1,65},{65,129},{129,193... | collective-permute-start | bytes 344072 | tf_op jit(solution)/shard_map/ppermute | solution.py:18
  62.2 1.6 %collective-permute-start.8 = (bf16[2,32,896]{2,1,0:T(8,128)(2,1)S(1)}, bf16[2,32,896]{2,1,0:T(8,128)(2,1)S(1)}, u32[]{:S(2)}, u32[]{:S(2)}) collective-permute-start(bf16[2,32,896]{2,1,0:T(8,128)(2,1)S(1)} %collective-permute-done.2.refs_2_), channel_id=1, source_target_pairs={{16,0},{0,16},{17,1},{1,17},{18,2},{2,18},{19,3},{3,19},{20,4},{4,... | collective-permute-start | bytes 344072 | tf_op jit(solution)/shard_map/ppermute | solution.py:18
  62.7 11.7 %collective-permute-start.10 = (bf16[4,32,896]{2,1,0:T(8,128)(2,1)S(1)}, bf16[4,32,896]{2,1,0:T(8,128)(2,1)S(1)}, u32[]{:S(2)}, u32[]{:S(2)}) collective-permute-start(bf16[4,32,896]{2,1,0:T(8,128)(2,1)S(1)} %collective-permute-done.4.refs_4_), channel_id=1, source_target_pairs={{16,0},{0,16},{17,1},{1,17},{18,2},{2,18},{19,3},{3,19},{20,4},{4,... | collective-permute-start | bytes 688136 | tf_op jit(solution)/shard_map/ppermute | solution.py:18
  62.7 11.6 %collective-permute-start.11 = (bf16[4,32,896]{2,1,0:T(8,128)(2,1)S(1)}, bf16[4,32,896]{2,1,0:T(8,128)(2,1)S(1)}, u32[]{:S(2)}, u32[]{:S(2)}) collective-permute-start(bf16[4,32,896]{2,1,0:T(8,128)(2,1)S(1)} %collective-permute-done.5.refs_5_), channel_id=1, source_target_pairs={{16,0},{0,16},{17,1},{1,17},{18,2},{2,18},{19,3},{3,19},{20,4},{4,... | collective-permute-start | bytes 688136 | tf_op jit(solution)/shard_map/ppermute | solution.py:18
  63.2 5.1 %collective-permute-start.21 = (bf16[112,512]{1,0:T(8,128)(2,1)S(1)}, bf16[112,512]{1,0:T(8,128)(2,1)S(1)}, u32[]{:S(2)}, u32[]{:S(2)}) collective-permute-start(bf16[112,512]{1,0:T(8,128)(2,1)S(1)} %get-tuple-element.13), channel_id=1, source_target_pairs={{32,0},{0,32},{33,1},{1,33},{34,2},{2,34},{35,3},{3,35},{36,4},{4,... | collective-permute-start | bytes 344072 | tf_op jit(solution)/shard_map/ppermute | solution.py:18
  64.4 23.5 %collective-permute-start.28 = (bf16[4,112,512]{2,1,0:T(8,128)(2,1)S(1)}, bf16[4,112,512]{2,1,0:T(8,128)(2,1)S(1)}, u32[]{:S(2)}, u32[]{:S(2)}) collective-permute-start(bf16[4,112,512]{2,1,0:T(8,128)(2,1)S(1)} %pad_maximum_fusion.refs_16_), channel_id=1, source_target_pairs={{32,0},{0,32},{33,1},{1,33},{34,2},{2,34},{35,3},{3,35},{36,4},{4,... | collective-permute-start | bytes 1376264 | tf_op jit(solution)/shard_map/ppermute | solution.py:18
  68.3 4.1 %collective-permute-start.9 = (bf16[2,32,896]{2,1,0:T(8,128)(2,1)S(1)}, bf16[2,32,896]{2,1,0:T(8,128)(2,1)S(1)}, u32[]{:S(2)}, u32[]{:S(2)}) collective-permute-start(bf16[2,32,896]{2,1,0:T(8,128)(2,1)S(1)} %collective-permute-done.3.refs_3_), channel_id=1, source_target_pairs={{16,0},{0,16},{17,1},{1,17},{18,2},{2,18},{19,3},{3,19},{20,4},{4,... | collective-permute-start | bytes 344072 | tf_op jit(solution)/shard_map/ppermute | solution.py:18
  73.1 6.9 %collective-permute-start.22 = (bf16[2,112,512]{2,1,0:T(8,128)(2,1)S(1)}, bf16[2,112,512]{2,1,0:T(8,128)(2,1)S(1)}, u32[]{:S(2)}, u32[]{:S(2)}) collective-permute-start(bf16[2,112,512]{2,1,0:T(8,128)(2,1)S(1)} %pad_maximum_fusion.4.refs_12_), channel_id=1, source_target_pairs={{64,0},{128,64},{192,128},{0,192},{65,1},{129,65},{193,129},{1,193... | collective-permute-start | bytes 688136 | tf_op jit(solution)/shard_map/ppermute | solution.py:18
  74.3 8.2 %collective-permute-start.23 = (bf16[2,112,512]{2,1,0:T(8,128)(2,1)S(1)}, bf16[2,112,512]{2,1,0:T(8,128)(2,1)}, u32[]{:S(2)}, u32[]{:S(2)}) collective-permute-start(bf16[2,112,512]{2,1,0:T(8,128)(2,1)S(1)} %pad_maximum_fusion.4.refs_12_), channel_id=1, source_target_pairs={{128,0},{192,64},{0,128},{64,192},{129,1},{193,65},{1,129},{65,193... | collective-permute-start | bytes 688136 | tf_op jit(solution)/shard_map/ppermute | solution.py:18
  74.3 13.6 %collective-permute-start.24 = (bf16[2,112,512]{2,1,0:T(8,128)(2,1)S(1)}, bf16[2,112,512]{2,1,0:T(8,128)(2,1)}, u32[]{:S(2)}, u32[]{:S(2)}) collective-permute-start(bf16[2,112,512]{2,1,0:T(8,128)(2,1)S(1)} %pad_maximum_fusion.4.refs_12_), channel_id=1, source_target_pairs={{192,0},{0,64},{64,128},{128,192},{193,1},{1,65},{65,129},{129,193... | collective-permute-start | bytes 688136 | tf_op jit(solution)/shard_map/ppermute | solution.py:18
  88.0 0.9 copy-start.3
  88.9 0.9 copy-start.5
  89.8 0.9 copy-start.7
  90.7 0.9 copy-start.9
  99.7 12.9 %collective-permute-start.30 = (bf16[2,112,512]{2,1,0:T(8,128)(2,1)S(1)}, bf16[2,112,512]{2,1,0:T(8,128)(2,1)S(1)}, u32[]{:S(2)}, u32[]{:S(2)}) collective-permute-start(bf16[2,112,512]{2,1,0:T(8,128)(2,1)S(1)} %get-tuple-element.16), channel_id=1, source_target_pairs={{0,64},{64,128},{128,192},{192,0},{1,65},{65,129},{129,193},{193,1... | collective-permute-start | bytes 688136 | tf_op jit(solution)/shard_map/ppermute | solution.py:23
  100.0 12.6 %collective-permute-start.31 = (bf16[2,112,512]{2,1,0:T(8,128)(2,1)S(1)}, bf16[2,112,512]{2,1,0:T(8,128)(2,1)S(1)}, u32[]{:S(2)}, u32[]{:S(2)}) collective-permute-start(bf16[2,112,512]{2,1,0:T(8,128)(2,1)S(1)} %get-tuple-element.17), channel_id=1, source_target_pairs={{0,192},{64,0},{128,64},{192,128},{1,193},{65,1},{129,65},{193,129... | collective-permute-start | bytes 688136 | tf_op jit(solution)/shard_map/ppermute | solution.py:23
  102.7 9.9 %collective-permute-start.32 = (bf16[2,112,512]{2,1,0:T(8,128)(2,1)S(1)}, bf16[2,112,512]{2,1,0:T(8,128)(2,1)S(1)}, u32[]{:S(2)}, u32[]{:S(2)}) collective-permute-start(bf16[2,112,512]{2,1,0:T(8,128)(2,1)S(1)} %get-tuple-element.18), channel_id=1, source_target_pairs={{0,128},{64,192},{128,0},{192,64},{1,129},{65,193},{129,1},{193,65... | collective-permute-start | bytes 688136 | tf_op jit(solution)/shard_map/ppermute | solution.py:23
  102.7 12.3 %collective-permute-start.34 = (bf16[4,112,512]{2,1,0:T(8,128)(2,1)S(1)}, bf16[4,112,512]{2,1,0:T(8,128)(2,1)S(1)}, u32[]{:S(2)}, u32[]{:S(2)}) collective-permute-start(bf16[4,112,512]{2,1,0:T(8,128)(2,1)S(1)} %get-tuple-element.20), channel_id=1, source_target_pairs={{0,32},{32,0},{1,33},{33,1},{2,34},{34,2},{3,35},{35,3},{4,36},{36... | collective-permute-start | bytes 1376264 | tf_op jit(solution)/shard_map/ppermute | solution.py:23
  112.7 6.6 %collective-permute-start.33 = (bf16[112,512]{1,0:T(8,128)(2,1)S(1)}, bf16[112,512]{1,0:T(8,128)(2,1)S(1)}, u32[]{:S(2)}, u32[]{:S(2)}) collective-permute-start(bf16[112,512]{1,0:T(8,128)(2,1)S(1)} %get-tuple-element.25), channel_id=1, source_target_pairs={{0,32},{32,0},{1,33},{33,1},{2,34},{34,2},{3,35},{35,3},{4,36},{36... | collective-permute-start | bytes 344072 | tf_op jit(solution)/shard_map/ppermute | solution.py:23
  115.2 5.1 %collective-permute-start.35 = (bf16[112,512]{1,0:T(8,128)(2,1)S(1)}, bf16[112,512]{1,0:T(8,128)(2,1)S(1)}, u32[]{:S(2)}, u32[]{:S(2)}) collective-permute-start(bf16[112,512]{1,0:T(8,128)(2,1)S(1)} %get-tuple-element.23), channel_id=1, source_target_pairs={{0,64},{64,128},{128,192},{192,0},{1,65},{65,129},{129,193},{193,1... | collective-permute-start | bytes 344072 | tf_op jit(solution)/shard_map/ppermute | solution.py:23
  115.8 5.1 %collective-permute-start.36 = (bf16[112,512]{1,0:T(8,128)(2,1)S(1)}, bf16[112,512]{1,0:T(8,128)(2,1)S(1)}, u32[]{:S(2)}, u32[]{:S(2)}) collective-permute-start(bf16[112,512]{1,0:T(8,128)(2,1)S(1)} %get-tuple-element.22), channel_id=1, source_target_pairs={{0,192},{64,0},{128,64},{192,128},{1,193},{65,1},{129,65},{193,129... | collective-permute-start | bytes 344072 | tf_op jit(solution)/shard_map/ppermute | solution.py:23
  117.9 5.5 %collective-permute-start.37 = (bf16[112,512]{1,0:T(8,128)(2,1)S(1)}, bf16[112,512]{1,0:T(8,128)(2,1)S(1)}, u32[]{:S(2)}, u32[]{:S(2)}) collective-permute-start(bf16[112,512]{1,0:T(8,128)(2,1)S(1)} %get-tuple-element.21), channel_id=1, source_target_pairs={{0,128},{64,192},{128,0},{192,64},{1,129},{65,193},{129,1},{193,65... | collective-permute-start | bytes 344072 | tf_op jit(solution)/shard_map/ppermute | solution.py:23
  124.7 16.0 %all-to-all-start.1 = ((bf16[16,56,224]{2,1,0:T(8,128)(2,1)}), bf16[16,56,224]{2,1,0:T(8,128)(2,1)S(1)}, u32[]{:S(2)}, u32[]{:S(2)}) async-start(bf16[16,56,224]{2,1,0:T(8,128)(2,1)} %shard_map.59), calls=%async_computation.1 | async-start | bytes 917504 | tf_op jit(solution)/shard_map/all_to_all | solution.py:293
  141.1 6.1 %copy-start.1 = (bf16[56,4,56]{2,1,0:T(4,128)(2,1)S(1)}, bf16[56,4,56]{2,1,0:T(4,128)(2,1)}, u32[]{:S(2)}) copy-start(bf16[56,4,56]{2,1,0:T(4,128)(2,1)} %own.1) | copy-start | bytes 75268
  141.3 6.7 %collective-permute-start.38 = (f32[56,112]{1,0:T(8,128)S(1)}, f32[56,112]{1,0:T(8,128)S(1)}, u32[]{:S(2)}, u32[]{:S(2)}) collective-permute-start(f32[56,112]{1,0:T(8,128)S(1)} %select_n.67), channel_id=1, source_target_pairs={{16,0},{0,16},{17,1},{1,17},{18,2},{2,18},{19,3},{3,19},{20,4},{4,... | collective-permute-start | bytes 75272 | tf_op jit(solution)/shard_map/ppermute | solution.py:18
  (7 other events, 5.0 us)
